TPU v7x, 128 devices: a whole 4x4x4 slice. The times are simulated.
128 devices in a mesh: data: 1, fsdp: 16 (over z, y), ep: 8 (over x, core).
Axes of the slice: x: 4, y: 4, z: 4, core: 2. Of those that a mesh axis runs over, the one named last changes fastest.
Arguments:
- x_in: bfloat16 [128, 384, 2048], P(('data', 'fsdp', 'ep'))
- w_qkv: bfloat16 [2048, 6144], P('fsdp')
- w_out: bfloat16 [2048, 2048], P('fsdp')
- w_gate: bfloat16 [64, 2048, 1408], P('ep', 'fsdp')
- w_up: bfloat16 [64, 2048, 1408], P('ep', 'fsdp')
- w_down: bfloat16 [64, 1408, 2048], P('ep', None, 'fsdp')
- ws_gate: bfloat16 [2048, 2816], P('fsdp')
- ws_up: bfloat16 [2048, 2816], P('fsdp')
- ws_down: bfloat16 [2816, 2048], P(None, 'fsdp')
- expert_ids: int32 [128, 384, 6], P(('data', 'fsdp', 'ep'))
- slot_ids: int32 [128, 384, 6], P(('data', 'fsdp', 'ep'))
- gate_vals: bfloat16 [128, 384, 6], P(('data', 'fsdp', 'ep'))
Outputs:
- output: bfloat16 [128, 384, 2048], P(('data', 'fsdp', 'ep'))
All inputs are finite; a program needn't handle non-finite values.
Results may differ from a plain program's by a relative error of at most 0.00961566.
Values are sent between devices in bfloat16 or wider.
A program may use at most 1 GiB of HBM per device.

v0:
```python
import jax
import jax.numpy as jnp
from jax import lax
from jax.sharding import PartitionSpec as P

HEAD_DIM = 128
ROPE_BASE = 10000.0
EPSILON = 1e-6


def rms_norm(values):
    vals_f32 = values.astype(jnp.float32)
    mean_sq = jnp.mean(vals_f32 * vals_f32, axis=-1, keepdims=True)
    return (vals_f32 * lax.rsqrt(mean_sq + EPSILON)).astype(jnp.bfloat16)


def rotary_embed(heads_in, positions):
    half_dim = HEAD_DIM // 2
    inv_freq = ROPE_BASE ** (-jnp.arange(half_dim, dtype=jnp.float32) * (2.0 / HEAD_DIM))
    angles = positions[:, None] * inv_freq[None, :]
    cos_tab = jnp.cos(angles)[:, None, :]
    sin_tab = jnp.sin(angles)[:, None, :]
    vals_f32 = heads_in.astype(jnp.float32)
    first_half = vals_f32[..., :half_dim]
    second_half = vals_f32[..., half_dim:]
    rotated = jnp.concatenate([first_half * cos_tab - second_half * sin_tab, second_half * cos_tab + first_half * sin_tab], axis=-1)
    return rotated.astype(jnp.bfloat16)


def attention_block(x_in, qkv_weight, out_weight):
    n_batch, seq_len, model_dim = x_in.shape
    n_heads = qkv_weight.shape[1] // (3 * HEAD_DIM)
    normed = rms_norm(x_in)
    qkv_proj = jnp.einsum("bsd,dn->bsn", normed, qkv_weight, preferred_element_type=jnp.float32).astype(jnp.bfloat16)
    qkv_proj = qkv_proj.reshape(n_batch, seq_len, 3, n_heads, HEAD_DIM)
    positions = jnp.arange(seq_len, dtype=jnp.float32)
    query_rot = rotary_embed(qkv_proj[:, :, 0], positions)
    key_rot = rotary_embed(qkv_proj[:, :, 1], positions)
    scores = jnp.einsum("bqhd,bkhd->bhqk", query_rot, key_rot, preferred_element_type=jnp.float32) * (HEAD_DIM ** -0.5)
    causal = jnp.arange(seq_len)[:, None] >= jnp.arange(seq_len)[None, :]
    attn_probs = jax.nn.softmax(jnp.where(causal, scores, -1e30), axis=-1).astype(jnp.bfloat16)
    attn_mixed = jnp.einsum("bhqk,bkhd->bqhd", attn_probs, qkv_proj[:, :, 2], preferred_element_type=jnp.float32).astype(jnp.bfloat16)
    attn_out = jnp.einsum("bsn,nm->bsm", attn_mixed.reshape(n_batch, seq_len, n_heads * HEAD_DIM), out_weight, preferred_element_type=jnp.float32)
    return (x_in.astype(jnp.float32) + attn_out).astype(jnp.bfloat16)


def capacity_for(n_tokens, top_k, n_experts):
    return ((5 * n_tokens * top_k) // (4 * n_experts) + 7) // 8 * 8


def dispatch_rows(normed_rows, expert_ids, slot_ids, n_experts, capacity):
    n_tokens, top_k = expert_ids.shape
    kept_mask = slot_ids >= 0
    target = jnp.where(kept_mask, expert_ids * capacity + slot_ids, n_experts * capacity).reshape(-1)
    source_tok = jnp.arange(n_tokens * top_k, dtype=jnp.int32) // top_k
    row_source = jnp.full((n_experts * capacity,), n_tokens, jnp.int32).at[target].set(source_tok, mode="drop")
    buffer = jnp.take(normed_rows, row_source, axis=0, mode="fill", fill_value=0)
    return buffer.reshape(n_experts, capacity, normed_rows.shape[-1])


def combine_rows(expert_out, expert_ids, slot_ids, gate_vals):
    n_experts, capacity, model_dim = expert_out.shape
    kept_mask = slot_ids >= 0
    source_row = jnp.where(kept_mask, expert_ids * capacity + slot_ids, 0)
    picked = jnp.take(expert_out.reshape(n_experts * capacity, model_dim), source_row, axis=0)
    weight = jnp.where(kept_mask, gate_vals, jnp.zeros_like(gate_vals))
    return jnp.einsum("tk,tkd->td", weight, picked, preferred_element_type=jnp.float32)


def expert_ffn(rows_in, gate_w, up_w, down_w):
    gate_act = jnp.einsum("ecd,edf->ecf", rows_in, gate_w, preferred_element_type=jnp.float32)
    up_act = jnp.einsum("ecd,edf->ecf", rows_in, up_w, preferred_element_type=jnp.float32)
    inner_act = (jax.nn.silu(gate_act) * up_act).astype(jnp.bfloat16)
    return jnp.einsum("ecf,efd->ecd", inner_act, down_w, preferred_element_type=jnp.float32).astype(jnp.bfloat16)


def shared_ffn(normed_rows, gate_w, up_w, down_w):
    gate_act = jnp.dot(normed_rows, gate_w, preferred_element_type=jnp.float32)
    up_act = jnp.dot(normed_rows, up_w, preferred_element_type=jnp.float32)
    inner_act = (jax.nn.silu(gate_act) * up_act).astype(jnp.bfloat16)
    return jnp.dot(inner_act, down_w, preferred_element_type=jnp.float32)


def solution(mesh):
    n_ep = mesh.shape["ep"]
    tok_spec = P(("data", "fsdp", "ep"))
    row_spec = P("fsdp", None)

    def local_step(x_in, w_qkv, w_out, w_gate, w_up, w_down, ws_gate, ws_up, ws_down, expert_ids, slot_ids, gate_vals):
        qkv_full = lax.all_gather(w_qkv, "fsdp", axis=0, tiled=True)
        out_full = lax.all_gather(w_out, "fsdp", axis=0, tiled=True)
        gate_full = lax.all_gather(w_gate, "fsdp", axis=1, tiled=True)
        up_full = lax.all_gather(w_up, "fsdp", axis=1, tiled=True)
        down_full = lax.all_gather(w_down, "fsdp", axis=2, tiled=True)
        sgate_full = lax.all_gather(ws_gate, "fsdp", axis=0, tiled=True)
        sup_full = lax.all_gather(ws_up, "fsdp", axis=0, tiled=True)
        sdown_full = lax.all_gather(ws_down, "fsdp", axis=1, tiled=True)
        n_batch, seq_len, model_dim = x_in.shape
        n_tokens = n_batch * seq_len
        top_k = expert_ids.shape[-1]
        n_experts = w_gate.shape[0] * n_ep
        capacity = capacity_for(n_tokens, top_k, n_experts)
        hidden = attention_block(x_in, qkv_full, out_full).reshape(n_tokens, model_dim)
        normed = rms_norm(hidden)
        ids_flat = expert_ids.reshape(n_tokens, top_k)
        slots_flat = slot_ids.reshape(n_tokens, top_k)
        buffer = dispatch_rows(normed, ids_flat, slots_flat, n_experts, capacity)
        received = lax.all_to_all(buffer, "ep", 0, 1, tiled=True)
        expert_out = expert_ffn(received, gate_full, up_full, down_full)
        returned = lax.all_to_all(expert_out, "ep", 1, 0, tiled=True)
        routed = combine_rows(returned, ids_flat, slots_flat, gate_vals.reshape(n_tokens, top_k))
        shared_out = shared_ffn(normed, sgate_full, sup_full, sdown_full)
        summed = hidden.astype(jnp.float32) + shared_out + routed
        return summed.astype(jnp.bfloat16).reshape(n_batch, seq_len, model_dim)

    return jax.shard_map(local_step, mesh=mesh, in_specs=(tok_spec, row_spec, row_spec, P("ep", "fsdp", None), P("ep", "fsdp", None), P("ep", None, "fsdp"), row_spec, row_spec, P(None, "fsdp"), tok_spec, tok_spec, tok_spec), out_specs=tok_spec, check_vma=False)
```

profile of v0, /device:TPU:1, one launch (start us, length us, event | category | flops | bytes accessed | tf_op | source)
XLA Modules:
  0.0 1336.4 jit_solution(913060500946157544)
XLA Ops:
  11.7 9.0 scatter_custom_fusion
  23.2 143.4 %all-gather.9.cloned.1.call-done = bf16[2048,6144]{1,0:T(8,128)(2,1)} async-done(((bf16[128,6144]{1,0:T(8,128)(2,1)}), bf16[2048,6144]{1,0:T(8,128)(2,1)}) %all-gather.9.cloned.1.call-update) | async-done | bytes 25165840 | tf_op jit(solution)/shard_map/all_gather | solution.py:90
  166.7 15.0 %fusion.20 = bf16[48,8,48,128]{3,1,2,0:T(8,128)(2,1)S(1)} fusion(bf16[2048,6144]{1,0:T(8,128)(2,1)} %all-gather.9.cloned.1.call-done, bf16[1,384,2048]{2,1,0:T(8,128)(2,1)S(1)} %copy-done, f32[384]{0:T(512)S(1)} %add_rsqrt_fusion.1), kind=kOutput, calls=%fused_computation.41 | convolution fusion | flops 9668395008 | bytes 31458816 | tf_op jit(solution)/shard_map/bsd,dn->bsn/dot_general | solution.py:34
  181.7 1.3 copy.53
  183.0 2.0 fusion.53
  184.9 2.9 copy.50
  188.5 2.3 fusion.24
  190.9 1.9 fusion.28
  192.8 5.5 fusion.54
  198.4 5.1 fusion.21
  203.4 35.7 %all-gather.11.cloned.1.call-done = bf16[2048,2048]{1,0:T(8,128)(2,1)} async-done(((bf16[128,2048]{1,0:T(8,128)(2,1)}), bf16[2048,2048]{1,0:T(8,128)(2,1)}) %all-gather.11.cloned.1.call-update) | async-done | bytes 8388624 | tf_op jit(solution)/shard_map/all_gather | solution.py:91
  239.2 7.2 fusion.14
  247.9 16.0 %gather_fusion = bf16[3072,2048]{1,0:T(8,128)(2,1)} fusion(bf16[384,2048]{1,0:T(8,128)(2,1)S(1)} %fusion.15, s32[3072]{0:T(1024)S(1)} %fusion.44), kind=kCustom, calls=%fused_computation | custom fusion | bytes 25178112 | tf_op jit(solution)/shard_map/jit(_take)/gather | solution.py:57
  263.9 10.7 broadcast_select_fusion
  274.6 6.2 all-to-all-start
  281.4 137.7 %all-to-all-done = bf16[64,48,2048]{2,1,0:T(8,128)(2,1)} async-done(((bf16[64,48,2048]{2,1,0:T(8,128)(2,1)}), bf16[64,48,2048]{2,1,0:T(8,128)(2,1)}, u32[]{:S(2)}, u32[]{:S(2)}) %all-to-all-start) | async-done | bytes 12582944 | tf_op jit(solution)/shard_map/all_to_all | solution.py:108
  419.2 10.8 copy.43
  430.0 72.4 %all-gather.19.cloned.1.call-done = bf16[8,2048,1408]{2,1,0:T(8,128)(2,1)} async-done(((bf16[8,128,1408]{2,1,0:T(8,128)(2,1)}), bf16[8,2048,1408]{2,1,0:T(8,128)(2,1)}) %all-gather.19.cloned.1.call-update) | async-done | bytes 46137360 | tf_op jit(solution)/shard_map/all_gather | solution.py:92
  502.4 32.1 %fusion.59 = f32[8,384,1408]{2,1,0:T(8,128)} fusion(bf16[8,384,2048]{2,1,0:T(8,128)(2,1)} %bitcast.97, bf16[8,2048,1408]{2,1,0:T(8,128)(2,1)} %all-gather.19.cloned.1.call-done), kind=kOutput, calls=%fused_computation.99 | convolution fusion | flops 17716740096 | bytes 76021760 | tf_op jit(solution)/shard_map/ecd,edf->ecf/dot_general | solution.py:71
  534.5 231.0 %all-gather.21.cloned.1.call-done = bf16[8,2048,1408]{2,1,0:T(8,128)(2,1)} async-done(((bf16[8,128,1408]{2,1,0:T(8,128)(2,1)}), bf16[8,2048,1408]{2,1,0:T(8,128)(2,1)}) %all-gather.21.cloned.1.call-update) | async-done | bytes 46137360 | tf_op jit(solution)/shard_map/all_gather | solution.py:93
  765.5 269.2 %all-gather.23.cloned.1.call-done = bf16[8,1408,2048]{2,1,0:T(8,128)(2,1)} async-done(((bf16[8,1408,128]{2,1,0:T(8,128)(2,1)}), bf16[8,1408,2048]{2,1,0:T(8,128)(2,1)}) %all-gather.23.cloned.1.call-update) | async-done | bytes 46137360 | tf_op jit(solution)/shard_map/all_gather | solution.py:94
  1034.7 50.3 %convolution_convert_fusion.1 = bf16[8,384,2048]{2,1,0:T(8,128)(2,1)} fusion(bf16[8,1408,2048]{2,1,0:T(8,128)(2,1)} %all-gather.23.cloned.1.call-done, f32[8,384,1408]{2,1,0:T(8,128)} %fusion.59, bf16[8,384,2048]{2,1,0:T(8,128)(2,1)} %bitcast.98, bf16[8,2048,1408]{2,1,0:T(8,128)(2,1)} %all-gather.21.cloned.1.call-done), kind=kOutput, calls=%fused_computation.14 | convolution fusion | flops 35465723904 | bytes 134742016 | tf_op jit(solution)/shard_map/ecf,efd->ecd/dot_general | solution.py:74
  1084.9 14.6 %copy.44 = bf16[8,384,2048]{2,0,1:T(8,128)(2,1)} copy(bf16[8,384,2048]{2,1,0:T(8,128)(2,1)} %convolution_convert_fusion.1) | data formatting | bytes 25165824 | tf_op jit(solution)/shard_map/convert_element_type | solution.py:74
  1099.5 7.7 all-to-all-start.1
  1108.0 14.0 %all-gather.13.cloned.1.call-done = bf16[2048,2816]{1,0:T(8,128)(2,1)} async-done(((bf16[128,2816]{1,0:T(8,128)(2,1)}), bf16[2048,2816]{1,0:T(8,128)(2,1)}) %all-gather.13.cloned.1.call-update) | async-done | bytes 11534352 | tf_op jit(solution)/shard_map/all_gather | solution.py:95
  1122.0 9.6 fusion.57
  1131.6 114.1 %all-to-all-done.1 = bf16[8,384,2048]{2,0,1:T(8,128)(2,1)} async-done(((bf16[8,384,2048]{2,0,1:T(8,128)(2,1)}), bf16[8,384,2048]{2,0,1:T(8,128)(2,1)}, u32[]{:S(2)}, u32[]{:S(2)}) %all-to-all-start.1) | async-done | bytes 12582944 | tf_op jit(solution)/shard_map/all_to_all | solution.py:110
  1245.7 14.5 %copy.45 = bf16[8,8,48,2048]{3,2,0,1:T(8,128)(2,1)} copy(bf16[8,8,48,2048]{3,0,2,1:T(8,128)(2,1)} %bitcast.23) | data formatting | bytes 25165824 | tf_op jit(solution)/shard_map/all_to_all | solution.py:110
  1260.2 24.5 %gather_fusion.1 = bf16[2304,2048]{1,0:T(8,128)(2,1)} fusion(bf16[3072,2048]{1,0:T(8,128)(2,1)} %bitcast.94, s32[3072]{0:T(1024)S(1)} %pad_clamp_fusion), kind=kCustom, calls=%fused_computation.1 | custom fusion | bytes 18883584 | tf_op jit(solution)/shard_map/jit(_take)/gather | solution.py:65
  1284.7 15.7 %reshape.326 = bf16[384,6,2048]{2,1,0:T(8,128)(2,1)} reshape(bf16[2304,2048]{1,0:T(8,128)(2,1)} %gather_fusion.1) | data formatting | bytes 18874368 | tf_op jit(solution)/shard_map/jit(_take)/gather | solution.py:65
  1300.3 7.9 fusion.1
  1308.4 20.9 %fusion.18 = bf16[1,384,2048]{2,1,0:T(8,128)(2,1)} fusion(f32[384,1,2048]{2,1,0:T(1,128)} %fusion.1, bf16[2816,2048]{1,0:T(8,128)(2,1)} %all-gather.17.cloned.1.call-done, bf16[384,2048]{1,0:T(8,128)(2,1)S(1)} %copy-done.4, bf16[2048,2816]{1,0:T(8,128)(2,1)} %all-gather.15.cloned.1.call-done, f32[384,2816]{1,0:T(8,128)} %fusion.57, f32[384]{0:T(512)S(1)} %copy-done.12), kind=kOutput, calls=%fused_computation.39 | convolution fusion | flops 8870363136 | bytes 33687040 | tf_op jit(solution)/shard_map/dot_general | solution.py:81
  (70 shorter events, 11.2 us)
Async XLA Ops:
  6.5 160.1 %all-gather.9.cloned.1.call-start = ((), (), s32[]{:S(2)}) async-start(), calls=%async_computation.2 | async-start | bytes 26738688 | tf_op jit(solution)/shard_map/all_gather | solution.py:90
  7.3 231.9 %all-gather.11.cloned.1.call-start = ((), (), s32[]{:S(2)}) async-start(), calls=%async_computation.3 | async-start | bytes 8912896 | tf_op jit(solution)/shard_map/all_gather | solution.py:91
  8.0 494.4 %all-gather.19.cloned.1.call-start = ((), (), s32[]{:S(2)}) async-start(), calls=%async_computation.7 | async-start | bytes 49020928 | tf_op jit(solution)/shard_map/all_gather | solution.py:92
  8.7 2.5 copy-start.6
  8.8 2.5 copy-start.8
  8.8 756.7 %all-gather.21.cloned.1.call-start = ((), (), s32[]{:S(2)}) async-start(), calls=%async_computation.8 | async-start | bytes 49020928 | tf_op jit(solution)/shard_map/all_gather | solution.py:93
  9.3 12.7 copy-start
  9.4 1025.3 %all-gather.23.cloned.1.call-start = ((), (), s32[]{:S(2)}) async-start(), calls=%async_computation.9 | async-start | bytes 49020928 | tf_op jit(solution)/shard_map/all_gather | solution.py:94
  9.9 1112.0 %all-gather.13.cloned.1.call-start = ((), (), s32[]{:S(2)}) async-start(), calls=%async_computation.4 | async-start | bytes 12255232 | tf_op jit(solution)/shard_map/all_gather | solution.py:95
  10.5 1297.8 %all-gather.15.cloned.1.call-start = ((), (), s32[]{:S(2)}) async-start(), calls=%async_computation.5 | async-start | bytes 12255232 | tf_op jit(solution)/shard_map/all_gather | solution.py:96
  190.9 1.9 copy-start.5
  192.8 5.5 copy-start.2
  198.3 40.8 %copy-start.1 = (bf16[1,384,2048]{2,1,0:T(8,128)(2,1)S(1)}, bf16[1,384,2048]{2,1,0:T(8,128)(2,1)}, u32[]{:S(2)}) copy-start(bf16[1,384,2048]{2,1,0:T(8,128)(2,1)} %param.12) | copy-start | bytes 4718596
  246.4 1.1 copy-start.3
  246.4 1.1 copy-start.11
  247.9 16.0 %copy-start.10 = (pred[64,48]{1,0:T(8,128)(4,1)S(1)}, pred[64,48]{1,0:T(8,128)(4,1)}, u32[]{:S(2)}) copy-start(pred[64,48]{1,0:T(8,128)(4,1)} %broadcast_in_dim.57) | copy-start | bytes 9220
  274.6 144.6 %all-to-all-start = ((bf16[64,48,2048]{2,1,0:T(8,128)(2,1)}), bf16[64,48,2048]{2,1,0:T(8,128)(2,1)}, u32[]{:S(2)}, u32[]{:S(2)}) async-start(bf16[64,48,2048]{2,1,0:T(8,128)(2,1)} %broadcast_select_fusion), calls=%async_computation | async-start | bytes 25165824 | tf_op jit(solution)/shard_map/all_to_all | solution.py:108
  280.7 1027.6 %all-gather.17.cloned.1.call-start = ((), (), s32[]{:S(2)}) async-start(), calls=%async_computation.6 | async-start | bytes 12255232 | tf_op jit(solution)/shard_map/all_gather | solution.py:97
  1099.5 7.7 copy-start.7
  1099.5 7.7 copy-start.9
  1099.5 8.1 copy-start.13
  1099.5 22.5 %copy-start.4 = (bf16[384,2048]{1,0:T(8,128)(2,1)S(1)}, bf16[384,2048]{1,0:T(8,128)(2,1)}, u32[]{:S(2)}) copy-start(bf16[384,2048]{1,0:T(8,128)(2,1)} %copy-done.3) | copy-start | bytes 4718596
  1099.5 22.5 %copy-start.12 = (f32[384]{0:T(512)S(1)}, f32[384]{0:T(512)}, u32[]{:S(2)}) copy-start(f32[384]{0:T(512)} %copy-done.11) | copy-start | bytes 4612
  1099.5 146.1 %all-to-all-start.1 = ((bf16[8,384,2048]{2,0,1:T(8,128)(2,1)}), bf16[8,384,2048]{2,0,1:T(8,128)(2,1)}, u32[]{:S(2)}, u32[]{:S(2)}) async-start(bf16[8,384,2048]{2,0,1:T(8,128)(2,1)} %copy.44), calls=%async_computation.1 | async-start | bytes 25165824 | tf_op jit(solution)/shard_map/all_to_all | solution.py:110
Sparse Core Ops, SparseCore 0:
  9.5 157.1 all-gather.8
  168.8 70.3 all-gather.10
  241.3 261.0 all-gather.18
  504.4 261.0 all-gather.20
  767.5 267.1 all-gather.22
  1036.6 85.2 all-gather.12
  1124.1 84.4 all-gather.14
  1210.7 90.6 all-gather.16
where the time goes:
time: 1350 us; the launch traced here: 1340 us
  waiting for transfers between devices  1020 us (76%)
  matrix products  150 us (11%)
  local copies, waits for them, and re-layouts  114 us (8%)
  other arithmetic  21.6 us (2%)
  starting transfers between devices  14.1 us (1%)
  between operations  14.1 us (1%)
    all_gather x1, waiting for transfers between devices, local_step(): down_full = lax.all_gather(w_down, 'fsdp', axis=2, tiled=True)  269 us
    all_gather x1, waiting for transfers between devices, local_step(): up_full = lax.all_gather(w_up, 'fsdp', axis=1, tiled=True)  231 us
    all_gather x1, waiting for transfers between devices, local_step(): qkv_full = lax.all_gather(w_qkv, 'fsdp', axis=0, tiled=True)  143 us
    all_to_all x1, waiting for transfers between devices, local_step(): received = lax.all_to_all(buffer, 'ep', 0, 1, tiled=True)  138 us
    all_to_all x1, waiting for transfers between devices, local_step(): returned = lax.all_to_all(expert_out, 'ep', 1, 0, tiled=True)  114 us
    all_gather x1, waiting for transfers between devices, local_step(): gate_full = lax.all_gather(w_gate, 'fsdp', axis=1, tiled=True)  72.4 us
    dot_general x1, matrix products, expert_ffn(): jnp.einsum('ecf,efd->ecd', inner_act, down_w, preferred_element_type=jnp....  50.3 us
    gather x2, local copies, waits for them, and re-layouts, combine_rows(): jnp.take(expert_out.reshape(n_experts * capacity, model_dim), source_row,...  40.1 us
  transfers between devices with their start and end apart: 10, of which 8 were waited for; matrix products, arithmetic and copies ran while one was open for 20% of the time, Pallas kernels for 0%

commit v1 on v0

v1 whole, which is shorter than its diff:
```python
import jax
import jax.numpy as jnp
from jax import lax
from jax.sharding import Mesh, PartitionSpec as P

HEAD_DIM = 128
ROPE_BASE = 10000.0
EPSILON = 1e-6
ALL = ("fsdp", "x", "core")
SWAP = [(0, 1), (1, 0)]


def rms_norm(values):
    vals_f32 = values.astype(jnp.float32)
    mean_sq = jnp.mean(vals_f32 * vals_f32, axis=-1, keepdims=True)
    return (vals_f32 * lax.rsqrt(mean_sq + EPSILON)).astype(jnp.bfloat16)


def rotary_embed(heads_in, positions):
    half_dim = HEAD_DIM // 2
    inv_freq = ROPE_BASE ** (-jnp.arange(half_dim, dtype=jnp.float32) * (2.0 / HEAD_DIM))
    angles = positions[:, None] * inv_freq[None, :]
    cos_tab = jnp.cos(angles)[:, None, :]
    sin_tab = jnp.sin(angles)[:, None, :]
    vals_f32 = heads_in.astype(jnp.float32)
    first_half = vals_f32[..., :half_dim]
    second_half = vals_f32[..., half_dim:]
    rotated = jnp.concatenate([first_half * cos_tab - second_half * sin_tab, second_half * cos_tab + first_half * sin_tab], axis=-1)
    return rotated.astype(jnp.bfloat16)


def attention_block(x_in, qkv_weight, out_weight):
    n_batch, seq_len, model_dim = x_in.shape
    n_heads = qkv_weight.shape[1] // (3 * HEAD_DIM)
    normed = rms_norm(x_in)
    qkv_proj = jnp.einsum("bsd,dn->bsn", normed, qkv_weight, preferred_element_type=jnp.float32).astype(jnp.bfloat16)
    qkv_proj = qkv_proj.reshape(n_batch, seq_len, 3, n_heads, HEAD_DIM)
    positions = jnp.arange(seq_len, dtype=jnp.float32)
    query_rot = rotary_embed(qkv_proj[:, :, 0], positions)
    key_rot = rotary_embed(qkv_proj[:, :, 1], positions)
    scores = jnp.einsum("bqhd,bkhd->bhqk", query_rot, key_rot, preferred_element_type=jnp.float32) * (HEAD_DIM ** -0.5)
    causal = jnp.arange(seq_len)[:, None] >= jnp.arange(seq_len)[None, :]
    attn_probs = jax.nn.softmax(jnp.where(causal, scores, -1e30), axis=-1).astype(jnp.bfloat16)
    attn_mixed = jnp.einsum("bhqk,bkhd->bqhd", attn_probs, qkv_proj[:, :, 2], preferred_element_type=jnp.float32).astype(jnp.bfloat16)
    attn_out = jnp.einsum("bsn,nm->bsm", attn_mixed.reshape(n_batch, seq_len, n_heads * HEAD_DIM), out_weight, preferred_element_type=jnp.float32)
    return (x_in.astype(jnp.float32) + attn_out).astype(jnp.bfloat16)


def capacity_for(n_tokens, top_k, n_experts):
    return ((5 * n_tokens * top_k) // (4 * n_experts) + 7) // 8 * 8


def nt_dot(lhs, rhs):
    return lax.dot_general(lhs, rhs, (((1,), (1,)), ((), ())), preferred_element_type=jnp.float32)


def solution(mesh):
    n_f, n_ep = mesh.shape["fsdp"], mesh.shape["ep"]
    n_core = 2
    n_x = n_ep // n_core
    phys = Mesh(mesh.devices.reshape(n_f, n_x, n_core), ALL)
    tok_spec = P(ALL)
    row_spec = P("fsdp", None)
    ep = ("x", "core")

    def gather_rows(shard):
        part = shard.shape[0] // n_ep
        mine = lax.axis_index("x") * n_core + lax.axis_index("core")
        piece = lax.dynamic_slice_in_dim(shard, mine * part, part, 0)
        return lax.all_gather(piece, ALL, axis=0, tiled=True)

    def collect_expert(shard):
        core = lax.axis_index("core")
        n_loc, depth, width = shard.shape
        half = depth // n_core
        keep = lax.dynamic_slice_in_dim(shard, core * half, half, 1)
        give = lax.dynamic_slice_in_dim(shard, (1 - core) * half, half, 1)
        got = lax.ppermute(give, "core", SWAP)
        first = core == 0
        both = jnp.concatenate([jnp.where(first, keep, got), jnp.where(first, got, keep)], axis=0)
        mine = lax.all_to_all(both, "fsdp", 0, 0, tiled=True)
        other = lax.ppermute(mine, "core", SWAP)
        whole = jnp.stack([jnp.where(first, mine, other), jnp.where(first, other, mine)], axis=1)
        return whole.reshape(n_f * depth, width)

    def local_step(x_in, w_qkv, w_out, w_gate, w_up, w_down, ws_gate, ws_up, ws_down, expert_ids, slot_ids, gate_vals):
        n_batch, seq_len, model_dim = x_in.shape
        n_tokens = n_batch * seq_len
        top_k = expert_ids.shape[-1]
        n_experts = w_gate.shape[0] * n_ep
        capacity = capacity_for(n_tokens, top_k, n_experts)
        part = capacity // n_core
        n_rows = n_experts * capacity
        s_ff = ws_gate.shape[1]

        qkv_full = gather_rows(w_qkv)
        out_full = gather_rows(w_out)
        gate_w = collect_expert(w_gate)
        up_w = collect_expert(w_up)
        down_w = collect_expert(jnp.swapaxes(w_down, 1, 2))
        shared_full = gather_rows(jnp.concatenate([ws_gate, ws_up, ws_down.T], axis=1))

        ids = expert_ids.reshape(n_tokens, top_k)
        slots = slot_ids.reshape(n_tokens, top_k)
        gates = gate_vals.reshape(n_tokens, top_k)
        kept = slots >= 0
        dest = ((ids % n_f) * n_x + ids // n_f) * n_core + slots // part
        row = jnp.where(kept, dest * part + slots % part, n_rows)
        source_tok = jnp.arange(n_tokens * top_k, dtype=jnp.int32) // top_k
        row_source = jnp.full((n_rows,), n_tokens, jnp.int32).at[row.reshape(-1)].set(source_tok, mode="drop")
        row_gate = jnp.zeros((n_rows,), gates.dtype).at[row.reshape(-1)].set(gates.reshape(-1), mode="drop")
        tok_iota = jnp.arange(n_tokens, dtype=jnp.int32)
        pick = (row_source[:, None] == tok_iota[None, :])
        spread = pick.astype(jnp.bfloat16)
        merge = jnp.where(row_source[None, :] == tok_iota[:, None], row_gate[None, :], jnp.zeros((), gates.dtype))

        hidden = attention_block(x_in, qkv_full, out_full).reshape(n_tokens, model_dim)
        normed = rms_norm(hidden)
        buffer = jnp.dot(spread, normed, preferred_element_type=jnp.float32).astype(jnp.bfloat16)
        received = lax.all_to_all(buffer.reshape(n_f * n_ep, part, model_dim), ALL, 0, 0, tiled=True)
        rows_in = received.reshape(n_rows, model_dim)
        gate_act = jnp.dot(rows_in, gate_w, preferred_element_type=jnp.float32)
        up_act = jnp.dot(rows_in, up_w, preferred_element_type=jnp.float32)
        inner = (jax.nn.silu(gate_act) * up_act).astype(jnp.bfloat16)
        expert_out = nt_dot(inner, down_w).astype(jnp.bfloat16)
        returned = lax.all_to_all(expert_out.reshape(n_f * n_ep, part, model_dim), ALL, 0, 0, tiled=True)
        routed = jnp.dot(merge, returned.reshape(n_rows, model_dim), preferred_element_type=jnp.float32)

        s_gate = jnp.dot(normed, shared_full[:, :s_ff], preferred_element_type=jnp.float32)
        s_up = jnp.dot(normed, shared_full[:, s_ff:2 * s_ff], preferred_element_type=jnp.float32)
        s_inner = (jax.nn.silu(s_gate) * s_up).astype(jnp.bfloat16)
        shared_out = nt_dot(s_inner, shared_full[:, 2 * s_ff:])
        summed = hidden.astype(jnp.float32) + shared_out + routed
        return summed.astype(jnp.bfloat16).reshape(n_batch, seq_len, model_dim)

    return jax.shard_map(local_step, mesh=phys, in_specs=(tok_spec, row_spec, row_spec, P(ep, "fsdp", None), P(ep, "fsdp", None), P(ep, None, "fsdp"), row_spec, row_spec, P(None, "fsdp"), tok_spec, tok_spec, tok_spec), out_specs=tok_spec, check_vma=False)
```

time: 1350 us -> 795 us (0.59)
  the two profiles are of different devices: /device:TPU:1 before, /device:TPU:121 now
where the time goes in v1:
time: 795 us; the launch traced here: 786 us
  waiting for transfers between devices  461 us (58%)
  matrix products  156 us (20%)
  local copies, waits for them, and re-layouts  70.2 us (9%)
  starting transfers between devices  48.9 us (6%)
  other arithmetic  35.7 us (4%)
  between operations  13.7 us (2%)
    all_to_all x1, waiting for transfers between devices, local_step(): lax.all_to_all(buffer.reshape(n_f * n_ep, part, model_dim), ALL, 0, 0, ti...  186 us
    all_to_all x1, waiting for transfers between devices, local_step(): lax.all_to_all(expert_out.reshape(n_f * n_ep, part, model_dim), ALL, 0, 0...  133 us
    all_gather x3, waiting for transfers between devices, gather_rows(): return lax.all_gather(piece, ALL, axis=0, tiled=True)  114 us
    dot_general x2, matrix products, nt_dot(): lax.dot_general(lhs, rhs, (((1,), (1,)), ((), ())), preferred_element_typ...  40.7 us
    dot_general x1, matrix products, local_step(): up_act = jnp.dot(rows_in, up_w, preferred_element_type=jnp.float32)  26.2 us
    dot_general x1, matrix products, local_step(): gate_act = jnp.dot(rows_in, gate_w, preferred_element_type=jnp.float32)  26 us
    all_to_all x3, waiting for transfers between devices, collect_expert(): mine = lax.all_to_all(both, 'fsdp', 0, 0, tiled=True)  23.4 us
    all_to_all x3, starting transfers between devices, collect_expert(): mine = lax.all_to_all(both, 'fsdp', 0, 0, tiled=True)  21.6 us
  transfers between devices with their start and end apart: 14, of which 6 were waited for; matrix products, arithmetic and copies ran while one was open for 31% of the time, Pallas kernels for 0%

profile of v1, /device:TPU:121, one launch (start us, length us, event | category | flops | bytes accessed | tf_op | source)
XLA Modules:
  0.0 785.7 jit_solution(12058086743883275057)
XLA Ops:
  18.2 6.8 constant_dynamic-slice_fusion.1
  25.0 4.1 copy.61
  30.7 3.7 broadcast_select_fusion.1
  36.4 6.4 all-to-all-start.1
  44.5 4.2 copy.60
  49.0 9.0 %scatter_custom_fusion = s32[3072]{0:T(1024)S(1)} fusion(s32[2304]{0:T(1024)S(1)} %fusion.63, s32[2304]{0:T(1024)S(1)} %add_select_fusion, s32[]{:T(128)} %constant.93.clone.1), kind=kCustom, calls=%fused_computation.118 | custom fusion | bytes 12292 | tf_op jit(solution)/shard_map/scatter | solution.py:110
  66.7 23.4 %all-to-all-done.1 = bf16[16,64,1408]{2,1,0:T(8,128)(2,1)} async-done(((bf16[16,64,1408]{2,1,0:T(8,128)(2,1)}), bf16[16,64,1408]{2,1,0:T(8,128)(2,1)}, u32[]{:S(2)}, u32[]{:S(2)}) %all-to-all-start.1) | async-done | bytes 2883616 | tf_op jit(solution)/shard_map/all_to_all | solution.py:81
  90.1 8.1 %all-to-all-start.2 = ((bf16[16,64,1408]{2,1,0:T(8,128)(2,1)}), bf16[16,64,1408]{2,1,0:T(8,128)(2,1)}, u32[]{:S(2)}, u32[]{:S(2)}) async-start(bf16[16,64,1408]{2,1,0:T(8,128)(2,1)} %pad_maximum_fusion.4), calls=%async_computation.2 | async-start | bytes 5767168 | tf_op jit(solution)/shard_map/all_to_all | solution.py:81
  98.3 62.9 %all-gather.4.cloned.1.call-done = bf16[2048,6144]{1,0:T(8,128)(2,1)} async-done(((bf16[16,6144]{1,0:T(8,128)(2,1)}), bf16[2048,6144]{1,0:T(8,128)(2,1)}) %all-gather.4.cloned.1.call-update) | async-done | bytes 25165840 | tf_op jit(solution)/shard_map/all_gather | solution.py:70
  161.2 15.0 %fusion.33 = bf16[48,8,48,128]{3,1,2,0:T(8,128)(2,1)S(1)} fusion(bf16[2048,6144]{1,0:T(8,128)(2,1)} %all-gather.4.cloned.1.call-done, bf16[1,384,2048]{2,1,0:T(8,128)(2,1)S(1)} %copy-done.3, f32[384]{0:T(512)S(1)} %add_rsqrt_fusion.1), kind=kOutput, calls=%fused_computation.59 | convolution fusion | flops 9668395008 | bytes 31458816 | tf_op jit(solution)/shard_map/bsd,dn->bsn/dot_general | solution.py:36
  179.5 2.9 copy.57
  187.2 5.1 fusion.82
  192.3 7.1 all-to-all-start.3
  199.5 6.2 fusion.35
  205.6 51.0 %all-gather.6.cloned.1.call-done = bf16[2048,2048]{1,0:T(8,128)(2,1)} async-done(((bf16[16,2048]{1,0:T(8,128)(2,1)}), bf16[2048,2048]{1,0:T(8,128)(2,1)}) %all-gather.6.cloned.1.call-update) | async-done | bytes 8388624 | tf_op jit(solution)/shard_map/all_gather | solution.py:70
  256.6 7.7 fusion.24
  265.4 10.2 %convolution_convert_fusion.1 = bf16[3072,2048]{1,0:T(8,128)(2,1)} fusion(s32[3072]{0:T(1024)S(1)} %scatter_custom_fusion, bf16[384,2048]{1,0:T(8,128)(2,1)S(1)} %get-tuple-element.37, f32[384]{0:T(512)S(1)} %add_rsqrt_fusion), kind=kOutput, calls=%fused_computation.11 | convolution fusion | flops 4841668608 | bytes 14169600 | tf_op jit(solution)/shard_map/dot_general | solution.py:119
  275.6 9.6 %all-to-all-start = ((bf16[128,24,2048]{2,1,0:T(8,128)(2,1)}), bf16[128,24,2048]{2,1,0:T(8,128)(2,1)}, u32[]{:S(2)}, u32[]{:S(2)}) async-start(bf16[128,24,2048]{2,1,0:T(8,128)(2,1)} %bitcast.86), calls=%async_computation | async-start | bytes 25165824 | tf_op jit(solution)/shard_map/all_to_all | solution.py:120
  286.2 4.4 collective-permute-done.3
  293.5 3.0 copy.52
  299.5 3.0 copy.55
  304.9 3.1 pad_maximum_fusion
  308.0 185.7 %all-to-all-done = bf16[128,24,2048]{2,1,0:T(8,128)(2,1)} async-done(((bf16[128,24,2048]{2,1,0:T(8,128)(2,1)}), bf16[128,24,2048]{2,1,0:T(8,128)(2,1)}, u32[]{:S(2)}, u32[]{:S(2)}) %all-to-all-start) | async-done | bytes 12582944 | tf_op jit(solution)/shard_map/all_to_all | solution.py:120
  493.6 26.0 %fusion.83 = f32[3072,1408]{1,0:T(8,128)} fusion(bf16[3072,2048]{1,0:T(8,128)(2,1)} %bitcast.18, bf16[2048,1408]{1,0:T(8,128)(2,1)} %bitcast.94), kind=kOutput, calls=%fused_computation.142 | convolution fusion | flops 17716740096 | bytes 35651584 | tf_op jit(solution)/shard_map/dot_general | solution.py:122
  519.7 26.2 %multiply_convert_fusion.clone.4 = bf16[3072,1408]{1,0:T(8,128)(2,1)} fusion(f32[3072,1408]{1,0:T(8,128)} %fusion.83, bf16[3072,2048]{1,0:T(8,128)(2,1)} %bitcast.18, bf16[2048,1408]{1,0:T(8,128)(2,1)S(1)} %bitcast.90), kind=kOutput, calls=%fused_computation.3.clone.clone.clone.1 | convolution fusion | flops 17742692352 | bytes 44302336 | tf_op jit(solution)/shard_map/dot_general | solution.py:123
  545.9 23.6 %convolution_convert_fusion = bf16[3072,2048]{1,0:T(8,128)(2,1)} fusion(bf16[2048,1408]{1,0:T(8,128)(2,1)S(1)} %bitcast.93, bf16[3072,1408]{1,0:T(8,128)(2,1)} %multiply_convert_fusion.clone.4), kind=kOutput, calls=%fused_computation.10 | convolution fusion | flops 17723031552 | bytes 27000832 | tf_op jit(solution)/shard_map/dot_general | solution.py:54
  569.5 15.4 %all-to-all-start.4 = ((bf16[128,24,2048]{2,1,0:T(8,128)(2,1)}), bf16[128,24,2048]{2,1,0:T(8,128)(2,1)}, u32[]{:S(2)}, u32[]{:S(2)}) async-start(bf16[128,24,2048]{2,1,0:T(8,128)(2,1)} %bitcast.87), calls=%async_computation.4 | async-start | bytes 25165824 | tf_op jit(solution)/shard_map/all_to_all | solution.py:126
  585.2 20.8 %scatter_custom_fusion.1 = bf16[3072]{0:T(1024)(128)(2,1)S(1)} fusion(s32[2304]{0:T(1024)} %copy-done.9, bf16[2304]{0:T(1024)(128)(2,1)S(1)} %reshape.431, bf16[]{:T(256)} %constant.101.clone.1), kind=kCustom, calls=%fused_computation.123 | custom fusion | bytes 6656 | tf_op jit(solution)/shard_map/scatter | solution.py:111
  606.1 11.1 %fusion.5 = f32[384,2816]{1,0:T(8,128)} fusion(bf16[2048,8448]{1,0:T(8,128)(2,1)} %all-gather.8.cloned.1.call-done, bf16[384,2048]{1,0:T(8,128)(2,1)S(1)} %copy-done.17, f32[384]{0:T(512)S(1)} %copy-done.15), kind=kOutput, calls=%fused_computation.8 | convolution fusion | flops 4431544320 | bytes 17434112 | tf_op jit(solution)/shard_map/dot_general | solution.py:129
  617.2 17.1 %fusion.1 = f32[384,2048]{1,0:T(8,128)} fusion(bf16[2048,8448]{1,0:T(8,128)(2,1)} %all-gather.8.cloned.1.call-done, f32[384,2816]{1,0:T(8,128)} %fusion.5, bf16[384,2048]{1,0:T(8,128)(2,1)S(1)} %copy-done.17, f32[384]{0:T(512)S(1)} %copy-done.15), kind=kOutput, calls=%fused_computation.4 | convolution fusion | flops 8867217408 | bytes 32114176 | tf_op jit(solution)/shard_map/dot_general | solution.py:54
  634.3 133.3 %all-to-all-done.4 = bf16[128,24,2048]{2,1,0:T(8,128)(2,1)} async-done(((bf16[128,24,2048]{2,1,0:T(8,128)(2,1)}), bf16[128,24,2048]{2,1,0:T(8,128)(2,1)}, u32[]{:S(2)}, u32[]{:S(2)}) %all-to-all-start.4) | async-done | bytes 12582944 | tf_op jit(solution)/shard_map/all_to_all | solution.py:126
  767.7 11.4 %fusion.28 = bf16[1,384,2048]{2,1,0:T(8,128)(2,1)} fusion(bf16[3072,2048]{1,0:T(8,128)(2,1)} %bitcast.32, f32[384,2048]{1,0:T(8,128)} %fusion.1, bf16[384,2048]{1,0:T(8,128)(2,1)S(1)} %copy-done.17, s32[3072]{0:T(1024)S(1)} %copy-done.11, bf16[3072]{0:T(1024)(128)(2,1)S(1)} %scatter_custom_fusion.1), kind=kOutput, calls=%fused_computation.55 | convolution fusion | flops 4837343232 | bytes 18892800 | tf_op jit(solution)/shard_map/dot_general | solution.py:127
  (108 shorter events, 44.6 us)
Async XLA Ops:
  6.5 154.7 %all-gather.4.cloned.1.call-start = ((), (), s32[]{:S(2)}) async-start(), calls=%async_computation.5 | async-start | bytes 25362432 | tf_op jit(solution)/shard_map/all_gather | solution.py:70
  8.7 247.9 %all-gather.6.cloned.1.call-start = ((), (), s32[]{:S(2)}) async-start(), calls=%async_computation.6 | async-start | bytes 8454144 | tf_op jit(solution)/shard_map/all_gather | solution.py:70
  10.2 595.9 %all-gather.8.cloned.1.call-start = ((), (), s32[]{:S(2)}) async-start(), calls=%async_computation.7 | async-start | bytes 34873344 | tf_op jit(solution)/shard_map/all_gather | solution.py:70
  14.8 14.8 %collective-permute-start = (bf16[8,64,1408]{2,1,0:T(8,128)(2,1)S(1)}, bf16[8,64,1408]{2,1,0:T(8,128)(2,1)S(1)}, u32[]{:S(2)}, u32[]{:S(2)}) collective-permute-start(bf16[8,64,1408]{2,1,0:T(8,128)(2,1)S(1)} %constant_dynamic-slice_fusion.3), channel_id=1, source_target_pairs={{0,1},{1,0},{2,3},{3,2},{4,5},{5,4},{6,7},{7,6},{8,9},{9,8},{10,11... | collective-permute-start | bytes 4325384 | tf_op jit(solution)/shard_map/ppermute | solution.py:78
  18.2 12.5 %collective-permute-start.2 = (bf16[8,64,1408]{2,1,0:T(8,128)(2,1)}, bf16[8,64,1408]{2,1,0:T(8,128)(2,1)}, u32[]{:S(2)}, u32[]{:S(2)}) collective-permute-start(bf16[8,64,1408]{2,1,0:T(8,128)(2,1)} %constant_dynamic-slice_fusion.2), channel_id=1, source_target_pairs={{0,1},{1,0},{2,3},{3,2},{4,5},{5,4},{6,7},{7,6},{8,9},{9,8},{10,11... | collective-permute-start | bytes 4325384 | tf_op jit(solution)/shard_map/ppermute | solution.py:78
  29.1 34.1 %collective-permute-start.4 = (bf16[8,64,1408]{2,1,0:T(8,128)(2,1)}, bf16[8,64,1408]{2,1,0:T(8,128)(2,1)}, u32[]{:S(2)}, u32[]{:S(2)}) collective-permute-start(bf16[8,64,1408]{2,1,0:T(8,128)(2,1)} %bitcast.27), channel_id=1, source_target_pairs={{0,1},{1,0},{2,3},{3,2},{4,5},{5,4},{6,7},{7,6},{8,9},{9,8},{10,11... | collective-permute-start | bytes 4325384 | tf_op jit(solution)/shard_map/ppermute | solution.py:78
  36.4 6.4 copy-start.8
  36.4 7.8 copy-start.12
  36.4 53.7 %all-to-all-start.1 = ((bf16[16,64,1408]{2,1,0:T(8,128)(2,1)}), bf16[16,64,1408]{2,1,0:T(8,128)(2,1)}, u32[]{:S(2)}, u32[]{:S(2)}) async-start(bf16[16,64,1408]{2,1,0:T(8,128)(2,1)} %pad_maximum_fusion.3), calls=%async_computation.1 | async-start | bytes 5767168 | tf_op jit(solution)/shard_map/all_to_all | solution.py:81
  49.0 14.2 %copy-start.9 = (s32[2304]{0:T(1024)}, s32[2304]{0:T(1024)S(1)}, u32[]{:S(2)}) copy-start(s32[2304]{0:T(1024)S(1)} %fusion.63) | copy-start | bytes 27652
  58.0 206.3 %copy-start.10 = (s32[3072]{0:T(1024)}, s32[3072]{0:T(1024)S(1)}, u32[]{:S(2)}) copy-start(s32[3072]{0:T(1024)S(1)} %scatter_custom_fusion) | copy-start | bytes 36868
  60.5 2.7 copy-start.2
  66.7 94.5 %copy-start.3 = (bf16[1,384,2048]{2,1,0:T(8,128)(2,1)S(1)}, bf16[1,384,2048]{2,1,0:T(8,128)(2,1)}, u32[]{:S(2)}) copy-start(bf16[1,384,2048]{2,1,0:T(8,128)(2,1)} %param.12) | copy-start | bytes 4718596
  90.1 102.2 %all-to-all-start.2 = ((bf16[16,64,1408]{2,1,0:T(8,128)(2,1)}), bf16[16,64,1408]{2,1,0:T(8,128)(2,1)}, u32[]{:S(2)}, u32[]{:S(2)}) async-start(bf16[16,64,1408]{2,1,0:T(8,128)(2,1)} %pad_maximum_fusion.4), calls=%async_computation.2 | async-start | bytes 5767168 | tf_op jit(solution)/shard_map/all_to_all | solution.py:81
  192.3 7.1 copy-start.5
  192.3 83.3 %all-to-all-start.3 = ((bf16[16,64,1408]{2,1,0:T(8,128)(2,1)}), bf16[16,64,1408]{2,1,0:T(8,128)(2,1)}, u32[]{:S(2)}, u32[]{:S(2)}) async-start(bf16[16,64,1408]{2,1,0:T(8,128)(2,1)} %pad_maximum_fusion.5), calls=%async_computation.3 | async-start | bytes 5767168 | tf_op jit(solution)/shard_map/all_to_all | solution.py:81
  199.5 57.1 %copy-start.4 = (bf16[1,384,2048]{2,1,0:T(8,128)(2,1)S(1)}, bf16[1,384,2048]{2,1,0:T(8,128)(2,1)}, u32[]{:S(2)}) copy-start(bf16[1,384,2048]{2,1,0:T(8,128)(2,1)} %param.12) | copy-start | bytes 4718596
  264.3 11.4 %copy-start.14 = (f32[384]{0:T(512)}, f32[384]{0:T(512)S(1)}, u32[]{:S(2)}) copy-start(f32[384]{0:T(512)S(1)} %add_rsqrt_fusion) | copy-start | bytes 4612
  275.6 218.0 %all-to-all-start = ((bf16[128,24,2048]{2,1,0:T(8,128)(2,1)}), bf16[128,24,2048]{2,1,0:T(8,128)(2,1)}, u32[]{:S(2)}, u32[]{:S(2)}) async-start(bf16[128,24,2048]{2,1,0:T(8,128)(2,1)} %bitcast.86), calls=%async_computation | async-start | bytes 25165824 | tf_op jit(solution)/shard_map/all_to_all | solution.py:120
  285.2 5.4 collective-permute-start.3
  285.7 10.8 %collective-permute-start.5 = (bf16[16,64,1408]{2,1,0:T(8,128)(2,1)}, bf16[16,64,1408]{2,1,0:T(8,128)(2,1)S(1)}, u32[]{:S(2)}, u32[]{:S(2)}) collective-permute-start(bf16[16,64,1408]{2,1,0:T(8,128)(2,1)} %all-to-all-done.3), channel_id=1, source_target_pairs={{0,1},{1,0},{2,3},{3,2},{4,5},{5,4},{6,7},{7,6},{8,9},{9,8},{10,11... | collective-permute-start | bytes 8650760 | tf_op jit(solution)/shard_map/ppermute | solution.py:82
  285.8 16.6 %collective-permute-start.1 = (bf16[16,64,1408]{2,1,0:T(8,128)(2,1)}, bf16[16,64,1408]{2,1,0:T(8,128)(2,1)S(1)}, u32[]{:S(2)}, u32[]{:S(2)}) collective-permute-start(bf16[16,64,1408]{2,1,0:T(8,128)(2,1)} %all-to-all-done.1), channel_id=1, source_target_pairs={{0,1},{1,0},{2,3},{3,2},{4,5},{5,4},{6,7},{7,6},{8,9},{9,8},{10,11... | collective-permute-start | bytes 8650760 | tf_op jit(solution)/shard_map/ppermute | solution.py:82
  304.9 214.8 %slice-start = ((s8[5767168]{0:T(1024)(128)(4,1)}), s8[1572864]{0:T(1024)(128)(4,1)S(1)}, s32[]{:S(2)}) async-start(s8[5767168]{0:T(1024)(128)(4,1)} %bitcast.88), calls=%async_computation.8 | async-start | bytes 3145728
  493.6 26.1 %slice-start.1 = ((s8[5767168]{0:T(1024)(128)(4,1)}), s8[4194304]{0:T(1024)(128)(4,1)S(1)}, s32[]{:S(2)}) async-start(s8[5767168]{0:T(1024)(128)(4,1)} %bitcast.88), calls=%async_computation.9 | async-start | bytes 8388608
  493.6 52.3 %slice-start.2 = ((s8[5767168]{0:T(1024)(128)(4,1)}), s8[4194304]{0:T(1024)(128)(4,1)S(1)}, s32[]{:S(2)}) async-start(s8[5767168]{0:T(1024)(128)(4,1)} %bitcast.91), calls=%async_computation.10 | async-start | bytes 8388608
  519.7 26.2 %slice-start.3 = ((s8[5767168]{0:T(1024)(128)(4,1)}), s8[1572864]{0:T(1024)(128)(4,1)S(1)}, s32[]{:S(2)}) async-start(s8[5767168]{0:T(1024)(128)(4,1)} %bitcast.91), calls=%async_computation.11 | async-start | bytes 3145728
  569.5 15.4 %copy-start.13 = (bf16[1,384,6]{1,2,0:T(8,128)(2,1)S(1)}, bf16[1,384,6]{1,2,0:T(8,128)(2,1)}, u32[]{:S(2)}) copy-start(bf16[1,384,6]{1,2,0:T(8,128)(2,1)} %param.23) | copy-start | bytes 13828
  569.5 36.6 %copy-start.15 = (f32[384]{0:T(512)S(1)}, f32[384]{0:T(512)}, u32[]{:S(2)}) copy-start(f32[384]{0:T(512)} %copy-done.14) | copy-start | bytes 4612
  569.5 36.6 %copy-start.17 = (bf16[384,2048]{1,0:T(8,128)(2,1)S(1)}, bf16[384,2048]{1,0:T(8,128)(2,1)}, u32[]{:S(2)}) copy-start(bf16[384,2048]{1,0:T(8,128)(2,1)} %copy-done.16) | copy-start | bytes 4718596
  569.5 198.1 %all-to-all-start.4 = ((bf16[128,24,2048]{2,1,0:T(8,128)(2,1)}), bf16[128,24,2048]{2,1,0:T(8,128)(2,1)}, u32[]{:S(2)}, u32[]{:S(2)}) async-start(bf16[128,24,2048]{2,1,0:T(8,128)(2,1)} %bitcast.87), calls=%async_computation.4 | async-start | bytes 25165824 | tf_op jit(solution)/shard_map/all_to_all | solution.py:126
  617.2 150.5 %copy-start.11 = (s32[3072]{0:T(1024)S(1)}, s32[3072]{0:T(1024)}, u32[]{:S(2)}) copy-start(s32[3072]{0:T(1024)} %copy-done.10) | copy-start | bytes 36868
  767.7 11.4 %copy-start.1 = (bf16[128,6144]{1,0:T(8,128)(2,1)S(1)}, bf16[128,6144]{1,0:T(8,128)(2,1)}, u32[]{:S(2)}) copy-start(bf16[128,6144]{1,0:T(8,128)(2,1)} %param.13) | copy-start | bytes 4718596
  (4 other events, 5.6 us)
Sparse Core Ops, SparseCore 0:
  10.4 150.7 all-gather.3
  164.2 92.3 all-gather.5
  259.6 231.1 all-gather.7

commit v2 on v1

--- a/solution.py
+++ b/solution.py
@@ -69,19 +69,21 @@
         piece = lax.dynamic_slice_in_dim(shard, mine * part, part, 0)
         return lax.all_gather(piece, ALL, axis=0, tiled=True)
 
-    def collect_expert(shard):
+    def stage_expert(shard):
         core = lax.axis_index("core")
-        n_loc, depth, width = shard.shape
-        half = depth // n_core
+        half = shard.shape[1] // n_core
         keep = lax.dynamic_slice_in_dim(shard, core * half, half, 1)
         give = lax.dynamic_slice_in_dim(shard, (1 - core) * half, half, 1)
         got = lax.ppermute(give, "core", SWAP)
         first = core == 0
-        both = jnp.concatenate([jnp.where(first, keep, got), jnp.where(first, got, keep)], axis=0)
+        return jnp.concatenate([jnp.where(first, keep, got), jnp.where(first, got, keep)], axis=0)
+
+    def collect_expert(both):
+        first = lax.axis_index("core") == 0
         mine = lax.all_to_all(both, "fsdp", 0, 0, tiled=True)
         other = lax.ppermute(mine, "core", SWAP)
         whole = jnp.stack([jnp.where(first, mine, other), jnp.where(first, other, mine)], axis=1)
-        return whole.reshape(n_f * depth, width)
+        return whole.reshape(-1, both.shape[2])
 
     def local_step(x_in, w_qkv, w_out, w_gate, w_up, w_down, ws_gate, ws_up, ws_down, expert_ids, slot_ids, gate_vals):
         n_batch, seq_len, model_dim = x_in.shape
@@ -93,11 +95,15 @@
         n_rows = n_experts * capacity
         s_ff = ws_gate.shape[1]
 
-        qkv_full = gather_rows(w_qkv)
-        out_full = gather_rows(w_out)
-        gate_w = collect_expert(w_gate)
-        up_w = collect_expert(w_up)
-        down_w = collect_expert(jnp.swapaxes(w_down, 1, 2))
+        n_qkv = w_qkv.shape[1]
+        attn_full = gather_rows(jnp.concatenate([w_qkv, w_out], axis=1))
+        gate_half = stage_expert(w_gate)
+        up_half = stage_expert(w_up)
+        down_half = stage_expert(jnp.swapaxes(w_down, 1, 2))
+        gate_w = collect_expert(gate_half)
+        attn_full, up_half, down_half = lax.optimization_barrier((attn_full, up_half, down_half))
+        up_w = collect_expert(up_half)
+        down_w = collect_expert(down_half)
         shared_full = gather_rows(jnp.concatenate([ws_gate, ws_up, ws_down.T], axis=1))
 
         ids = expert_ids.reshape(n_tokens, top_k)
@@ -105,26 +111,38 @@
         gates = gate_vals.reshape(n_tokens, top_k)
         kept = slots >= 0
         dest = ((ids % n_f) * n_x + ids // n_f) * n_core + slots // part
-        row = jnp.where(kept, dest * part + slots % part, n_rows)
+        spot = slots % part
         source_tok = jnp.arange(n_tokens * top_k, dtype=jnp.int32) // top_k
-        row_source = jnp.full((n_rows,), n_tokens, jnp.int32).at[row.reshape(-1)].set(source_tok, mode="drop")
-        row_gate = jnp.zeros((n_rows,), gates.dtype).at[row.reshape(-1)].set(gates.reshape(-1), mode="drop")
         tok_iota = jnp.arange(n_tokens, dtype=jnp.int32)
-        pick = (row_source[:, None] == tok_iota[None, :])
-        spread = pick.astype(jnp.bfloat16)
+        n_dev = n_f * n_ep
+        first_part = (2 * part // 3 + 7) // 8 * 8
+        bounds = ((0, first_part), (first_part, part))
+        low = spot < first_part
+        row = jnp.where(low, dest * first_part + spot, n_dev * first_part + dest * (part - first_part) + spot - first_part)
+        row = jnp.where(kept, row, n_rows).reshape(-1)
+        row_source = jnp.full((n_rows,), n_tokens, jnp.int32).at[row].set(source_tok, mode="drop")
+        row_gate = jnp.zeros((n_rows,), gates.dtype).at[row].set(gates.reshape(-1), mode="drop")
+        spread = (row_source[:, None] == tok_iota[None, :]).astype(jnp.bfloat16)
         merge = jnp.where(row_source[None, :] == tok_iota[:, None], row_gate[None, :], jnp.zeros((), gates.dtype))
 
-        hidden = attention_block(x_in, qkv_full, out_full).reshape(n_tokens, model_dim)
+        hidden = attention_block(x_in, attn_full[:, :n_qkv], attn_full[:, n_qkv:]).reshape(n_tokens, model_dim)
         normed = rms_norm(hidden)
-        buffer = jnp.dot(spread, normed, preferred_element_type=jnp.float32).astype(jnp.bfloat16)
-        received = lax.all_to_all(buffer.reshape(n_f * n_ep, part, model_dim), ALL, 0, 0, tiled=True)
-        rows_in = received.reshape(n_rows, model_dim)
-        gate_act = jnp.dot(rows_in, gate_w, preferred_element_type=jnp.float32)
-        up_act = jnp.dot(rows_in, up_w, preferred_element_type=jnp.float32)
-        inner = (jax.nn.silu(gate_act) * up_act).astype(jnp.bfloat16)
-        expert_out = nt_dot(inner, down_w).astype(jnp.bfloat16)
-        returned = lax.all_to_all(expert_out.reshape(n_f * n_ep, part, model_dim), ALL, 0, 0, tiled=True)
-        routed = jnp.dot(merge, returned.reshape(n_rows, model_dim), preferred_element_type=jnp.float32)
+        received = []
+        for lo, hi in bounds:
+            sl = slice(n_dev * lo, n_dev * hi)
+            buffer = jnp.dot(spread[sl], normed, preferred_element_type=jnp.float32).astype(jnp.bfloat16)
+            received.append(lax.all_to_all(buffer.reshape(n_dev, hi - lo, model_dim), ALL, 0, 0, tiled=True))
+        routed = None
+        for (lo, hi), got in zip(bounds, received):
+            sl = slice(n_dev * lo, n_dev * hi)
+            rows_in = got.reshape(n_dev * (hi - lo), model_dim)
+            gate_act = jnp.dot(rows_in, gate_w, preferred_element_type=jnp.float32)
+            up_act = jnp.dot(rows_in, up_w, preferred_element_type=jnp.float32)
+            inner = (jax.nn.silu(gate_act) * up_act).astype(jnp.bfloat16)
+            expert_out = nt_dot(inner, down_w).astype(jnp.bfloat16)
+            back = lax.all_to_all(expert_out.reshape(n_dev, hi - lo, model_dim), ALL, 0, 0, tiled=True)
+            term = jnp.dot(merge[:, sl], back.reshape(n_dev * (hi - lo), model_dim), preferred_element_type=jnp.float32)
+            routed = term if routed is None else routed + term
 
         s_gate = jnp.dot(normed, shared_full[:, :s_ff], preferred_element_type=jnp.float32)
         s_up = jnp.dot(normed, shared_full[:, s_ff:2 * s_ff], preferred_element_type=jnp.float32)

time: 795 us -> 685 us (0.86)
  the two profiles are of different devices: /device:TPU:121 before, /device:TPU:1 now
where the time goes in v2:
time: 685 us; the launch traced here: 673 us
  waiting for transfers between devices  308 us (45%)
  matrix products  175 us (26%)
  local copies, waits for them, and re-layouts  68.9 us (10%)
  starting transfers between devices  66.9 us (10%)
  other arithmetic  40.1 us (6%)
  between operations  14 us (2%)
    all_to_all x2, waiting for transfers between devices, local_step(): lax.all_to_all(buffer.reshape(n_dev, hi - lo, model_dim), ALL, 0, 0, tile...  117 us
    all_gather x2, waiting for transfers between devices, gather_rows(): return lax.all_gather(piece, ALL, axis=0, tiled=True)  75.9 us
    all_to_all x2, waiting for transfers between devices, local_step(): lax.all_to_all(expert_out.reshape(n_dev, hi - lo, model_dim), ALL, 0, 0,...  74.7 us
    dot_general x3, matrix products, nt_dot(): lax.dot_general(lhs, rhs, (((1,), (1,)), ((), ())), preferred_element_typ...  74 us
    all_to_all x3, waiting for transfers between devices, collect_expert(): mine = lax.all_to_all(both, 'fsdp', 0, 0, tiled=True)  34.5 us
    all_to_all x2, starting transfers between devices, local_step(): lax.all_to_all(expert_out.reshape(n_dev, hi - lo, model_dim), ALL, 0, 0,...  23.4 us
    all_to_all x3, starting transfers between devices, collect_expert(): mine = lax.all_to_all(both, 'fsdp', 0, 0, tiled=True)  21.9 us
    scatter x1, local copies, waits for them, and re-layouts, local_step(): jnp.zeros((n_rows,), gates.dtype).at[row]  20.8 us
  transfers between devices with their start and end apart: 15, of which 8 were waited for; matrix products, arithmetic and copies ran while one was open for 40% of the time, Pallas kernels for 0%

profile of v2, /device:TPU:1, one launch (start us, length us, event | category | flops | bytes accessed | tf_op | source)
XLA Modules:
  0.0 673.1 jit_solution(1736621634689022529)
XLA Ops:
  16.5 4.1 copy.58
  32.5 9.0 %scatter_custom_fusion = s32[3072]{0:T(1024)S(1)} fusion(s32[2304]{0:T(1024)S(1)} %fusion.88, s32[2304]{0:T(1024)S(1)} %add_select_fusion, s32[]{:T(128)} %constant.100.clone.1), kind=kCustom, calls=%fused_computation.135 | custom fusion | bytes 12292 | tf_op jit(solution)/shard_map/scatter | solution.py:123
  47.6 8.1 %all-to-all-start.1 = ((bf16[16,64,1408]{2,1,0:T(8,128)(2,1)}), bf16[16,64,1408]{2,1,0:T(8,128)(2,1)S(1)}, u32[]{:S(2)}, u32[]{:S(2)}) async-start(bf16[16,64,1408]{2,1,0:T(8,128)(2,1)} %pad_maximum_fusion.5), calls=%async_computation.1 | async-start | bytes 5767168 | tf_op jit(solution)/shard_map/all_to_all | solution.py:83
  67.1 75.8 %all-gather.3.cloned.1.call-done = bf16[2048,8192]{1,0:T(8,128)(2,1)} async-done(((bf16[16,8192]{1,0:T(8,128)(2,1)}), bf16[2048,8192]{1,0:T(8,128)(2,1)}) %all-gather.3.cloned.1.call-update) | async-done | bytes 33554448 | tf_op jit(solution)/shard_map/all_gather | solution.py:70
  144.5 7.1 %all-to-all-start.2 = ((bf16[16,64,1408]{2,1,0:T(8,128)(2,1)}), bf16[16,64,1408]{2,1,0:T(8,128)(2,1)S(1)}, u32[]{:S(2)}, u32[]{:S(2)}) async-start(bf16[16,64,1408]{2,1,0:T(8,128)(2,1)} %pad_maximum_fusion.3), calls=%async_computation.2 | async-start | bytes 5767168 | tf_op jit(solution)/shard_map/all_to_all | solution.py:83
  151.6 16.9 %fusion.54 = bf16[48,8,48,128]{3,1,2,0:T(8,128)(2,1)} fusion(bf16[2048,8192]{1,0:T(8,128)(2,1)} %all-gather.3.cloned.1.call-done, bf16[1,384,2048]{2,1,0:T(8,128)(2,1)} %param.12, f32[384]{0:T(512)S(1)} %add_rsqrt_fusion.1), kind=kOutput, calls=%fused_computation.71 | convolution fusion | flops 9668395008 | bytes 31458816 | tf_op jit(solution)/shard_map/bsd,dn->bsn/dot_general | solution.py:36
  184.2 5.1 fusion.107
  189.3 4.5 all-to-all-done.2
  193.8 6.8 %all-to-all-start.3 = ((bf16[16,64,1408]{2,1,0:T(8,128)(2,1)}), bf16[16,64,1408]{2,1,0:T(8,128)(2,1)}, u32[]{:S(2)}, u32[]{:S(2)}) async-start(bf16[16,64,1408]{2,1,0:T(8,128)(2,1)} %pad_maximum_fusion.4), calls=%async_computation.3 | async-start | bytes 5767168 | tf_op jit(solution)/shard_map/all_to_all | solution.py:83
  200.6 5.5 fusion.58
  206.1 7.4 %fusion.39 = (f32[384]{0:T(512)S(1)}, bf16[384,2048]{1,0:T(8,128)(2,1)S(1)}) fusion(bf16[384,2048]{0,1:T(8,128)(2,1)S(1)} %bitcast.116, bf16[2048,8192]{1,0:T(8,128)(2,1)} %all-gather.3.cloned.1.call-done, bf16[1,384,2048]{2,1,0:T(8,128)(2,1)S(1)} %copy-done.5), kind=kOutput, calls=%fused_computation.51 | convolution fusion | flops 3225943552 | bytes 13108736 | tf_op jit(solution)/shard_map/bsn,nm->bsm/dot_general | solution.py:45
  214.6 7.2 %convolution_convert_fusion.1 = bf16[2048,2048]{1,0:T(8,128)(2,1)} fusion(pred[3072,384]{1,0:T(32,128)(4,1)S(1)} %copy-done.6, bf16[384,2048]{1,0:T(8,128)(2,1)S(1)} %get-tuple-element.43, f32[384]{0:T(512)S(1)} %add_rsqrt_fusion), kind=kOutput, calls=%fused_computation.19 | convolution fusion | flops 3227779072 | bytes 10749952 | tf_op jit(solution)/shard_map/dot_general | solution.py:133
  221.8 30.1 %all-to-all-done.3 = bf16[16,64,1408]{2,1,0:T(8,128)(2,1)} async-done(((bf16[16,64,1408]{2,1,0:T(8,128)(2,1)}), bf16[16,64,1408]{2,1,0:T(8,128)(2,1)}, u32[]{:S(2)}, u32[]{:S(2)}) %all-to-all-start.3) | async-done | bytes 2883616 | tf_op jit(solution)/shard_map/all_to_all | solution.py:83
  251.9 6.6 all-to-all-start
  260.4 5.8 collective-permute-done.3
  271.5 4.5 convert_bitcast_fusion.1
  285.9 112.4 %all-to-all-done = bf16[128,16,2048]{2,1,0:T(8,128)(2,1)} async-done(((bf16[128,16,2048]{2,1,0:T(8,128)(2,1)}), bf16[128,16,2048]{2,1,0:T(8,128)(2,1)}, u32[]{:S(2)}, u32[]{:S(2)}) %all-to-all-start) | async-done | bytes 8388640 | tf_op jit(solution)/shard_map/all_to_all | solution.py:134
  398.3 11.2 %all-to-all-start.5 = ((bf16[128,8,2048]{2,1,0:T(8,128)(2,1)}), bf16[128,8,2048]{2,1,0:T(8,128)(2,1)}, u32[]{:S(2)}, u32[]{:S(2)}) async-start(bf16[128,8,2048]{2,1,0:T(8,128)(2,1)} %convert_bitcast_fusion.1), calls=%async_computation.5 | async-start | bytes 8388608 | tf_op jit(solution)/shard_map/all_to_all | solution.py:134
  409.5 18.5 %fusion.108 = f32[2048,1408]{1,0:T(8,128)} fusion(bf16[2048,2048]{1,0:T(8,128)(2,1)} %bitcast.20, bf16[2048,1408]{1,0:T(8,128)(2,1)} %bitcast.108), kind=kOutput, calls=%fused_computation.156 | convolution fusion | flops 11811160064 | bytes 25690112 | tf_op jit(solution)/shard_map/dot_general | solution.py:139
  428.0 35.1 %convolution_convert_fusion = bf16[2048,2048]{1,0:T(8,128)(2,1)} fusion(bf16[2048,1408]{1,0:T(8,128)(2,1)} %bitcast.112, f32[2048,1408]{1,0:T(8,128)} %fusion.108, bf16[2048,2048]{1,0:T(8,128)(2,1)} %bitcast.20, bf16[2048,1408]{1,0:T(8,128)(2,1)} %bitcast.110), kind=kOutput, calls=%fused_computation.18 | convolution fusion | flops 23643815936 | bytes 39845888 | tf_op jit(solution)/shard_map/dot_general | solution.py:54
  463.1 4.9 all-to-all-done.5
  468.0 9.5 %all-to-all-start.4 = ((bf16[128,16,2048]{2,1,0:T(8,128)(2,1)}), bf16[128,16,2048]{2,1,0:T(8,128)(2,1)}, u32[]{:S(2)}, u32[]{:S(2)}) async-start(bf16[128,16,2048]{2,1,0:T(8,128)(2,1)} %bitcast.107), calls=%async_computation.4 | async-start | bytes 16777216 | tf_op jit(solution)/shard_map/all_to_all | solution.py:143
  477.9 20.8 %scatter_custom_fusion.1 = bf16[3072]{0:T(1024)(128)(2,1)S(1)} fusion(s32[2304]{0:T(1024)} %copy-done.11, bf16[2304]{0:T(1024)(128)(2,1)S(1)} %reshape.464, bf16[]{:T(256)} %constant.110.clone.1), kind=kCustom, calls=%fused_computation.140 | custom fusion | bytes 6656 | tf_op jit(solution)/shard_map/scatter | solution.py:124
  499.5 11.7 %fusion.30 = f32[1024,1408]{1,0:T(8,128)} fusion(bf16[2048,1408]{1,0:T(8,128)(2,1)} %bitcast.111, bf16[128,8,2048]{2,1,0:T(8,128)(2,1)} %all-to-all-done.5), kind=kOutput, calls=%fused_computation.42 | convolution fusion | flops 5905580032 | bytes 15728640 | tf_op jit(solution)/shard_map/dot_general | solution.py:140
  511.2 20.9 %convert_bitcast_fusion = bf16[128,8,2048]{2,1,0:T(8,128)(2,1)} fusion(bf16[2048,1408]{1,0:T(8,128)(2,1)} %bitcast.113, f32[1024,1408]{1,0:T(8,128)} %fusion.30, bf16[2048,1408]{1,0:T(8,128)(2,1)} %bitcast.109, bf16[128,8,2048]{2,1,0:T(8,128)(2,1)} %all-to-all-done.5), kind=kOutput, calls=%fused_computation.46 | convolution fusion | flops 11821907968 | bytes 25690112 | tf_op jit(solution)/shard_map/dot_general | solution.py:54
  532.1 54.2 %all-to-all-done.4 = bf16[128,16,2048]{2,1,0:T(8,128)(2,1)} async-done(((bf16[128,16,2048]{2,1,0:T(8,128)(2,1)}), bf16[128,16,2048]{2,1,0:T(8,128)(2,1)}, u32[]{:S(2)}, u32[]{:S(2)}) %all-to-all-start.4) | async-done | bytes 8388640 | tf_op jit(solution)/shard_map/all_to_all | solution.py:143
  586.2 13.9 %all-to-all-start.6 = ((bf16[128,8,2048]{2,1,0:T(8,128)(2,1)}), bf16[128,8,2048]{2,1,0:T(8,128)(2,1)}, u32[]{:S(2)}, u32[]{:S(2)}) async-start(bf16[128,8,2048]{2,1,0:T(8,128)(2,1)} %convert_bitcast_fusion), calls=%async_computation.6 | async-start | bytes 8388608 | tf_op jit(solution)/shard_map/all_to_all | solution.py:143
  600.1 11.6 %fusion.7 = f32[384,2816]{1,0:T(8,128)} fusion(bf16[2048,8448]{1,0:T(8,128)(2,1)} %all-gather.5.cloned.1.call-done, bf16[384,2048]{1,0:T(8,128)(2,1)} %copy-done.16, f32[384]{0:T(512)S(1)} %copy-done.15), kind=kOutput, calls=%fused_computation.9 | convolution fusion | flops 4431544320 | bytes 17434112 | tf_op jit(solution)/shard_map/dot_general | solution.py:147
  611.7 18.0 %fusion.3 = f32[384,2048]{1,0:T(8,128)} fusion(bf16[2048,8448]{1,0:T(8,128)(2,1)} %all-gather.5.cloned.1.call-done, f32[384,2816]{1,0:T(8,128)} %fusion.7, bf16[384,2048]{1,0:T(8,128)(2,1)} %copy-done.16, f32[384]{0:T(512)S(1)} %copy-done.15), kind=kOutput, calls=%fused_computation.5 | convolution fusion | flops 8867217408 | bytes 32114176 | tf_op jit(solution)/shard_map/dot_general | solution.py:54
  629.7 8.5 %fusion.65 = f32[384,2048]{1,0:T(8,128)} fusion(bf16[2048,2048]{1,0:T(8,128)(2,1)} %bitcast.32, bf16[384,3072]{1,0:T(8,128)(2,1)S(1)} %fusion.18), kind=kOutput, calls=%fused_computation.84 | convolution fusion | flops 3221225472 | bytes 13107200 | tf_op jit(solution)/shard_map/dot_general | solution.py:144
  638.1 20.5 %all-to-all-done.6 = bf16[128,8,2048]{2,1,0:T(8,128)(2,1)} async-done(((bf16[128,8,2048]{2,1,0:T(8,128)(2,1)}), bf16[128,8,2048]{2,1,0:T(8,128)(2,1)}, u32[]{:S(2)}, u32[]{:S(2)}) %all-to-all-start.6) | async-done | bytes 4194336 | tf_op jit(solution)/shard_map/all_to_all | solution.py:143
  658.6 7.5 %fusion.48 = bf16[1,384,2048]{2,1,0:T(8,128)(2,1)} fusion(f32[384,2048]{1,0:T(8,128)} %fusion.65, bf16[128,8,2048]{2,1,0:T(8,128)(2,1)} %all-to-all-done.6, f32[384,2048]{1,0:T(8,128)} %fusion.3, bf16[384,2048]{1,0:T(8,128)(2,1)} %copy-done.16, bf16[384,3072]{1,0:T(8,128)(2,1)S(1)} %fusion.18), kind=kOutput, calls=%fused_computation.69 | convolution fusion | flops 1614544896 | bytes 14417920 | tf_op jit(solution)/shard_map/dot_general | solution.py:144
  (103 shorter events, 75.7 us)
Async XLA Ops:
  6.5 136.4 %all-gather.3.cloned.1.call-start = ((), (), s32[]{:S(2)}) async-start(), calls=%async_computation.7 | async-start | bytes 33816576 | tf_op jit(solution)/shard_map/all_gather | solution.py:70
  6.5 5.9 copy-start
  8.4 591.7 %all-gather.5.cloned.1.call-start = ((), (), s32[]{:S(2)}) async-start(), calls=%async_computation.8 | async-start | bytes 34873344 | tf_op jit(solution)/shard_map/all_gather | solution.py:70
  20.7 7.1 %copy-start.2 = (bf16[8,1408,64]{2,1,0:T(8,128)(2,1)S(1)}, bf16[8,1408,64]{2,1,0:T(8,128)(2,1)}, u32[]{:S(2)}) copy-start(bf16[8,1408,64]{2,1,0:T(8,128)(2,1)} %get-tuple-element.30) | copy-start | bytes 4325380
  20.7 37.6 %collective-permute-start.1 = (bf16[8,64,1408]{2,1,0:T(8,128)(2,1)}, bf16[8,64,1408]{2,1,0:T(8,128)(2,1)}, u32[]{:S(2)}, u32[]{:S(2)}) collective-permute-start(bf16[8,64,1408]{2,1,0:T(8,128)(2,1)} %bitcast.115), channel_id=1, source_target_pairs={{0,1},{1,0},{2,3},{3,2},{4,5},{5,4},{6,7},{7,6},{8,9},{9,8},{10,11... | collective-permute-start | bytes 4325384 | tf_op jit(solution)/shard_map/ppermute | solution.py:77
  24.6 5.9 copy-start.10
  24.6 37.8 %collective-permute-start = (bf16[8,64,1408]{2,1,0:T(8,128)(2,1)}, bf16[8,64,1408]{2,1,0:T(8,128)(2,1)}, u32[]{:S(2)}, u32[]{:S(2)}) collective-permute-start(bf16[8,64,1408]{2,1,0:T(8,128)(2,1)} %constant_dynamic-slice_fusion.3), channel_id=1, source_target_pairs={{0,1},{1,0},{2,3},{3,2},{4,5},{5,4},{6,7},{7,6},{8,9},{9,8},{10,11... | collective-permute-start | bytes 4325384 | tf_op jit(solution)/shard_map/ppermute | solution.py:77
  27.4 4.6 copy-start.12
  27.4 16.4 %collective-permute-start.2 = (bf16[8,64,1408]{2,1,0:T(8,128)(2,1)}, bf16[8,64,1408]{2,1,0:T(8,128)(2,1)}, u32[]{:S(2)}, u32[]{:S(2)}) collective-permute-start(bf16[8,64,1408]{2,1,0:T(8,128)(2,1)} %constant_dynamic-slice_fusion), channel_id=1, source_target_pairs={{0,1},{1,0},{2,3},{3,2},{4,5},{5,4},{6,7},{7,6},{8,9},{9,8},{10,11... | collective-permute-start | bytes 4325384 | tf_op jit(solution)/shard_map/ppermute | solution.py:77
  30.5 13.3 %copy-start.3 = (bf16[8,128,1408]{2,1,0:T(8,128)(2,1)S(1)}, bf16[8,128,1408]{2,1,0:T(8,128)(2,1)}, u32[]{:S(2)}) copy-start(bf16[8,128,1408]{2,1,0:T(8,128)(2,1)} %param.15) | copy-start | bytes 8650756
  32.5 13.3 %copy-start.11 = (s32[2304]{0:T(1024)}, s32[2304]{0:T(1024)S(1)}, u32[]{:S(2)}) copy-start(s32[2304]{0:T(1024)S(1)} %fusion.88) | copy-start | bytes 27652
  41.5 4.3 copy-start.8
  47.6 95.3 %all-to-all-start.1 = ((bf16[16,64,1408]{2,1,0:T(8,128)(2,1)}), bf16[16,64,1408]{2,1,0:T(8,128)(2,1)S(1)}, u32[]{:S(2)}, u32[]{:S(2)}) async-start(bf16[16,64,1408]{2,1,0:T(8,128)(2,1)} %pad_maximum_fusion.5), calls=%async_computation.1 | async-start | bytes 5767168 | tf_op jit(solution)/shard_map/all_to_all | solution.py:83
  60.4 2.9 copy-start.4
  142.9 1.6 copy-start.1
  144.5 49.3 %all-to-all-start.2 = ((bf16[16,64,1408]{2,1,0:T(8,128)(2,1)}), bf16[16,64,1408]{2,1,0:T(8,128)(2,1)S(1)}, u32[]{:S(2)}, u32[]{:S(2)}) async-start(bf16[16,64,1408]{2,1,0:T(8,128)(2,1)} %pad_maximum_fusion.3), calls=%async_computation.2 | async-start | bytes 5767168 | tf_op jit(solution)/shard_map/all_to_all | solution.py:83
  193.8 58.0 %all-to-all-start.3 = ((bf16[16,64,1408]{2,1,0:T(8,128)(2,1)}), bf16[16,64,1408]{2,1,0:T(8,128)(2,1)}, u32[]{:S(2)}, u32[]{:S(2)}) async-start(bf16[16,64,1408]{2,1,0:T(8,128)(2,1)} %pad_maximum_fusion.4), calls=%async_computation.3 | async-start | bytes 5767168 | tf_op jit(solution)/shard_map/all_to_all | solution.py:83
  200.6 5.5 copy-start.5
  206.1 8.5 %copy-start.6 = (pred[3072,384]{1,0:T(32,128)(4,1)S(1)}, pred[3072,384]{1,0:T(32,128)(4,1)}, u32[]{:S(2)}) copy-start(pred[3072,384]{1,0:T(32,128)(4,1)} %iota_compare_fusion) | copy-start | bytes 3538948
  213.5 58.0 %copy-start.14 = (f32[384]{0:T(512)}, f32[384]{0:T(512)S(1)}, u32[]{:S(2)}) copy-start(f32[384]{0:T(512)S(1)} %add_rsqrt_fusion) | copy-start | bytes 4612
  251.9 146.4 %all-to-all-start = ((bf16[128,16,2048]{2,1,0:T(8,128)(2,1)}), bf16[128,16,2048]{2,1,0:T(8,128)(2,1)}, u32[]{:S(2)}, u32[]{:S(2)}) async-start(bf16[128,16,2048]{2,1,0:T(8,128)(2,1)} %bitcast.106), calls=%async_computation | async-start | bytes 16777216 | tf_op jit(solution)/shard_map/all_to_all | solution.py:134
  258.4 7.7 %collective-permute-start.3 = (bf16[16,64,1408]{2,1,0:T(8,128)(2,1)}, bf16[16,64,1408]{2,1,0:T(8,128)(2,1)S(1)}, u32[]{:S(2)}, u32[]{:S(2)}) collective-permute-start(bf16[16,64,1408]{2,1,0:T(8,128)(2,1)} %copy-done.1), channel_id=1, source_target_pairs={{0,1},{1,0},{2,3},{3,2},{4,5},{5,4},{6,7},{7,6},{8,9},{9,8},{10,11... | collective-permute-start | bytes 8650760 | tf_op jit(solution)/shard_map/ppermute | solution.py:84
  259.7 16.4 %collective-permute-start.4 = (bf16[16,64,1408]{2,1,0:T(8,128)(2,1)S(1)}, bf16[16,64,1408]{2,1,0:T(8,128)(2,1)S(1)}, u32[]{:S(2)}, u32[]{:S(2)}) collective-permute-start(bf16[16,64,1408]{2,1,0:T(8,128)(2,1)S(1)} %all-to-all-done.2), channel_id=1, source_target_pairs={{0,1},{1,0},{2,3},{3,2},{4,5},{5,4},{6,7},{7,6},{8,9},{9,8},{10,11... | collective-permute-start | bytes 8650760 | tf_op jit(solution)/shard_map/ppermute | solution.py:84
  259.8 16.3 %collective-permute-start.5 = (bf16[16,64,1408]{2,1,0:T(8,128)(2,1)}, bf16[16,64,1408]{2,1,0:T(8,128)(2,1)S(1)}, u32[]{:S(2)}, u32[]{:S(2)}) collective-permute-start(bf16[16,64,1408]{2,1,0:T(8,128)(2,1)} %all-to-all-done.3), channel_id=1, source_target_pairs={{0,1},{1,0},{2,3},{3,2},{4,5},{5,4},{6,7},{7,6},{8,9},{9,8},{10,11... | collective-permute-start | bytes 8650760 | tf_op jit(solution)/shard_map/ppermute | solution.py:84
  268.5 3.0 copy-start.7
  268.5 3.0 copy-start.17
  398.3 69.7 %all-to-all-start.5 = ((bf16[128,8,2048]{2,1,0:T(8,128)(2,1)}), bf16[128,8,2048]{2,1,0:T(8,128)(2,1)}, u32[]{:S(2)}, u32[]{:S(2)}) async-start(bf16[128,8,2048]{2,1,0:T(8,128)(2,1)} %convert_bitcast_fusion.1), calls=%async_computation.5 | async-start | bytes 8388608 | tf_op jit(solution)/shard_map/all_to_all | solution.py:134
  468.0 9.5 %copy-start.13 = (bf16[1,384,6]{1,2,0:T(8,128)(2,1)S(1)}, bf16[1,384,6]{1,2,0:T(8,128)(2,1)}, u32[]{:S(2)}) copy-start(bf16[1,384,6]{1,2,0:T(8,128)(2,1)} %param.23) | copy-start | bytes 13828
  468.0 30.7 %copy-start.9 = (s32[3072]{0:T(1024)S(1)}, s32[3072]{0:T(1024)}, u32[]{:S(2)}) copy-start(s32[3072]{0:T(1024)} %copy-done.8) | copy-start | bytes 36868
  468.0 118.2 %all-to-all-start.4 = ((bf16[128,16,2048]{2,1,0:T(8,128)(2,1)}), bf16[128,16,2048]{2,1,0:T(8,128)(2,1)}, u32[]{:S(2)}, u32[]{:S(2)}) async-start(bf16[128,16,2048]{2,1,0:T(8,128)(2,1)} %bitcast.107), calls=%async_computation.4 | async-start | bytes 16777216 | tf_op jit(solution)/shard_map/all_to_all | solution.py:143
  532.1 68.1 %copy-start.15 = (f32[384]{0:T(512)S(1)}, f32[384]{0:T(512)}, u32[]{:S(2)}) copy-start(f32[384]{0:T(512)} %copy-done.14) | copy-start | bytes 4612
  586.2 72.4 %all-to-all-start.6 = ((bf16[128,8,2048]{2,1,0:T(8,128)(2,1)}), bf16[128,8,2048]{2,1,0:T(8,128)(2,1)}, u32[]{:S(2)}, u32[]{:S(2)}) async-start(bf16[128,8,2048]{2,1,0:T(8,128)(2,1)} %convert_bitcast_fusion), calls=%async_computation.6 | async-start | bytes 8388608 | tf_op jit(solution)/shard_map/all_to_all | solution.py:143
  (1 other events, 1.1 us)
Sparse Core Ops, SparseCore 0:
  10.3 132.5 all-gather.2
  145.9 235.4 all-gather.4

commit v3 on v1

v3 whole, which is shorter than its diff:
```python
import functools

import jax
import jax.numpy as jnp
from jax import lax
from jax.experimental import pallas as pl
from jax.experimental.pallas import tpu as pltpu
from jax.sharding import Mesh, PartitionSpec as P


HEAD_DIM = 128
ROPE_BASE = 10000.0
EPSILON = 1e-6
ALL = ("fsdp", "x", "core")
SWAP = [(0, 1), (1, 0)]


def rms_norm(values):
    vals_f32 = values.astype(jnp.float32)
    mean_sq = jnp.mean(vals_f32 * vals_f32, axis=-1, keepdims=True)
    return (vals_f32 * lax.rsqrt(mean_sq + EPSILON)).astype(jnp.bfloat16)


def rotary_embed(heads_in, positions):
    half_dim = HEAD_DIM // 2
    inv_freq = ROPE_BASE ** (-jnp.arange(half_dim, dtype=jnp.float32) * (2.0 / HEAD_DIM))
    angles = positions[:, None] * inv_freq[None, :]
    cos_tab = jnp.cos(angles)[:, None, :]
    sin_tab = jnp.sin(angles)[:, None, :]
    vals_f32 = heads_in.astype(jnp.float32)
    first_half = vals_f32[..., :half_dim]
    second_half = vals_f32[..., half_dim:]
    rotated = jnp.concatenate([first_half * cos_tab - second_half * sin_tab, second_half * cos_tab + first_half * sin_tab], axis=-1)
    return rotated.astype(jnp.bfloat16)


def attention_block(x_in, qkv_weight, out_weight):
    n_batch, seq_len, _ = x_in.shape
    n_heads = qkv_weight.shape[1] // (3 * HEAD_DIM)
    normed = rms_norm(x_in)
    qkv_proj = jnp.einsum("bsd,dn->bsn", normed, qkv_weight, preferred_element_type=jnp.float32).astype(jnp.bfloat16)
    qkv_proj = qkv_proj.reshape(n_batch, seq_len, 3, n_heads, HEAD_DIM)
    positions = jnp.arange(seq_len, dtype=jnp.float32)
    query_rot = rotary_embed(qkv_proj[:, :, 0], positions)
    key_rot = rotary_embed(qkv_proj[:, :, 1], positions)
    scores = jnp.einsum("bqhd,bkhd->bhqk", query_rot, key_rot, preferred_element_type=jnp.float32) * (HEAD_DIM ** -0.5)
    causal = jnp.arange(seq_len)[:, None] >= jnp.arange(seq_len)[None, :]
    attn_probs = jax.nn.softmax(jnp.where(causal, scores, -1e30), axis=-1).astype(jnp.bfloat16)
    attn_mixed = jnp.einsum("bhqk,bkhd->bqhd", attn_probs, qkv_proj[:, :, 2], preferred_element_type=jnp.float32).astype(jnp.bfloat16)
    attn_out = jnp.einsum("bsn,nm->bsm", attn_mixed.reshape(n_batch, seq_len, n_heads * HEAD_DIM), out_weight, preferred_element_type=jnp.float32)
    return (x_in.astype(jnp.float32) + attn_out).astype(jnp.bfloat16)


def capacity_for(n_tokens, top_k, n_experts):
    return ((5 * n_tokens * top_k) // (4 * n_experts) + 7) // 8 * 8


def nt_dot(lhs, rhs):
    return lax.dot_general(lhs, rhs, (((1,), (1,)), ((), ())), preferred_element_type=jnp.float32)


def exchange_kernel(n_chunk, inp, half, out, r1, r2, r3, b1, b2, own, w13, w2, xin, inner, yall, w_sem, in_sem, tx, rx, fin, ld):
    f, x, core = lax.axis_index("fsdp"), lax.axis_index("x"), lax.axis_index("core")
    z, y = f // 4, f % 4
    copy = pltpu.make_async_copy

    def dev(dx=0, dz=0, dy=0, dc=0):
        return {"fsdp": (z + dz + 4) % 4 * 4 + (y + dy + 4) % 4, "x": (x + dx + 4) % 4, "core": (core + dc) % 2}

    def send(src, dst, ssem, rsem, to):
        pltpu.make_async_remote_copy(src_ref=src, dst_ref=dst, send_sem=ssem, recv_sem=rsem, device_id=to, device_id_type=pl.DeviceIdType.MESH).start()

    def wait(ref, sem):
        copy(ref, ref, sem).wait()

    for k in range(n_chunk):
        for a in (1, 3, 2):
            send(inp.at[k, a], r1.at[k, a - 1], tx.at[0], rx.at[0, k], dev(dx=a))

    n_tile = half.shape[2] // 384
    for part in range(2):
        for j in range(n_tile):
            src = half.at[:, :, pl.ds((part * n_tile + j) * 128, 128)]
            dst = w13.at[:, core, :, pl.ds(j * 256 + part * 128, 128)]
            copy(src, dst, w_sem.at[0]).start()
            send(src, dst, w_sem.at[2], w_sem.at[4], dev(dc=1))
    down_h = half.at[:, :, pl.ds(n_tile * 256, n_tile * 128)]
    copy(down_h, w2.at[:, core], w_sem.at[1]).start()
    send(down_h, w2.at[:, core], w_sem.at[3], w_sem.at[5], dev(dc=1))

    def step(t, carry):
        @pl.when(t < n_chunk)
        def _():
            k = t
            wait(r1.at[k], rx.at[0, k])
            for b in (1, 3, 2):
                send(r1.at[k, :, b], r2.at[k, b - 1, pl.ds(1, 3)], tx.at[1], rx.at[1, k], dev(dz=b))
                send(inp.at[k, 0, b], r2.at[k, b - 1, 0], tx.at[1], rx.at[1, k], dev(dz=b))

        @pl.when((t >= 1) & (t < n_chunk + 1))
        def _():
            k = t - 1
            wait(r2.at[k], rx.at[1, k])
            for c in (1, 3, 2):
                send(r2.at[k, :, :, c], r3.at[k, c - 1, pl.ds(1, 3)], tx.at[2], rx.at[2, k], dev(dy=c))
                send(r1.at[k, :, 0, c], r3.at[k, c - 1, 0, pl.ds(1, 3)], tx.at[2], rx.at[2, k], dev(dy=c))
                send(inp.at[k, 0, 0, c], r3.at[k, c - 1, 0, 0], tx.at[2], rx.at[2, k], dev(dy=c))

        @pl.when((t >= 4) & (t < n_chunk + 4))
        def _():
            k = t - 4
            wait(b1.at[k], rx.at[3, k])
            for b in (1, 3, 2):
                to = dev(dz=-b)
                send(b1.at[k, :, b, pl.ds(1, 3)], b2.at[k, b - 1, pl.ds(1, 3)], tx.at[4], rx.at[4, k], to)
                send(own.at[k, b, pl.ds(1, 3)], b2.at[k, b - 1, 0], tx.at[4], rx.at[4, k], to)
                send(b1.at[k, :, b, 0], out.at[k, 0, b, pl.ds(1, 3)], tx.at[5], fin.at[1], to)
                send(own.at[k, b, 0], out.at[k, 0, b, 0], tx.at[5], fin.at[1], to)

        @pl.when((t >= 5) & (t < n_chunk + 5))
        def _():
            k = t - 5
            wait(b2.at[k], rx.at[4, k])
            for a in (1, 3, 2):
                to = dev(dx=-a)
                send(b2.at[k, :, :, a - 1], out.at[k, a, pl.ds(1, 3)], tx.at[6], fin.at[0], to)
                send(b1.at[k, :, 0, a], out.at[k, a, 0, pl.ds(1, 3)], tx.at[6], fin.at[0], to)
                send(own.at[k, 0, a], out.at[k, a, 0, 0], tx.at[6], fin.at[0], to)

        @pl.when((t >= 2) & (t < n_chunk + 2))
        def _():
            k = t - 2
            wait(r3.at[k], rx.at[2, k])

            @pl.when(t == 2)
            def _():
                for i in (0, 2, 4):
                    wait(w13.at[:, 0], w_sem.at[i])
                for i in (1, 3, 5):
                    wait(w2.at[:, 0], w_sem.at[i])

            copy(r3.at[k], xin.at[pl.ds(1, 3)], in_sem).start()
            copy(r2.at[k, :, :, 0], xin.at[0, pl.ds(1, 3)], in_sem).start()
            copy(r1.at[k, :, 0, 0], xin.at[0, 0, pl.ds(1, 3)], in_sem).start()
            copy(inp.at[k, 0, 0, 0], xin.at[0, 0, 0], in_sem).start()
            wait(xin, in_sem)
            rows = xin.shape[0] * xin.shape[1] * xin.shape[2] * xin.shape[3]

            def up_tile(j, c2):
                lhs = xin[...].reshape(rows, xin.shape[4])
                cols = w13[:, :, :, pl.ds(pl.multiple_of(j * 256, 256), 256)].reshape(-1, 256)
                both = jnp.dot(lhs, cols, preferred_element_type=jnp.float32)
                act = jax.nn.silu(both[:, :128]) * both[:, 128:]
                inner[:, pl.ds(pl.multiple_of(j * 128, 128), 128)] = act.astype(jnp.bfloat16)
                return c2

            lax.fori_loop(0, n_tile, up_tile, 0)

            def down_tile(n, c2):
                rhs = w2[pl.ds(n * 2, 2)].reshape(256, w2.shape[3])
                res = lax.dot_general(inner[...], rhs, (((1,), (1,)), ((), ())), preferred_element_type=jnp.float32)
                yall[k, :, :, :, :, pl.ds(pl.multiple_of(n * 256, 256), 256)] = res.astype(jnp.bfloat16).reshape(4, 4, 4, 8, 256)
                return c2

            lax.fori_loop(0, w2.shape[0] // 2, down_tile, 0)
            copy(yall.at[k, 0], own.at[k], ld.at[0]).start()
            copy(yall.at[k, 0, 0, 0], out.at[k, 0, 0, 0], ld.at[1]).start()
            for c in (1, 3, 2):
                send(yall.at[k, c], b1.at[k, c - 1], tx.at[3], rx.at[3, k], dev(dy=-c))
                send(yall.at[k, c, 0, 0], out.at[k, 0, 0, c], tx.at[7], fin.at[2], dev(dy=-c))
            wait(own.at[k], ld.at[0])
            wait(out.at[k, 0, 0, 0], ld.at[1])

        return carry

    lax.fori_loop(0, n_chunk + 5, step, 0)
    wait(out.at[:, pl.ds(1, 3)], tx.at[6])
    wait(out.at[:, 0, pl.ds(1, 3)], tx.at[5])
    wait(out.at[:, 0, 0, pl.ds(1, 3)], tx.at[7])
    for ref, i in ((r1, 0), (r2, 1), (r3, 2), (b1, 3), (b2, 4)):
        wait(ref, tx.at[i])
    wait(out.at[:, pl.ds(1, 3)], fin.at[0])
    wait(out.at[:, 0, pl.ds(1, 3)], fin.at[1])
    wait(out.at[:, 0, 0, pl.ds(1, 3)], fin.at[2])


def run_exchange(inp, half):
    n_chunk, _, _, _, blk, dim = inp.shape
    width = half.shape[2] // 3
    bf = jnp.bfloat16
    shapes = [(4, 4, 4), (3, 4, 4), (3, 4, 4), (3, 4, 4), (3, 4, 4), (3, 4, 3), (4, 4)]
    outs = pl.pallas_call(
        functools.partial(exchange_kernel, n_chunk),
        out_shape=[jax.ShapeDtypeStruct((n_chunk,) + sh + (blk, dim), bf) for sh in shapes],
        in_specs=[pl.BlockSpec(memory_space=pl.ANY)] * 2,
        out_specs=[pl.BlockSpec(memory_space=pl.ANY)] * len(shapes),
        scratch_shapes=[
            pltpu.VMEM((16, 2, 64, 2 * width), bf),
            pltpu.VMEM((16, 2, 64, width), bf),
            pltpu.VMEM((4, 4, 4, blk, dim), bf),
            pltpu.VMEM((64 * blk, width), bf),
            pltpu.VMEM((n_chunk, 4, 4, 4, blk, dim), bf),
            pltpu.SemaphoreType.DMA((6,)),
            pltpu.SemaphoreType.DMA,
            pltpu.SemaphoreType.DMA((8,)),
            pltpu.SemaphoreType.DMA((5, n_chunk)),
            pltpu.SemaphoreType.DMA((3,)),
            pltpu.SemaphoreType.DMA((2,)),
        ],
        compiler_params=pltpu.CompilerParams(has_side_effects=True, vmem_limit_bytes=60 * 2**20),
        name="expert_exchange",
    )(inp, half)
    return outs[0]


def solution(mesh):
    n_f, n_ep = mesh.shape["fsdp"], mesh.shape["ep"]
    n_core = 2
    n_x = n_ep // n_core
    phys = Mesh(mesh.devices.reshape(n_f, n_x, n_core), ALL)
    tok_spec = P(ALL)
    row_spec = P("fsdp", None)
    ep = ("x", "core")

    def gather_rows(*shards):
        part = shards[0].shape[0] // n_ep
        mine = lax.axis_index("x") * n_core + lax.axis_index("core")
        piece = jnp.concatenate([lax.dynamic_slice_in_dim(shard, mine * part, part, 0) for shard in shards], axis=1)
        return lax.all_gather(piece, ALL, axis=0, tiled=True)

    def stage_expert(shard):
        core = lax.axis_index("core")
        half = shard.shape[1] // n_core
        keep = lax.dynamic_slice_in_dim(shard, core * half, half, 1)
        give = lax.dynamic_slice_in_dim(shard, (1 - core) * half, half, 1)
        got = lax.ppermute(give, "core", SWAP)
        first = core == 0
        return jnp.concatenate([jnp.where(first, keep, got), jnp.where(first, got, keep)], axis=0)

    def local_step(x_in, w_qkv, w_out, w_gate, w_up, w_down, ws_gate, ws_up, ws_down, expert_ids, slot_ids, gate_vals):
        n_batch, seq_len, model_dim = x_in.shape
        n_tokens = n_batch * seq_len
        top_k = expert_ids.shape[-1]
        n_experts = w_gate.shape[0] * n_ep
        capacity = capacity_for(n_tokens, top_k, n_experts)
        n_rows = n_experts * capacity
        s_ff = ws_gate.shape[1]

        n_qkv = w_qkv.shape[1]
        n_attn = n_qkv + w_out.shape[1]
        dense = gather_rows(w_qkv, w_out, ws_gate, ws_up, lax.optimization_barrier(ws_down.T))
        half = jnp.concatenate([stage_expert(w_gate), stage_expert(w_up), stage_expert(jnp.swapaxes(w_down, 1, 2))], axis=2)
        dense, half = lax.optimization_barrier((dense, half))
        half = lax.all_to_all(half, "fsdp", 0, 0, tiled=True)
        qkv_full, out_full, shared_full = dense[:, :n_qkv], dense[:, n_qkv:n_attn], dense[:, n_attn:]

        ids = expert_ids.reshape(n_tokens, top_k)
        slots = slot_ids.reshape(n_tokens, top_k)
        gates = gate_vals.reshape(n_tokens, top_k)
        kept = slots >= 0
        far, chip = lax.axis_index("fsdp"), lax.axis_index("x")
        rel_x = (ids // n_f - chip) % 4
        rel_z = (ids % n_f // 4 - far // 4) % 4
        rel_y = (ids % 4 - far % 4) % 4
        n_chunk = capacity // 8
        row = ((slots // 8 * 4 + rel_x) * 4 + rel_z) * 4 + rel_y
        row = jnp.where(kept, row * 8 + slots % 8, n_rows).reshape(-1)
        source_tok = jnp.arange(n_tokens * top_k, dtype=jnp.int32) // top_k
        tok_iota = jnp.arange(n_tokens, dtype=jnp.int32)
        row_source = jnp.full((n_rows,), n_tokens, jnp.int32).at[row].set(source_tok, mode="drop")
        row_gate = jnp.zeros((n_rows,), gates.dtype).at[row].set(gates.reshape(-1), mode="drop")
        spread = (row_source[:, None] == tok_iota[None, :]).astype(jnp.bfloat16)
        merge = jnp.where(row_source[None, :] == tok_iota[:, None], row_gate[None, :], jnp.zeros((), gates.dtype))

        hidden = attention_block(x_in, qkv_full, out_full).reshape(n_tokens, model_dim)
        normed = rms_norm(hidden)
        buffer = jnp.dot(spread, normed, preferred_element_type=jnp.float32).astype(jnp.bfloat16)
        s_gate = jnp.dot(normed, shared_full[:, :s_ff], preferred_element_type=jnp.float32)
        s_up = jnp.dot(normed, shared_full[:, s_ff:2 * s_ff], preferred_element_type=jnp.float32)
        s_inner = (jax.nn.silu(s_gate) * s_up).astype(jnp.bfloat16)
        shared_out = nt_dot(s_inner, shared_full[:, 2 * s_ff:])
        buffer, shared_out = lax.optimization_barrier((buffer, shared_out))
        back = run_exchange(buffer.reshape(n_chunk, 4, 4, 4, 8, model_dim), half)
        routed = jnp.dot(merge, back.reshape(n_rows, model_dim), preferred_element_type=jnp.float32)

        summed = hidden.astype(jnp.float32) + shared_out + routed
        return summed.astype(jnp.bfloat16).reshape(n_batch, seq_len, model_dim)

    return jax.shard_map(local_step, mesh=phys, in_specs=(tok_spec, row_spec, row_spec, P(ep, "fsdp", None), P(ep, "fsdp", None), P(ep, None, "fsdp"), row_spec, row_spec, P(None, "fsdp"), tok_spec, tok_spec, tok_spec), out_specs=tok_spec, check_vma=False)
```

time: 795 us -> 752 us (0.946)
  the two profiles are of different devices: /device:TPU:121 before, /device:TPU:1 now
where the time goes in v3:
time: 752 us; the launch traced here: 740 us
  Pallas kernels  382 us (51%)
  waiting for transfers between devices  173 us (23%)
  matrix products  79.8 us (11%)
  local copies, waits for them, and re-layouts  62.3 us (8%)
  other arithmetic  21.2 us (3%)
  between operations  14 us (2%)
    pallas_call x1, Pallas kernels, run_exchange(): pl.pallas_call(functools.partial(exchange_kernel, n_chunk), out_shape=[ja...  382 us
    all_gather x1, waiting for transfers between devices, gather_rows(): return lax.all_gather(piece, ALL, axis=0, tiled=True)  107 us
    all_to_all x1, waiting for transfers between devices, local_step(): half = lax.all_to_all(half, 'fsdp', 0, 0, tiled=True)  66.4 us
    scatter x1, local copies, waits for them, and re-layouts, local_step(): jnp.zeros((n_rows,), gates.dtype).at[row]  21.2 us
    unnamed x33, local copies, waits for them, and re-layouts  17.7 us
    dot_general x1, matrix products, nt_dot(): lax.dot_general(lhs, rhs, (((1,), (1,)), ((), ())), preferred_element_typ...  17 us
    dot_general x1, matrix products, attention_block(): jnp.einsum('bsd,dn->bsn', normed, qkv_weight, preferred_element_type=jnp....  15.8 us
  transfers between devices with their start and end apart: 5, of which 2 were waited for; matrix products, arithmetic and copies ran while one was open for 17% of the time, Pallas kernels for 0%

profile of v3, /device:TPU:1, one launch (start us, length us, event | category | flops | bytes accessed | tf_op | source)
XLA Modules:
  0.0 740.2 jit_solution(12890256923635463385)
XLA Ops:
  6.5 1.1 copy-done
  7.6 0.9 dynamic-slice_dynamic-update-slice_fusion
  12.6 6.8 constant_dynamic-slice_fusion.1
  19.5 4.1 copy.32
  23.6 1.5 collective-permute-start.2
  25.1 2.7 constant_dynamic-slice_fusion.3
  27.9 1.2 constant_dynamic-slice_fusion.2
  31.8 3.2 copy.31
  35.4 9.0 %scatter_custom_fusion = s32[3072]{0:T(1024)S(1)} fusion(s32[2304]{0:T(1024)S(1)} %fusion.77, s32[2304]{0:T(1024)S(1)} %add_select_fusion, s32[]{:T(128)} %constant.148.clone.1), kind=kCustom, calls=%fused_computation.130 | custom fusion | bytes 12292 | tf_op jit(solution)/shard_map/scatter | solution.py:270
  44.4 21.2 %scatter_custom_fusion.1 = bf16[3072]{0:T(1024)(128)(2,1)S(1)} fusion(s32[2304]{0:T(1024)S(1)} %fusion.77, bf16[2304]{0:T(1024)(128)(2,1)S(1)} %reshape.636, bf16[]{:T(256)} %constant.159.clone.1), kind=kCustom, calls=%fused_computation.132 | custom fusion | bytes 6146 | tf_op jit(solution)/shard_map/scatter | solution.py:271
  65.6 2.7 broadcast_select_fusion.3
  68.4 2.0 broadcast_select_fusion.1
  70.4 1.6 bitcast_select_fusion.1
  72.1 3.8 maximum_maximum_fusion
  75.9 106.9 %all-gather.2.cloned.1.call-done = bf16[2048,16640]{1,0:T(8,128)(2,1)} async-done(((bf16[16,16640]{1,0:T(8,128)(2,1)}), bf16[2048,16640]{1,0:T(8,128)(2,1)}) %all-gather.2.cloned.1.call-update) | async-done | bytes 68157456 | tf_op jit(solution)/shard_map/all_gather | solution.py:229
  182.8 15.8 %fusion.44 = bf16[48,8,48,128]{3,1,2,0:T(8,128)(2,1)S(1)} fusion(bf16[2048,16640]{1,0:T(8,128)(2,1)} %all-gather.2.cloned.1.call-done, bf16[1,384,2048]{2,1,0:T(8,128)(2,1)} %param.12, f32[384]{0:T(512)S(1)} %add_rsqrt_fusion.1), kind=kOutput, calls=%fused_computation.50 | convolution fusion | flops 9668395008 | bytes 31458816 | tf_op jit(solution)/shard_map/bsd,dn->bsn/dot_general | solution.py:41
  198.6 1.3 copy.36
  199.9 2.6 fusion.94
  202.5 2.9 copy.33
  205.4 5.2 all-to-all-start
  210.5 2.2 fusion.62
  212.7 2.3 fusion.51
  215.1 1.9 fusion.55
  217.0 5.1 fusion.95
  222.1 5.1 fusion.48
  227.2 7.3 fusion.31
  234.5 10.6 %convolution_convert_fusion = bf16[3072,2048]{1,0:T(8,128)(2,1)} fusion(s32[3072]{0:T(1024)S(1)} %scatter_custom_fusion, bf16[384,2048]{1,0:T(8,128)(2,1)S(1)} %get-tuple-element.37, f32[384]{0:T(512)S(1)} %add_rsqrt_fusion), kind=kOutput, calls=%fused_computation.11 | convolution fusion | flops 4841668608 | bytes 14169600 | tf_op jit(solution)/shard_map/dot_general | solution.py:277
  245.0 11.0 %fusion.7 = f32[384,2816]{1,0:T(8,128)} fusion(bf16[2048,16640]{1,0:T(8,128)(2,1)} %all-gather.2.cloned.1.call-done, bf16[384,2048]{1,0:T(8,128)(2,1)S(1)} %get-tuple-element.37, f32[384]{0:T(512)S(1)} %add_rsqrt_fusion), kind=kOutput, calls=%fused_computation.9 | convolution fusion | flops 4431544320 | bytes 17434112 | tf_op jit(solution)/shard_map/dot_general | solution.py:278
  256.0 17.0 %fusion.3 = f32[384,2048]{1,0:T(8,128)} fusion(bf16[2048,16640]{1,0:T(8,128)(2,1)} %all-gather.2.cloned.1.call-done, f32[384,2816]{1,0:T(8,128)} %fusion.7, bf16[384,2048]{1,0:T(8,128)(2,1)S(1)} %get-tuple-element.37, f32[384]{0:T(512)S(1)} %add_rsqrt_fusion), kind=kOutput, calls=%fused_computation.5 | convolution fusion | flops 8867217408 | bytes 32114176 | tf_op jit(solution)/shard_map/dot_general | solution.py:59
  273.0 66.4 %all-to-all-done.half = bf16[16,64,4224]{2,1,0:T(8,128)(2,1)} async-done(((bf16[16,64,4224]{2,1,0:T(8,128)(2,1)}), bf16[16,64,4224]{2,1,0:T(8,128)(2,1)}, u32[]{:S(2)}, u32[]{:S(2)}) %all-to-all-start) | async-done | bytes 8650784 | tf_op jit(solution)/shard_map/all_to_all | solution.py:254
  339.4 382.4 %expert_exchange.1 = (bf16[6,4,4,4,8,2048]{5,4,3,2,1,0:T(8,128)(2,1)}, bf16[6,3,4,4,8,2048]{5,4,3,2,1,0:T(8,128)(2,1)}, bf16[6,3,4,4,8,2048]{5,4,3,2,1,0:T(8,128...) custom-call(bf16[6,4,4,4,8,2048]{5,4,3,2,1,0:T(8,128)(2,1)} %bitcast, ...), custom_call_target="tpu_custom_call" | custom-call | tf_op jit(solution)/shard_map/expert_exchange/pallas_call | solution.py:192
  721.8 11.3 %fusion.37 = bf16[1,384,2048]{2,1,0:T(8,128)(2,1)} fusion(bf16[3072,2048]{1,0:T(8,128)(2,1)} %bitcast.55, f32[384,2048]{1,0:T(8,128)} %fusion.3, bf16[384,2048]{1,0:T(8,128)(2,1)S(1)} %get-tuple-element.37, s32[3072]{0:T(1024)S(1)} %scatter_custom_fusion, bf16[3072]{0:T(1024)(128)(2,1)S(1)} %scatter_custom_fusion.1), kind=kOutput, calls=%fused_computation.46 | convolution fusion | flops 4837343232 | bytes 18892800 | tf_op jit(solution)/shard_map/dot_general | solution.py:284
  (48 shorter events, 7.2 us)
Async XLA Ops:
  6.5 1.1 copy-start
  6.5 176.3 %all-gather.2.cloned.1.call-start = ((), (), s32[]{:S(2)}) async-start(), calls=%async_computation.1 | async-start | bytes 68689920 | tf_op jit(solution)/shard_map/all_gather | solution.py:229
  11.8 0.8 copy-start.7
  23.6 4.3 copy-start.2
  23.6 6.0 copy-start.8
  23.6 6.3 copy-start.9
  23.6 7.0 copy-start.4
  23.6 46.8 %collective-permute-start.2 = (bf16[8,64,1408]{2,1,0:T(8,128)(2,1)}, bf16[8,64,1408]{2,1,0:T(8,128)(2,1)}, u32[]{:S(2)}, u32[]{:S(2)}) collective-permute-start(bf16[8,64,1408]{2,1,0:T(8,128)(2,1)} %bitcast.54), channel_id=1, source_target_pairs={{0,1},{1,0},{2,3},{3,2},{4,5},{5,4},{6,7},{7,6},{8,9},{9,8},{10,11... | collective-permute-start | bytes 4325384 | tf_op jit(solution)/shard_map/ppermute | solution.py:236
  27.8 37.8 %collective-permute-start = (bf16[8,64,1408]{2,1,0:T(8,128)(2,1)}, bf16[8,64,1408]{2,1,0:T(8,128)(2,1)}, u32[]{:S(2)}, u32[]{:S(2)}) collective-permute-start(bf16[8,64,1408]{2,1,0:T(8,128)(2,1)} %constant_dynamic-slice_fusion.3), channel_id=1, source_target_pairs={{0,1},{1,0},{2,3},{3,2},{4,5},{5,4},{6,7},{7,6},{8,9},{9,8},{10,11... | collective-permute-start | bytes 4325384 | tf_op jit(solution)/shard_map/ppermute | solution.py:236
  29.2 39.1 %collective-permute-start.1 = (bf16[8,64,1408]{2,1,0:T(8,128)(2,1)}, bf16[8,64,1408]{2,1,0:T(8,128)(2,1)}, u32[]{:S(2)}, u32[]{:S(2)}) collective-permute-start(bf16[8,64,1408]{2,1,0:T(8,128)(2,1)} %constant_dynamic-slice_fusion.2), channel_id=1, source_target_pairs={{0,1},{1,0},{2,3},{3,2},{4,5},{5,4},{6,7},{7,6},{8,9},{9,8},{10,11... | collective-permute-start | bytes 4325384 | tf_op jit(solution)/shard_map/ppermute | solution.py:236
  30.6 4.4 copy-start.10
  65.6 2.9 copy-start.3
  205.4 134.0 %all-to-all-start = ((bf16[16,64,4224]{2,1,0:T(8,128)(2,1)}), bf16[16,64,4224]{2,1,0:T(8,128)(2,1)}, u32[]{:S(2)}, u32[]{:S(2)}) async-start(bf16[16,64,4224]{2,1,0:T(8,128)(2,1)} %maximum_maximum_fusion), calls=%async_computation | async-start | bytes 17301504 | tf_op jit(solution)/shard_map/all_to_all | solution.py:254
  217.0 5.1 copy-start.6
  222.1 5.1 copy-start.5
  721.8 11.3 %copy-start.1 = (bf16[2816,128]{1,0:T(8,128)(2,1)S(1)}, bf16[2816,128]{1,0:T(8,128)(2,1)}, u32[]{:S(2)}) copy-start(bf16[2816,128]{1,0:T(8,128)(2,1)} %param.20) | copy-start | bytes 2162692
Sparse Core Ops, SparseCore 0:
  12.7 170.0 all-gather.1

commit v4 on v3

v4 whole, which is shorter than its diff:
```python
import functools

import jax
import jax.numpy as jnp
from jax import lax
from jax.experimental import pallas as pl
from jax.experimental.pallas import tpu as pltpu
from jax.sharding import Mesh, PartitionSpec as P


HEAD_DIM = 128
ROPE_BASE = 10000.0
EPSILON = 1e-6
ALL = ("fsdp", "x", "core")
SWAP = [(0, 1), (1, 0)]


def rms_norm(values):
    vals_f32 = values.astype(jnp.float32)
    mean_sq = jnp.mean(vals_f32 * vals_f32, axis=-1, keepdims=True)
    return (vals_f32 * lax.rsqrt(mean_sq + EPSILON)).astype(jnp.bfloat16)


def rotary_embed(heads_in, positions):
    half_dim = HEAD_DIM // 2
    inv_freq = ROPE_BASE ** (-jnp.arange(half_dim, dtype=jnp.float32) * (2.0 / HEAD_DIM))
    angles = positions[:, None] * inv_freq[None, :]
    cos_tab = jnp.cos(angles)[:, None, :]
    sin_tab = jnp.sin(angles)[:, None, :]
    vals_f32 = heads_in.astype(jnp.float32)
    first_half = vals_f32[..., :half_dim]
    second_half = vals_f32[..., half_dim:]
    rotated = jnp.concatenate([first_half * cos_tab - second_half * sin_tab, second_half * cos_tab + first_half * sin_tab], axis=-1)
    return rotated.astype(jnp.bfloat16)


def attention_block(x_in, qkv_weight, out_weight):
    n_batch, seq_len, _ = x_in.shape
    n_heads = qkv_weight.shape[1] // (3 * HEAD_DIM)
    normed = rms_norm(x_in)
    qkv_proj = jnp.einsum("bsd,dn->bsn", normed, qkv_weight, preferred_element_type=jnp.float32).astype(jnp.bfloat16)
    qkv_proj = qkv_proj.reshape(n_batch, seq_len, 3, n_heads, HEAD_DIM)
    positions = jnp.arange(seq_len, dtype=jnp.float32)
    query_rot = rotary_embed(qkv_proj[:, :, 0], positions)
    key_rot = rotary_embed(qkv_proj[:, :, 1], positions)
    scores = jnp.einsum("bqhd,bkhd->bhqk", query_rot, key_rot, preferred_element_type=jnp.float32) * (HEAD_DIM ** -0.5)
    causal = jnp.arange(seq_len)[:, None] >= jnp.arange(seq_len)[None, :]
    attn_probs = jax.nn.softmax(jnp.where(causal, scores, -1e30), axis=-1).astype(jnp.bfloat16)
    attn_mixed = jnp.einsum("bhqk,bkhd->bqhd", attn_probs, qkv_proj[:, :, 2], preferred_element_type=jnp.float32).astype(jnp.bfloat16)
    attn_out = jnp.einsum("bsn,nm->bsm", attn_mixed.reshape(n_batch, seq_len, n_heads * HEAD_DIM), out_weight, preferred_element_type=jnp.float32)
    return (x_in.astype(jnp.float32) + attn_out).astype(jnp.bfloat16)


def capacity_for(n_tokens, top_k, n_experts):
    return ((5 * n_tokens * top_k) // (4 * n_experts) + 7) // 8 * 8


def nt_dot(lhs, rhs):
    return lax.dot_general(lhs, rhs, (((1,), (1,)), ((), ())), preferred_element_type=jnp.float32)


def exchange_kernel(n_chunk, inp, gate_h, rest_h, out, r1, r2, r3, b1, b2, own, w13, w2, xin, inner, yall, w_sem, in_sem, tx, rx, fin, ld):
    f, x, core = lax.axis_index("fsdp"), lax.axis_index("x"), lax.axis_index("core")
    z, y = f // 4, f % 4
    copy = pltpu.make_async_copy

    def dev(axis, hop):
        d = [0, 0, 0]
        d[axis % 3] = hop + 4
        return {"fsdp": (z + d[1]) % 4 * 4 + (y + d[2]) % 4, "x": (x + d[0]) % 4, "core": core}

    def send(src, dst, ssem, rsem, to):
        pltpu.make_async_remote_copy(src_ref=src, dst_ref=dst, send_sem=ssem, recv_sem=rsem, device_id=to, device_id_type=pl.DeviceIdType.MESH).start()

    def wait(ref, sem):
        copy(ref, ref, sem).wait()

    def hop1(k):
        for h in (1, 3, 2):
            send(inp.at[k, h], r1.at[k, h - 1], tx.at[0], rx.at[0, k], dev(k, h))

    def hop2(k):
        wait(r1.at[k], rx.at[0, k])
        for h in (1, 3, 2):
            to = dev(k + 1, h)
            send(r1.at[k, :, h], r2.at[k, h - 1, pl.ds(1, 3)], tx.at[1], rx.at[1, k], to)
            send(inp.at[k, 0, h], r2.at[k, h - 1, 0], tx.at[1], rx.at[1, k], to)

    def hop3(k):
        wait(r2.at[k], rx.at[1, k])
        for h in (1, 3, 2):
            to = dev(k + 2, h)
            send(r2.at[k, :, :, h], r3.at[k, h - 1, pl.ds(1, 3)], tx.at[2], rx.at[2, k], to)
            send(r1.at[k, :, 0, h], r3.at[k, h - 1, 0, pl.ds(1, 3)], tx.at[2], rx.at[2, k], to)
            send(inp.at[k, 0, 0, h], r3.at[k, h - 1, 0, 0], tx.at[2], rx.at[2, k], to)

    def back2(k):
        wait(b1.at[k], rx.at[3, k])
        for h in (1, 3, 2):
            to = dev(k + 1, -h)
            send(b1.at[k, :, h, pl.ds(1, 3)], b2.at[k, h - 1, pl.ds(1, 3)], tx.at[4], rx.at[4, k], to)
            send(own.at[k, h, pl.ds(1, 3)], b2.at[k, h - 1, 0], tx.at[4], rx.at[4, k], to)
            send(b1.at[k, :, h, 0], out.at[k, 0, h, pl.ds(1, 3)], tx.at[5], fin.at[1], to)
            send(own.at[k, h, 0], out.at[k, 0, h, 0], tx.at[5], fin.at[1], to)

    def back3(k):
        wait(b2.at[k], rx.at[4, k])
        for h in (1, 3, 2):
            to = dev(k, -h)
            send(b2.at[k, :, :, h - 1], out.at[k, h, pl.ds(1, 3)], tx.at[6], fin.at[0], to)
            send(b1.at[k, :, 0, h], out.at[k, h, 0, pl.ds(1, 3)], tx.at[6], fin.at[0], to)
            send(own.at[k, 0, h], out.at[k, h, 0, 0], tx.at[6], fin.at[0], to)

    def load(k):
        wait(r3.at[k], rx.at[2, k])
        copy(r3.at[k], xin.at[pl.ds(1, 3)], in_sem).start()
        copy(r2.at[k, :, :, 0], xin.at[0, pl.ds(1, 3)], in_sem).start()
        copy(r1.at[k, :, 0, 0], xin.at[0, 0, pl.ds(1, 3)], in_sem).start()
        copy(inp.at[k, 0, 0, 0], xin.at[0, 0, 0], in_sem).start()
        wait(xin, in_sem)

    n_tile = gate_h.shape[2] // 128

    def experts(k):
        load(k)
        rows = xin.shape[0] * xin.shape[1] * xin.shape[2] * xin.shape[3]

        def up_tile(j, carry):
            lhs = xin[...].reshape(rows, xin.shape[4])
            cols = w13[:, :, :, pl.ds(pl.multiple_of(j * 256, 256), 256)].reshape(-1, 256)
            both = jnp.dot(lhs, cols, preferred_element_type=jnp.float32)
            act = jax.nn.silu(both[:, :128]) * both[:, 128:]
            inner[:, pl.ds(pl.multiple_of(j * 128, 128), 128)] = act.astype(jnp.bfloat16)
            return carry

        lax.fori_loop(0, n_tile, up_tile, 0)

        def down_tile(n, carry):
            rhs = w2[pl.ds(n * 2, 2)].reshape(256, w2.shape[3])
            res = lax.dot_general(inner[...], rhs, (((1,), (1,)), ((), ())), preferred_element_type=jnp.float32)
            yall[k, :, :, :, :, pl.ds(pl.multiple_of(n * 256, 256), 256)] = res.astype(jnp.bfloat16).reshape(4, 4, 4, 8, 256)
            return carry

        lax.fori_loop(0, w2.shape[0] // 2, down_tile, 0)

    def back1(k):
        copy(yall.at[k, 0], own.at[k], ld.at[0, k]).start()
        copy(yall.at[k, 0, 0, 0], out.at[k, 0, 0, 0], ld.at[1, k]).start()
        for h in (1, 3, 2):
            to = dev(k + 2, -h)
            send(yall.at[k, h], b1.at[k, h - 1], tx.at[3], rx.at[3, k], to)
            send(yall.at[k, h, 0, 0], out.at[k, 0, 0, h], tx.at[7], fin.at[2], to)

    def landed(k):
        wait(own.at[k], ld.at[0, k])
        wait(out.at[k, 0, 0, 0], ld.at[1, k])

    early, late = range(0, n_chunk // 2), range(n_chunk // 2, n_chunk)
    for k in early:
        hop1(k)
    partner = {"core": 1 - core}
    for part, (half, base) in enumerate(((gate_h, 0), (rest_h, 0))):
        for j in range(n_tile):
            src = half.at[:, :, pl.ds(base + j * 128, 128)]
            dst = w13.at[:, core, :, pl.ds(j * 256 + part * 128, 128)]
            copy(src, dst, w_sem.at[0]).start()
            send(src, dst, w_sem.at[2], w_sem.at[4], partner)
    down_h = rest_h.at[:, :, pl.ds(n_tile * 128, n_tile * 128)]
    copy(down_h, w2.at[:, core], w_sem.at[1]).start()
    send(down_h, w2.at[:, core], w_sem.at[3], w_sem.at[5], partner)

    for k in early:
        hop2(k)
    for k in late:
        hop1(k)
    for k in early:
        hop3(k)
    for k in late:
        hop2(k)
    for i in (0, 2, 4):
        wait(w13.at[:, 0], w_sem.at[i])
    for i in (1, 3, 5):
        wait(w2.at[:, 0], w_sem.at[i])
    for i, k in enumerate(early):
        experts(k)
        back1(k)
        if i == 0:
            for q in late:
                hop3(q)
    for k in early:
        landed(k)
        back2(k)
    for i, k in enumerate(late):
        experts(k)
        back1(k)
        if i == 1:
            for q in early:
                back3(q)
    for k in late:
        landed(k)
        back2(k)
    for k in late:
        back3(k)

    wait(out.at[:, pl.ds(1, 3)], tx.at[6])
    wait(out.at[:, 0, pl.ds(1, 3)], tx.at[5])
    wait(out.at[:, 0, 0, pl.ds(1, 3)], tx.at[7])
    for ref, i in ((r1, 0), (r2, 1), (r3, 2), (b1, 3), (b2, 4)):
        wait(ref, tx.at[i])
    wait(out.at[:, pl.ds(1, 3)], fin.at[0])
    wait(out.at[:, 0, pl.ds(1, 3)], fin.at[1])
    wait(out.at[:, 0, 0, pl.ds(1, 3)], fin.at[2])


def run_exchange(inp, gate_h, rest_h):
    n_chunk, _, _, _, blk, dim = inp.shape
    width = gate_h.shape[2]
    bf = jnp.bfloat16
    shapes = [(4, 4, 4), (3, 4, 4), (3, 4, 4), (3, 4, 4), (3, 4, 4), (3, 4, 3), (4, 4)]
    outs = pl.pallas_call(
        functools.partial(exchange_kernel, n_chunk),
        out_shape=[jax.ShapeDtypeStruct((n_chunk,) + sh + (blk, dim), bf) for sh in shapes],
        in_specs=[pl.BlockSpec(memory_space=pl.ANY)] * 3,
        out_specs=[pl.BlockSpec(memory_space=pl.ANY)] * len(shapes),
        scratch_shapes=[
            pltpu.VMEM((16, 2, 64, 2 * width), bf),
            pltpu.VMEM((16, 2, 64, width), bf),
            pltpu.VMEM((4, 4, 4, blk, dim), bf),
            pltpu.VMEM((64 * blk, width), bf),
            pltpu.VMEM((n_chunk, 4, 4, 4, blk, dim), bf),
            pltpu.SemaphoreType.DMA((6,)),
            pltpu.SemaphoreType.DMA,
            pltpu.SemaphoreType.DMA((8,)),
            pltpu.SemaphoreType.DMA((5, n_chunk)),
            pltpu.SemaphoreType.DMA((3,)),
            pltpu.SemaphoreType.DMA((2, n_chunk)),
        ],
        compiler_params=pltpu.CompilerParams(has_side_effects=True, vmem_limit_bytes=60 * 2**20),
        name="expert_exchange",
    )(inp, gate_h, rest_h)
    return outs[0]


def solution(mesh):
    n_f, n_ep = mesh.shape["fsdp"], mesh.shape["ep"]
    n_core = 2
    n_x = n_ep // n_core
    phys = Mesh(mesh.devices.reshape(n_f, n_x, n_core), ALL)
    tok_spec = P(ALL)
    row_spec = P("fsdp", None)
    ep = ("x", "core")

    def gather_rows(*shards):
        part = shards[0].shape[0] // n_ep
        mine = lax.axis_index("x") * n_core + lax.axis_index("core")
        piece = jnp.concatenate([lax.dynamic_slice_in_dim(shard, mine * part, part, 0) for shard in shards], axis=1)
        return lax.all_gather(piece, ALL, axis=0, tiled=True)

    def stage_expert(shard):
        core = lax.axis_index("core")
        half = shard.shape[1] // n_core
        keep = lax.dynamic_slice_in_dim(shard, core * half, half, 1)
        give = lax.dynamic_slice_in_dim(shard, (1 - core) * half, half, 1)
        got = lax.ppermute(give, "core", SWAP)
        first = core == 0
        return jnp.concatenate([jnp.where(first, keep, got), jnp.where(first, got, keep)], axis=0)

    def local_step(x_in, w_qkv, w_out, w_gate, w_up, w_down, ws_gate, ws_up, ws_down, expert_ids, slot_ids, gate_vals):
        n_batch, seq_len, model_dim = x_in.shape
        n_tokens = n_batch * seq_len
        top_k = expert_ids.shape[-1]
        n_experts = w_gate.shape[0] * n_ep
        capacity = capacity_for(n_tokens, top_k, n_experts)
        n_rows = n_experts * capacity
        s_ff = ws_gate.shape[1]

        n_qkv = w_qkv.shape[1]
        n_attn = n_qkv + w_out.shape[1]
        dense = gather_rows(w_qkv, w_out, ws_gate, ws_up, lax.optimization_barrier(ws_down.T))
        gate_h = lax.all_to_all(stage_expert(w_gate), "fsdp", 0, 0, tiled=True)
        rest = jnp.concatenate([stage_expert(w_up), stage_expert(jnp.swapaxes(w_down, 1, 2))], axis=2)
        dense, rest, gate_h = lax.optimization_barrier((dense, rest, gate_h))
        rest_h = lax.all_to_all(rest, "fsdp", 0, 0, tiled=True)
        qkv_full, out_full, shared_full = dense[:, :n_qkv], dense[:, n_qkv:n_attn], dense[:, n_attn:]

        ids = expert_ids.reshape(n_tokens, top_k)
        slots = slot_ids.reshape(n_tokens, top_k)
        gates = gate_vals.reshape(n_tokens, top_k)
        kept = slots >= 0
        far, chip = lax.axis_index("fsdp"), lax.axis_index("x")
        rel_x = (ids // n_f - chip) % 4
        rel_z = (ids % n_f // 4 - far // 4) % 4
        rel_y = (ids % 4 - far % 4) % 4
        n_chunk = capacity // 8
        turn = slots // 8 % 3
        hop_a = jnp.where(turn == 0, rel_x, jnp.where(turn == 1, rel_z, rel_y))
        hop_b = jnp.where(turn == 0, rel_z, jnp.where(turn == 1, rel_y, rel_x))
        hop_c = jnp.where(turn == 0, rel_y, jnp.where(turn == 1, rel_x, rel_z))
        row = ((slots // 8 * 4 + hop_a) * 4 + hop_b) * 4 + hop_c
        row = jnp.where(kept, row * 8 + slots % 8, n_rows).reshape(-1)
        source_tok = jnp.arange(n_tokens * top_k, dtype=jnp.int32) // top_k
        tok_iota = jnp.arange(n_tokens, dtype=jnp.int32)
        row_source = jnp.full((n_rows,), n_tokens, jnp.int32).at[row].set(source_tok, mode="drop")
        row_gate = jnp.zeros((n_rows,), gates.dtype).at[row].set(gates.reshape(-1), mode="drop")
        spread = (row_source[:, None] == tok_iota[None, :]).astype(jnp.bfloat16)
        merge = jnp.where(row_source[None, :] == tok_iota[:, None], row_gate[None, :], jnp.zeros((), gates.dtype))

        hidden = attention_block(x_in, qkv_full, out_full).reshape(n_tokens, model_dim)
        normed = rms_norm(hidden)
        buffer = jnp.dot(spread, normed, preferred_element_type=jnp.float32).astype(jnp.bfloat16)
        s_gate = jnp.dot(normed, shared_full[:, :s_ff], preferred_element_type=jnp.float32)
        s_up = jnp.dot(normed, shared_full[:, s_ff:2 * s_ff], preferred_element_type=jnp.float32)
        s_inner = (jax.nn.silu(s_gate) * s_up).astype(jnp.bfloat16)
        shared_out = nt_dot(s_inner, shared_full[:, 2 * s_ff:])
        buffer, shared_out = lax.optimization_barrier((buffer, shared_out))
        back = run_exchange(buffer.reshape(n_chunk, 4, 4, 4, 8, model_dim), gate_h, rest_h)
        routed = jnp.dot(merge, back.reshape(n_rows, model_dim), preferred_element_type=jnp.float32)

        summed = hidden.astype(jnp.float32) + shared_out + routed
        return summed.astype(jnp.bfloat16).reshape(n_batch, seq_len, model_dim)

    return jax.shard_map(local_step, mesh=phys, in_specs=(tok_spec, row_spec, row_spec, P(ep, "fsdp", None), P(ep, "fsdp", None), P(ep, None, "fsdp"), row_spec, row_spec, P(None, "fsdp"), tok_spec, tok_spec, tok_spec), out_specs=tok_spec, check_vma=False)
```

time: 752 us -> 654 us (0.87)
  the two profiles are of different devices: /device:TPU:1 before, /device:TPU:16 now
where the time goes in v4:
time: 654 us; the launch traced here: 644 us
  Pallas kernels  308 us (47%)
  waiting for transfers between devices  142 us (22%)
  matrix products  79.9 us (12%)
  local copies, waits for them, and re-layouts  61.9 us (9%)
  other arithmetic  23.9 us (4%)
  starting transfers between devices  15 us (2%)
  between operations  14.2 us (2%)
    pallas_call x1, Pallas kernels, run_exchange(): pl.pallas_call(functools.partial(exchange_kernel, n_chunk), out_shape=[ja...  308 us
    all_gather x1, waiting for transfers between devices, gather_rows(): return lax.all_gather(piece, ALL, axis=0, tiled=True)  110 us
    scatter x1, local copies, waits for them, and re-layouts, local_step(): jnp.zeros((n_rows,), gates.dtype).at[row]  20.9 us
    all_to_all x1, waiting for transfers between devices, local_step(): rest_h = lax.all_to_all(rest, 'fsdp', 0, 0, tiled=True)  19.3 us
    unnamed x27, local copies, waits for them, and re-layouts  17.5 us
    dot_general x1, matrix products, nt_dot(): lax.dot_general(lhs, rhs, (((1,), (1,)), ((), ())), preferred_element_typ...  17.2 us
    dot_general x1, matrix products, attention_block(): jnp.einsum('bsd,dn->bsn', normed, qkv_weight, preferred_element_type=jnp....  15.4 us
  transfers between devices with their start and end apart: 6, of which 3 were waited for; matrix products, arithmetic and copies ran while one was open for 20% of the time, Pallas kernels for 0%

profile of v4, /device:TPU:16, one launch (start us, length us, event | category | flops | bytes accessed | tf_op | source)
XLA Modules:
  0.0 644.4 jit_solution(6172369555777911963)
XLA Ops:
  12.6 1.5 constant_dynamic-slice_fusion
  14.2 6.8 %constant_dynamic-slice_fusion.2 = (bf16[8,1408,64]{2,1,0:T(8,128)(2,1)}, bf16[8,1408,64]{2,1,0:T(8,128)(2,1)}) fusion(bf16[8,1408,128]{2,1,0:T(8,128)(2,1)} %param.17, s32[]{:T(128)S(6)} %select_n.283, s32[]{:T(128)S(6)} %select_n.284), kind=kLoop, calls=%fused_computation.138 | loop fusion | bytes 5767176 | tf_op jit(solution)/shard_map/dynamic-slice
  21.1 4.2 copy.32
  25.7 2.6 constant_dynamic-slice_fusion.3
  29.4 2.4 broadcast_select_fusion.1
  31.8 1.8 pad_maximum_fusion
  33.7 8.4 %all-to-all-start = ((bf16[16,64,1408]{2,1,0:T(8,128)(2,1)}), bf16[16,64,1408]{2,1,0:T(8,128)(2,1)}, u32[]{:S(2)}, u32[]{:S(2)}) async-start(bf16[16,64,1408]{2,1,0:T(8,128)(2,1)} %pad_maximum_fusion), calls=%async_computation | async-start | bytes 5767168 | tf_op jit(solution)/shard_map/all_to_all | solution.py:280
  42.1 3.2 copy.31
  45.6 9.0 %scatter_custom_fusion = s32[3072]{0:T(1024)S(1)} fusion(s32[2304]{0:T(1024)S(1)} %fusion.74, s32[2304]{0:T(1024)S(1)} %add_select_fusion, s32[]{:T(128)} %constant.158.clone.1), kind=kCustom, calls=%fused_computation.132 | custom fusion | bytes 12292 | tf_op jit(solution)/shard_map/scatter | solution.py:303
  54.6 20.9 %scatter_custom_fusion.1 = bf16[3072]{0:T(1024)(128)(2,1)S(1)} fusion(s32[2304]{0:T(1024)S(1)} %fusion.74, bf16[2304]{0:T(1024)(128)(2,1)S(1)} %reshape.678, bf16[]{:T(256)} %constant.169.clone.1), kind=kCustom, calls=%fused_computation.134 | custom fusion | bytes 6146 | tf_op jit(solution)/shard_map/scatter | solution.py:304
  75.5 1.8 fusion.28
  78.1 2.4 broadcast_select_fusion.3
  80.5 1.6 bitcast_select_fusion.1
  82.1 3.0 maximum_maximum_fusion
  85.2 12.3 %all-to-all-done.gate_h = bf16[16,64,1408]{2,1,0:T(8,128)(2,1)} async-done(((bf16[16,64,1408]{2,1,0:T(8,128)(2,1)}), bf16[16,64,1408]{2,1,0:T(8,128)(2,1)}, u32[]{:S(2)}, u32[]{:S(2)}) %all-to-all-start) | async-done | bytes 2883616 | tf_op jit(solution)/shard_map/all_to_all | solution.py:280
  97.4 110.0 %all-gather.2.cloned.1.call-done = bf16[2048,16640]{1,0:T(8,128)(2,1)} async-done(((bf16[16,16640]{1,0:T(8,128)(2,1)}), bf16[2048,16640]{1,0:T(8,128)(2,1)}) %all-gather.2.cloned.1.call-update) | async-done | bytes 68157456 | tf_op jit(solution)/shard_map/all_gather | solution.py:257
  207.5 15.4 %fusion.44 = bf16[48,8,48,128]{3,1,2,0:T(8,128)(2,1)S(1)} fusion(bf16[2048,16640]{1,0:T(8,128)(2,1)} %all-gather.2.cloned.1.call-done, bf16[1,384,2048]{2,1,0:T(8,128)(2,1)} %param.12, f32[384]{0:T(512)S(1)} %add_rsqrt_fusion.1), kind=kOutput, calls=%fused_computation.51 | convolution fusion | flops 9668395008 | bytes 31458816 | tf_op jit(solution)/shard_map/bsd,dn->bsn/dot_general | solution.py:41
  224.2 2.6 fusion.92
  226.8 2.9 copy.33
  229.7 6.0 all-to-all-start.1
  235.7 2.2 fusion.62
  237.9 2.3 fusion.51
  240.2 1.9 fusion.55
  242.1 5.1 fusion.93
  247.2 5.1 fusion.48
  252.3 7.3 %fusion.31 = (f32[384]{0:T(512)S(1)}, bf16[384,2048]{1,0:T(8,128)(2,1)S(1)}) fusion(bf16[384,2048]{0,1:T(8,128)(2,1)S(1)} %bitcast.55, bf16[2048,16640]{1,0:T(8,128)(2,1)} %all-gather.2.cloned.1.call-done, bf16[1,384,2048]{2,1,0:T(8,128)(2,1)S(1)} %copy-done.2), kind=kOutput, calls=%fused_computation.38 | convolution fusion | flops 3225943552 | bytes 13108736 | tf_op jit(solution)/shard_map/bsn,nm->bsm/dot_general | solution.py:50
  259.7 10.6 %convolution_convert_fusion = bf16[3072,2048]{1,0:T(8,128)(2,1)} fusion(s32[3072]{0:T(1024)S(1)} %scatter_custom_fusion, bf16[384,2048]{1,0:T(8,128)(2,1)S(1)} %get-tuple-element.39, f32[384]{0:T(512)S(1)} %add_rsqrt_fusion), kind=kOutput, calls=%fused_computation.11 | convolution fusion | flops 4841668608 | bytes 14169600 | tf_op jit(solution)/shard_map/dot_general | solution.py:310
  270.3 11.1 %fusion.7 = f32[384,2816]{1,0:T(8,128)} fusion(bf16[2048,16640]{1,0:T(8,128)(2,1)} %all-gather.2.cloned.1.call-done, bf16[384,2048]{1,0:T(8,128)(2,1)S(1)} %get-tuple-element.39, f32[384]{0:T(512)S(1)} %add_rsqrt_fusion), kind=kOutput, calls=%fused_computation.9 | convolution fusion | flops 4431544320 | bytes 17434112 | tf_op jit(solution)/shard_map/dot_general | solution.py:311
  281.3 17.2 %fusion.3 = f32[384,2048]{1,0:T(8,128)} fusion(bf16[2048,16640]{1,0:T(8,128)(2,1)} %all-gather.2.cloned.1.call-done, f32[384,2816]{1,0:T(8,128)} %fusion.7, bf16[384,2048]{1,0:T(8,128)(2,1)S(1)} %get-tuple-element.39, f32[384]{0:T(512)S(1)} %add_rsqrt_fusion), kind=kOutput, calls=%fused_computation.5 | convolution fusion | flops 8867217408 | bytes 32114176 | tf_op jit(solution)/shard_map/dot_general | solution.py:59
  298.6 19.3 %all-to-all-done.1.rest_h = bf16[16,64,2816]{2,1,0:T(8,128)(2,1)} async-done(((bf16[16,64,2816]{2,1,0:T(8,128)(2,1)}), bf16[16,64,2816]{2,1,0:T(8,128)(2,1)}, u32[]{:S(2)}, u32[]{:S(2)}) %all-to-all-start.1) | async-done | bytes 5767200 | tf_op jit(solution)/shard_map/all_to_all | solution.py:283
  317.9 308.0 %expert_exchange.1 = (bf16[6,4,4,4,8,2048]{5,4,3,2,1,0:T(8,128)(2,1)}, bf16[6,3,4,4,8,2048]{5,4,3,2,1,0:T(8,128)(2,1)}, bf16[6,3,4,4,8,2048]{5,4,3,2,1,0:T(8,128...) custom-call(bf16[6,4,4,4,8,2048]{5,4,3,2,1,0:T(8,128)(2,1)} %bitcast, ...), custom_call_target="tpu_custom_call" | custom-call | tf_op jit(solution)/shard_map/expert_exchange/pallas_call | solution.py:220
  625.8 11.3 %fusion.37 = bf16[1,384,2048]{2,1,0:T(8,128)(2,1)} fusion(bf16[3072,2048]{1,0:T(8,128)(2,1)} %bitcast.54, f32[384,2048]{1,0:T(8,128)} %fusion.3, bf16[384,2048]{1,0:T(8,128)(2,1)S(1)} %get-tuple-element.39, s32[3072]{0:T(1024)S(1)} %scatter_custom_fusion, bf16[3072]{0:T(1024)(128)(2,1)S(1)} %scatter_custom_fusion.1), kind=kOutput, calls=%fused_computation.47 | convolution fusion | flops 4837343232 | bytes 18892800 | tf_op jit(solution)/shard_map/dot_general | solution.py:317
  (45 shorter events, 10.1 us)
Async XLA Ops:
  6.5 1.1 copy-start
  6.5 200.9 %all-gather.2.cloned.1.call-start = ((), (), s32[]{:S(2)}) async-start(), calls=%async_computation.2 | async-start | bytes 68689920 | tf_op jit(solution)/shard_map/all_gather | solution.py:257
  11.8 0.9 copy-start.4
  14.1 15.3 %collective-permute-start.2 = (bf16[8,64,1408]{2,1,0:T(8,128)(2,1)S(1)}, bf16[8,64,1408]{2,1,0:T(8,128)(2,1)}, u32[]{:S(2)}, u32[]{:S(2)}) collective-permute-start(bf16[8,64,1408]{2,1,0:T(8,128)(2,1)S(1)} %constant_dynamic-slice_fusion), channel_id=1, source_target_pairs={{0,1},{1,0},{2,3},{3,2},{4,5},{5,4},{6,7},{7,6},{8,9},{9,8},{10,11... | collective-permute-start | bytes 4325384 | tf_op jit(solution)/shard_map/ppermute | solution.py:264
  21.1 7.3 %copy-start.5 = (s32[1,384,6]{1,0,2:T(1,128)S(1)}, s32[1,384,6]{1,0,2:T(1,128)}, u32[]{:S(2)}) copy-start(s32[1,384,6]{1,0,2:T(1,128)} %param.22) | copy-start | bytes 27652
  21.1 7.6 %copy-start.6 = (s32[1,384,6]{1,0,2:T(1,128)S(1)}, s32[1,384,6]{1,0,2:T(1,128)}, u32[]{:S(2)}) copy-start(s32[1,384,6]{1,0,2:T(1,128)} %param.21) | copy-start | bytes 27652
  25.2 55.2 %collective-permute-start.1 = (bf16[8,64,1408]{2,1,0:T(8,128)(2,1)}, bf16[8,64,1408]{2,1,0:T(8,128)(2,1)}, u32[]{:S(2)}, u32[]{:S(2)}) collective-permute-start(bf16[8,64,1408]{2,1,0:T(8,128)(2,1)} %bitcast.3), channel_id=1, source_target_pairs={{0,1},{1,0},{2,3},{3,2},{4,5},{5,4},{6,7},{7,6},{8,9},{9,8},{10,11... | collective-permute-start | bytes 4325384 | tf_op jit(solution)/shard_map/ppermute | solution.py:264
  28.3 49.7 %collective-permute-start = (bf16[8,64,1408]{2,1,0:T(8,128)(2,1)}, bf16[8,64,1408]{2,1,0:T(8,128)(2,1)}, u32[]{:S(2)}, u32[]{:S(2)}) collective-permute-start(bf16[8,64,1408]{2,1,0:T(8,128)(2,1)} %constant_dynamic-slice_fusion.3), channel_id=1, source_target_pairs={{0,1},{1,0},{2,3},{3,2},{4,5},{5,4},{6,7},{7,6},{8,9},{9,8},{10,11... | collective-permute-start | bytes 4325384 | tf_op jit(solution)/shard_map/ppermute | solution.py:264
  33.7 63.7 %all-to-all-start = ((bf16[16,64,1408]{2,1,0:T(8,128)(2,1)}), bf16[16,64,1408]{2,1,0:T(8,128)(2,1)}, u32[]{:S(2)}, u32[]{:S(2)}) async-start(bf16[16,64,1408]{2,1,0:T(8,128)(2,1)} %pad_maximum_fusion), calls=%async_computation | async-start | bytes 5767168 | tf_op jit(solution)/shard_map/all_to_all | solution.py:280
  42.0 3.2 copy-start.7
  229.7 88.2 %all-to-all-start.1 = ((bf16[16,64,2816]{2,1,0:T(8,128)(2,1)}), bf16[16,64,2816]{2,1,0:T(8,128)(2,1)}, u32[]{:S(2)}, u32[]{:S(2)}) async-start(bf16[16,64,2816]{2,1,0:T(8,128)(2,1)} %maximum_maximum_fusion), calls=%async_computation.1 | async-start | bytes 11534336 | tf_op jit(solution)/shard_map/all_to_all | solution.py:283
  242.1 5.1 copy-start.3
  247.2 5.1 copy-start.2
  625.8 11.3 %copy-start.1 = (bf16[2816,128]{1,0:T(8,128)(2,1)S(1)}, bf16[2816,128]{1,0:T(8,128)(2,1)}, u32[]{:S(2)}) copy-start(bf16[2816,128]{1,0:T(8,128)(2,1)} %param.20) | copy-start | bytes 2162692
Sparse Core Ops, SparseCore 0:
  12.8 194.6 all-gather.1

commit v5 on v4

--- a/solution.py
+++ b/solution.py
@@ -59,7 +59,7 @@
     return lax.dot_general(lhs, rhs, (((1,), (1,)), ((), ())), preferred_element_type=jnp.float32)
 
 
-def exchange_kernel(n_chunk, inp, gate_h, rest_h, out, r1, r2, r3, b1, b2, own, w13, w2, xin, inner, yall, w_sem, in_sem, tx, rx, fin, ld):
+def exchange_kernel(n_chunk, spread_in, rows_in, gate_h, rest_h, out, r1, r2, r3, b1, b2, own, inp, spread, rows, w13, w2, xin, inner, yall, w_sem, in_sem, tx, rx, fin, ld):
     f, x, core = lax.axis_index("fsdp"), lax.axis_index("x"), lax.axis_index("core")
     z, y = f // 4, f % 4
     copy = pltpu.make_async_copy
@@ -155,51 +155,85 @@
         wait(own.at[k], ld.at[0, k])
         wait(out.at[k, 0, 0, 0], ld.at[1, k])
 
-    early, late = range(0, n_chunk // 2), range(n_chunk // 2, n_chunk)
-    for k in early:
-        hop1(k)
+    def place(k):
+        block = spread[pl.ds(k * per_chunk, per_chunk), :]
+        for n in range(rows.shape[1] // 512):
+            cols = pl.ds(n * 512, 512)
+            picked = jnp.dot(block, rows[:, cols], preferred_element_type=jnp.float32)
+            inp[k, :, :, :, :, cols] = picked.astype(jnp.bfloat16).reshape(inp.shape[1:5] + (512,))
+
+    per_chunk = spread.shape[0] // n_chunk
     partner = {"core": 1 - core}
-    for part, (half, base) in enumerate(((gate_h, 0), (rest_h, 0))):
+    copy(rows_in, rows, ld.at[0, 0]).start()
+    copy(spread_in, spread, ld.at[1, 0]).start()
+    barrier = pltpu.get_barrier_semaphore()
+    for axis in range(3):
+        for h in (1, 2, 3):
+            pl.semaphore_signal(barrier, inc=1, device_id=dev(axis, h), device_id_type=pl.DeviceIdType.MESH)
+    pl.semaphore_signal(barrier, inc=1, device_id=partner, device_id_type=pl.DeviceIdType.MESH)
+    wait(rows, ld.at[0, 0])
+    wait(spread, ld.at[1, 0])
+    place(0)
+    pl.semaphore_wait(barrier, 10)
+    hop1(0)
+    place(1)
+    hop1(1)
+    place(2)
+    hop1(2)
+    for part, half in enumerate((gate_h, rest_h)):
         for j in range(n_tile):
-            src = half.at[:, :, pl.ds(base + j * 128, 128)]
+            src = half.at[:, :, pl.ds(j * 128, 128)]
             dst = w13.at[:, core, :, pl.ds(j * 256 + part * 128, 128)]
             copy(src, dst, w_sem.at[0]).start()
             send(src, dst, w_sem.at[2], w_sem.at[4], partner)
     down_h = rest_h.at[:, :, pl.ds(n_tile * 128, n_tile * 128)]
     copy(down_h, w2.at[:, core], w_sem.at[1]).start()
     send(down_h, w2.at[:, core], w_sem.at[3], w_sem.at[5], partner)
-
-    for k in early:
-        hop2(k)
-    for k in late:
-        hop1(k)
-    for k in early:
-        hop3(k)
-    for k in late:
-        hop2(k)
+    for k in (4, 5, 3):
+        place(k)
+        if k != 3:
+            hop1(k)
+    hop2(0)
+    hop2(1)
+    hop2(2)
+    hop1(3)
+    hop3(2)
+    hop2(5)
+    hop2(4)
+    hop3(0)
+    hop2(3)
+    hop3(1)
+    hop3(4)
     for i in (0, 2, 4):
         wait(w13.at[:, 0], w_sem.at[i])
     for i in (1, 3, 5):
         wait(w2.at[:, 0], w_sem.at[i])
-    for i, k in enumerate(early):
+
+    def turn(k):
         experts(k)
         back1(k)
-        if i == 0:
-            for q in late:
-                hop3(q)
-    for k in early:
+
+    def fold(k):
         landed(k)
         back2(k)
-    for i, k in enumerate(late):
-        experts(k)
-        back1(k)
-        if i == 1:
-            for q in early:
-                back3(q)
-    for k in late:
-        landed(k)
-        back2(k)
-    for k in late:
+
+    turn(2)
+    hop3(5)
+    hop3(3)
+    for k in (0, 1, 3):
+        turn(k)
+    fold(2)
+    fold(0)
+    turn(4)
+    fold(1)
+    turn(5)
+    back3(0)
+    fold(3)
+    back3(2)
+    fold(5)
+    back3(1)
+    fold(4)
+    for k in (5, 4, 3):
         back3(k)
 
     wait(out.at[:, pl.ds(1, 3)], tx.at[6])
@@ -212,17 +246,21 @@
     wait(out.at[:, 0, 0, pl.ds(1, 3)], fin.at[2])
 
 
-def run_exchange(inp, gate_h, rest_h):
-    n_chunk, _, _, _, blk, dim = inp.shape
+def run_exchange(spread, rows, gate_h, rest_h):
+    blk, dim = 8, rows.shape[1]
+    n_chunk = spread.shape[0] // (64 * blk)
     width = gate_h.shape[2]
     bf = jnp.bfloat16
     shapes = [(4, 4, 4), (3, 4, 4), (3, 4, 4), (3, 4, 4), (3, 4, 4), (3, 4, 3), (4, 4)]
     outs = pl.pallas_call(
         functools.partial(exchange_kernel, n_chunk),
         out_shape=[jax.ShapeDtypeStruct((n_chunk,) + sh + (blk, dim), bf) for sh in shapes],
-        in_specs=[pl.BlockSpec(memory_space=pl.ANY)] * 3,
+        in_specs=[pl.BlockSpec(memory_space=pl.ANY)] * 4,
         out_specs=[pl.BlockSpec(memory_space=pl.ANY)] * len(shapes),
         scratch_shapes=[
+            pltpu.VMEM((n_chunk, 4, 4, 4, blk, dim), bf),
+            pltpu.VMEM(spread.shape, bf),
+            pltpu.VMEM(rows.shape, bf),
             pltpu.VMEM((16, 2, 64, 2 * width), bf),
             pltpu.VMEM((16, 2, 64, width), bf),
             pltpu.VMEM((4, 4, 4, blk, dim), bf),
@@ -235,9 +273,9 @@
             pltpu.SemaphoreType.DMA((3,)),
             pltpu.SemaphoreType.DMA((2, n_chunk)),
         ],
-        compiler_params=pltpu.CompilerParams(has_side_effects=True, vmem_limit_bytes=60 * 2**20),
+        compiler_params=pltpu.CompilerParams(has_side_effects=True, collective_id=0, vmem_limit_bytes=60 * 2**20),
         name="expert_exchange",
-    )(inp, gate_h, rest_h)
+    )(spread, rows, gate_h, rest_h)
     return outs[0]
 
 
@@ -291,7 +329,6 @@
         rel_x = (ids // n_f - chip) % 4
         rel_z = (ids % n_f // 4 - far // 4) % 4
         rel_y = (ids % 4 - far % 4) % 4
-        n_chunk = capacity // 8
         turn = slots // 8 % 3
         hop_a = jnp.where(turn == 0, rel_x, jnp.where(turn == 1, rel_z, rel_y))
         hop_b = jnp.where(turn == 0, rel_z, jnp.where(turn == 1, rel_y, rel_x))
@@ -307,13 +344,12 @@
 
         hidden = attention_block(x_in, qkv_full, out_full).reshape(n_tokens, model_dim)
         normed = rms_norm(hidden)
-        buffer = jnp.dot(spread, normed, preferred_element_type=jnp.float32).astype(jnp.bfloat16)
         s_gate = jnp.dot(normed, shared_full[:, :s_ff], preferred_element_type=jnp.float32)
         s_up = jnp.dot(normed, shared_full[:, s_ff:2 * s_ff], preferred_element_type=jnp.float32)
         s_inner = (jax.nn.silu(s_gate) * s_up).astype(jnp.bfloat16)
         shared_out = nt_dot(s_inner, shared_full[:, 2 * s_ff:])
-        buffer, shared_out = lax.optimization_barrier((buffer, shared_out))
-        back = run_exchange(buffer.reshape(n_chunk, 4, 4, 4, 8, model_dim), gate_h, rest_h)
+        routed_rows, shared_out = lax.optimization_barrier((normed, shared_out))
+        back = run_exchange(spread, routed_rows, gate_h, rest_h)
         routed = jnp.dot(merge, back.reshape(n_rows, model_dim), preferred_element_type=jnp.float32)
 
         summed = hidden.astype(jnp.float32) + shared_out + routed

time: 654 us -> 640 us (0.979)
  the two profiles are of different devices: /device:TPU:16 before, /device:TPU:1 now
where the time goes in v5:
time: 640 us; the launch traced here: 628 us
  Pallas kernels  284 us (44%)
  waiting for transfers between devices  157 us (25%)
  matrix products  68.3 us (11%)
  local copies, waits for them, and re-layouts  64.3 us (10%)
  other arithmetic  25.2 us (4%)
  starting transfers between devices  15.1 us (2%)
  between operations  13.9 us (2%)
    pallas_call x1, Pallas kernels, run_exchange(): pl.pallas_call(functools.partial(exchange_kernel, n_chunk), out_shape=[ja...  284 us
    all_gather x1, waiting for transfers between devices, gather_rows(): return lax.all_gather(piece, ALL, axis=0, tiled=True)  106 us
    all_to_all x1, waiting for transfers between devices, local_step(): rest_h = lax.all_to_all(rest, 'fsdp', 0, 0, tiled=True)  32.9 us
    scatter x1, local copies, waits for them, and re-layouts, local_step(): jnp.zeros((n_rows,), gates.dtype).at[row]  20.7 us
    unnamed x35, local copies, waits for them, and re-layouts  18.8 us
    all_to_all x1, waiting for transfers between devices, local_step(): gate_h = lax.all_to_all(stage_expert(w_gate), 'fsdp', 0, 0, tiled=True)  17.6 us
    dot_general x1, matrix products, nt_dot(): lax.dot_general(lhs, rhs, (((1,), (1,)), ((), ())), preferred_element_typ...  17.2 us
    dot_general x1, matrix products, attention_block(): jnp.einsum('bsd,dn->bsn', normed, qkv_weight, preferred_element_type=jnp....  15.4 us
  transfers between devices with their start and end apart: 6, of which 3 were waited for; matrix products, arithmetic and copies ran while one was open for 19% of the time, Pallas kernels for 0%

profile of v5, /device:TPU:1, one launch (start us, length us, event | category | flops | bytes accessed | tf_op | source)
XLA Modules:
  0.0 627.8 jit_solution(16836480211095010309)
XLA Ops:
  12.6 2.6 constant_dynamic-slice_fusion
  15.2 1.4 collective-permute-start.2
  16.5 6.9 %constant_dynamic-slice_fusion.2 = (bf16[8,1408,64]{2,1,0:T(8,128)(2,1)}, bf16[8,1408,64]{2,1,0:T(8,128)(2,1)}) fusion(bf16[8,1408,128]{2,1,0:T(8,128)(2,1)} %param.17, s32[]{:T(128)S(6)} %select_n.283, s32[]{:T(128)S(6)} %select_n.284), kind=kLoop, calls=%fused_computation.137 | loop fusion | bytes 5767176 | tf_op jit(solution)/shard_map/dynamic-slice
  23.4 4.4 copy.32
  27.8 2.6 constant_dynamic-slice_fusion.3
  33.1 2.4 broadcast_select_fusion.1
  35.6 1.9 pad_maximum_fusion
  37.4 8.0 %all-to-all-start = ((bf16[16,64,1408]{2,1,0:T(8,128)(2,1)}), bf16[16,64,1408]{2,1,0:T(8,128)(2,1)}, u32[]{:S(2)}, u32[]{:S(2)}) async-start(bf16[16,64,1408]{2,1,0:T(8,128)(2,1)} %pad_maximum_fusion), calls=%async_computation | async-start | bytes 5767168 | tf_op jit(solution)/shard_map/all_to_all | solution.py:318
  45.5 3.2 copy.31
  49.0 9.2 %scatter_custom_fusion = s32[3072]{0:T(1024)S(1)} fusion(s32[2304]{0:T(1024)S(1)} %fusion.74, s32[2304]{0:T(1024)S(1)} %add_select_fusion, s32[]{:T(128)} %constant.159.clone.1), kind=kCustom, calls=%fused_computation.131 | custom fusion | bytes 12292 | tf_op jit(solution)/shard_map/scatter | solution.py:340
  58.2 20.7 %scatter_custom_fusion.1 = bf16[3072]{0:T(1024)(128)(2,1)S(1)} fusion(s32[2304]{0:T(1024)S(1)} %fusion.74, bf16[2304]{0:T(1024)(128)(2,1)S(1)} %reshape.674, bf16[]{:T(256)} %constant.169.clone.1), kind=kCustom, calls=%fused_computation.133 | custom fusion | bytes 6146 | tf_op jit(solution)/shard_map/scatter | solution.py:341
  78.9 2.4 fusion.19.spread_in
  81.3 2.4 broadcast_select_fusion.3
  83.7 1.6 bitcast_select_fusion.1
  85.4 3.0 maximum_maximum_fusion
  88.3 17.6 %all-to-all-done.gate_h = bf16[16,64,1408]{2,1,0:T(8,128)(2,1)} async-done(((bf16[16,64,1408]{2,1,0:T(8,128)(2,1)}), bf16[16,64,1408]{2,1,0:T(8,128)(2,1)}, u32[]{:S(2)}, u32[]{:S(2)}) %all-to-all-start) | async-done | bytes 2883616 | tf_op jit(solution)/shard_map/all_to_all | solution.py:318
  105.9 106.2 %all-gather.2.cloned.1.call-done = bf16[2048,16640]{1,0:T(8,128)(2,1)} async-done(((bf16[16,16640]{1,0:T(8,128)(2,1)}), bf16[2048,16640]{1,0:T(8,128)(2,1)}) %all-gather.2.cloned.1.call-update) | async-done | bytes 68157456 | tf_op jit(solution)/shard_map/all_gather | solution.py:295
  212.2 15.4 %fusion.44 = bf16[48,8,48,128]{3,1,2,0:T(8,128)(2,1)S(1)} fusion(bf16[2048,16640]{1,0:T(8,128)(2,1)} %all-gather.2.cloned.1.call-done, bf16[1,384,2048]{2,1,0:T(8,128)(2,1)} %param.12, f32[384]{0:T(512)S(1)} %add_rsqrt_fusion.1), kind=kOutput, calls=%fused_computation.50 | convolution fusion | flops 9668395008 | bytes 31458816 | tf_op jit(solution)/shard_map/bsd,dn->bsn/dot_general | solution.py:41
  228.9 2.5 fusion.88
  231.4 2.9 copy.33
  234.3 5.2 all-to-all-start.1
  239.5 2.2 fusion.62
  241.7 2.3 fusion.51
  244.0 1.9 fusion.55
  245.9 5.1 fusion.89
  251.0 5.1 fusion.48
  256.1 7.3 %fusion.32 = (f32[384]{0:T(512)S(1)}, bf16[384,2048]{1,0:T(8,128)(2,1)S(1)}) fusion(bf16[384,2048]{0,1:T(8,128)(2,1)S(1)} %bitcast.56, bf16[2048,16640]{1,0:T(8,128)(2,1)} %all-gather.2.cloned.1.call-done, bf16[1,384,2048]{2,1,0:T(8,128)(2,1)S(1)} %copy-done.4), kind=kOutput, calls=%fused_computation.38 | convolution fusion | flops 3225943552 | bytes 13108736 | tf_op jit(solution)/shard_map/bsn,nm->bsm/dot_general | solution.py:50
  265.0 10.1 %fusion.7 = f32[384,2816]{1,0:T(8,128)} fusion(bf16[384,2048]{1,0:T(8,128)(2,1)S(1)} %fusion.33.rows_in, bf16[2048,16640]{1,0:T(8,128)(2,1)} %all-gather.2.cloned.1.call-done), kind=kOutput, calls=%fused_computation.9 | convolution fusion | flops 4429185024 | bytes 17432576 | tf_op jit(solution)/shard_map/dot_general | solution.py:347
  275.1 17.2 %fusion.3 = f32[384,2048]{1,0:T(8,128)} fusion(bf16[2048,16640]{1,0:T(8,128)(2,1)} %all-gather.2.cloned.1.call-done, bf16[384,2048]{1,0:T(8,128)(2,1)S(1)} %fusion.33.rows_in, f32[384,2816]{1,0:T(8,128)} %fusion.7), kind=kOutput, calls=%fused_computation.5 | convolution fusion | flops 8864858112 | bytes 32112640 | tf_op jit(solution)/shard_map/dot_general | solution.py:59
  292.3 32.9 %all-to-all-done.1.rest_h = bf16[16,64,2816]{2,1,0:T(8,128)(2,1)} async-done(((bf16[16,64,2816]{2,1,0:T(8,128)(2,1)}), bf16[16,64,2816]{2,1,0:T(8,128)(2,1)}, u32[]{:S(2)}, u32[]{:S(2)}) %all-to-all-start.1) | async-done | bytes 5767200 | tf_op jit(solution)/shard_map/all_to_all | solution.py:321
  325.2 284.3 %expert_exchange.1 = (bf16[6,4,4,4,8,2048]{5,4,3,2,1,0:T(8,128)(2,1)}, bf16[6,3,4,4,8,2048]{5,4,3,2,1,0:T(8,128)(2,1)}, bf16[6,3,4,4,8,2048]{5,4,3,2,1,0:T(8,128...) custom-call(bf16[3072,384]{1,0:T(8,128)(2,1)} %fusion.19.spread_in, ...), custom_call_target="tpu_custom_call" | custom-call | tf_op jit(solution)/shard_map/expert_exchange/pallas_call | solution.py:255
  609.5 11.3 %fusion.38 = bf16[1,384,2048]{2,1,0:T(8,128)(2,1)} fusion(bf16[3072,2048]{1,0:T(8,128)(2,1)} %bitcast.55, f32[384,2048]{1,0:T(8,128)} %fusion.3, bf16[384,2048]{1,0:T(8,128)(2,1)S(1)} %copy-done.7, s32[3072]{0:T(1024)S(1)} %scatter_custom_fusion, bf16[3072]{0:T(1024)(128)(2,1)S(1)} %scatter_custom_fusion.1), kind=kOutput, calls=%fused_computation.47 | convolution fusion | flops 4837343232 | bytes 18892800 | tf_op jit(solution)/shard_map/dot_general | solution.py:353
  (54 shorter events, 11.8 us)
Async XLA Ops:
  6.5 1.1 copy-start
  6.5 205.6 %all-gather.2.cloned.1.call-start = ((), (), s32[]{:S(2)}) async-start(), calls=%async_computation.2 | async-start | bytes 68689920 | tf_op jit(solution)/shard_map/all_gather | solution.py:295
  11.8 0.8 copy-start.8
  15.2 18.0 %collective-permute-start.2 = (bf16[8,64,1408]{2,1,0:T(8,128)(2,1)}, bf16[8,64,1408]{2,1,0:T(8,128)(2,1)}, u32[]{:S(2)}, u32[]{:S(2)}) collective-permute-start(bf16[8,64,1408]{2,1,0:T(8,128)(2,1)} %constant_dynamic-slice_fusion), channel_id=1, source_target_pairs={{0,1},{1,0},{2,3},{3,2},{4,5},{5,4},{6,7},{7,6},{8,9},{9,8},{10,11... | collective-permute-start | bytes 4325384 | tf_op jit(solution)/shard_map/ppermute | solution.py:302
  23.4 7.5 %copy-start.9 = (s32[1,384,6]{1,0,2:T(1,128)S(1)}, s32[1,384,6]{1,0,2:T(1,128)}, u32[]{:S(2)}) copy-start(s32[1,384,6]{1,0,2:T(1,128)} %param.22) | copy-start | bytes 27652
  23.4 7.8 %copy-start.10 = (s32[1,384,6]{1,0,2:T(1,128)S(1)}, s32[1,384,6]{1,0,2:T(1,128)}, u32[]{:S(2)}) copy-start(s32[1,384,6]{1,0,2:T(1,128)} %param.21) | copy-start | bytes 27652
  23.4 8.6 %copy-start.3 = (bf16[1,384,2048]{2,1,0:T(8,128)(2,1)S(1)}, bf16[1,384,2048]{2,1,0:T(8,128)(2,1)}, u32[]{:S(2)}) copy-start(bf16[1,384,2048]{2,1,0:T(8,128)(2,1)} %param.12) | copy-start | bytes 4718596
  27.8 55.9 %collective-permute-start.1 = (bf16[8,64,1408]{2,1,0:T(8,128)(2,1)}, bf16[8,64,1408]{2,1,0:T(8,128)(2,1)}, u32[]{:S(2)}, u32[]{:S(2)}) collective-permute-start(bf16[8,64,1408]{2,1,0:T(8,128)(2,1)} %bitcast.54), channel_id=1, source_target_pairs={{0,1},{1,0},{2,3},{3,2},{4,5},{5,4},{6,7},{7,6},{8,9},{9,8},{10,11... | collective-permute-start | bytes 4325384 | tf_op jit(solution)/shard_map/ppermute | solution.py:302
  30.4 50.9 %collective-permute-start = (bf16[8,64,1408]{2,1,0:T(8,128)(2,1)}, bf16[8,64,1408]{2,1,0:T(8,128)(2,1)}, u32[]{:S(2)}, u32[]{:S(2)}) collective-permute-start(bf16[8,64,1408]{2,1,0:T(8,128)(2,1)} %constant_dynamic-slice_fusion.3), channel_id=1, source_target_pairs={{0,1},{1,0},{2,3},{3,2},{4,5},{5,4},{6,7},{7,6},{8,9},{9,8},{10,11... | collective-permute-start | bytes 4325384 | tf_op jit(solution)/shard_map/ppermute | solution.py:302
  37.4 68.5 %all-to-all-start = ((bf16[16,64,1408]{2,1,0:T(8,128)(2,1)}), bf16[16,64,1408]{2,1,0:T(8,128)(2,1)}, u32[]{:S(2)}, u32[]{:S(2)}) async-start(bf16[16,64,1408]{2,1,0:T(8,128)(2,1)} %pad_maximum_fusion), calls=%async_computation | async-start | bytes 5767168 | tf_op jit(solution)/shard_map/all_to_all | solution.py:318
  45.4 3.2 copy-start.11
  234.3 91.0 %all-to-all-start.1 = ((bf16[16,64,2816]{2,1,0:T(8,128)(2,1)}), bf16[16,64,2816]{2,1,0:T(8,128)(2,1)}, u32[]{:S(2)}, u32[]{:S(2)}) async-start(bf16[16,64,2816]{2,1,0:T(8,128)(2,1)} %maximum_maximum_fusion), calls=%async_computation.1 | async-start | bytes 11534336 | tf_op jit(solution)/shard_map/all_to_all | solution.py:321
  245.9 5.1 copy-start.5
  251.0 5.1 copy-start.4
  263.4 1.2 copy-start.6
  264.9 10.1 %copy-start.2 = (bf16[384,2048]{1,0:T(8,128)(2,1)}, bf16[384,2048]{1,0:T(8,128)(2,1)S(1)}, u32[]{:S(2)}) copy-start(bf16[384,2048]{1,0:T(8,128)(2,1)S(1)} %fusion.33.rows_in) | copy-start | bytes 4718596
  292.3 317.2 %copy-start.7 = (bf16[384,2048]{1,0:T(8,128)(2,1)S(1)}, bf16[384,2048]{1,0:T(8,128)(2,1)}, u32[]{:S(2)}) copy-start(bf16[384,2048]{1,0:T(8,128)(2,1)} %copy-done.6) | copy-start | bytes 4718596
  609.5 11.3 %copy-start.1 = (bf16[2816,128]{1,0:T(8,128)(2,1)S(1)}, bf16[2816,128]{1,0:T(8,128)(2,1)}, u32[]{:S(2)}) copy-start(bf16[2816,128]{1,0:T(8,128)(2,1)} %param.20) | copy-start | bytes 2162692
Sparse Core Ops, SparseCore 0:
  12.7 199.4 all-gather.1

commit v6 on v5

--- a/solution.py
+++ b/solution.py
@@ -21,34 +21,62 @@
     return (vals_f32 * lax.rsqrt(mean_sq + EPSILON)).astype(jnp.bfloat16)
 
 
-def rotary_embed(heads_in, positions):
+def attention_kernel(q_ref, k_ref, v_ref, cos_ref, sin_ref, out_ref):
+    seq_len, width = q_ref.shape
+    cos_tab, sin_tab = cos_ref[...], sin_ref[...]
+    block = 128
+
+    def rotate(vals):
+        vals_f32 = vals.astype(jnp.float32)
+        return (vals_f32 * cos_tab + pltpu.roll(vals_f32, HEAD_DIM // 2, 1) * sin_tab).astype(jnp.bfloat16)
+
+    for h in range(width // HEAD_DIM):
+        cols = slice(h * HEAD_DIM, (h + 1) * HEAD_DIM)
+        query, key, value = rotate(q_ref[:, cols]), rotate(k_ref[:, cols]), v_ref[:, cols]
+        for i in range(seq_len // block):
+            seen = (i + 1) * block
+            scores = lax.dot_general(query[i * block:seen], key[:seen], (((1,), (1,)), ((), ())), preferred_element_type=jnp.float32) * (HEAD_DIM ** -0.5)
+            row = lax.broadcasted_iota(jnp.int32, scores.shape, 0) + i * block
+            scores = jnp.where(row >= lax.broadcasted_iota(jnp.int32, scores.shape, 1), scores, -1e30)
+            weights = jnp.exp(scores - jnp.max(scores, axis=-1, keepdims=True))
+            probs = (weights / jnp.sum(weights, axis=-1, keepdims=True)).astype(jnp.bfloat16)
+            mixed = jnp.dot(probs, value[:seen], preferred_element_type=jnp.float32)
+            out_ref[i * block:seen, cols] = mixed.astype(jnp.bfloat16)
+
+
+def attention_block(x_in, qkv_weight, out_weight):
+    _, seq_len, model_dim = x_in.shape
+    n_heads = qkv_weight.shape[1] // (3 * HEAD_DIM)
     half_dim = HEAD_DIM // 2
+    tokens = x_in.reshape(seq_len, model_dim)
+    normed = rms_norm(tokens)
+    qkv_proj = jnp.dot(normed, qkv_weight, preferred_element_type=jnp.float32).astype(jnp.bfloat16)
+    positions = jnp.arange(seq_len, dtype=jnp.float32)
     inv_freq = ROPE_BASE ** (-jnp.arange(half_dim, dtype=jnp.float32) * (2.0 / HEAD_DIM))
     angles = positions[:, None] * inv_freq[None, :]
-    cos_tab = jnp.cos(angles)[:, None, :]
-    sin_tab = jnp.sin(angles)[:, None, :]
-    vals_f32 = heads_in.astype(jnp.float32)
-    first_half = vals_f32[..., :half_dim]
-    second_half = vals_f32[..., half_dim:]
-    rotated = jnp.concatenate([first_half * cos_tab - second_half * sin_tab, second_half * cos_tab + first_half * sin_tab], axis=-1)
-    return rotated.astype(jnp.bfloat16)
-
-
-def attention_block(x_in, qkv_weight, out_weight):
-    n_batch, seq_len, _ = x_in.shape
-    n_heads = qkv_weight.shape[1] // (3 * HEAD_DIM)
-    normed = rms_norm(x_in)
-    qkv_proj = jnp.einsum("bsd,dn->bsn", normed, qkv_weight, preferred_element_type=jnp.float32).astype(jnp.bfloat16)
-    qkv_proj = qkv_proj.reshape(n_batch, seq_len, 3, n_heads, HEAD_DIM)
-    positions = jnp.arange(seq_len, dtype=jnp.float32)
-    query_rot = rotary_embed(qkv_proj[:, :, 0], positions)
-    key_rot = rotary_embed(qkv_proj[:, :, 1], positions)
-    scores = jnp.einsum("bqhd,bkhd->bhqk", query_rot, key_rot, preferred_element_type=jnp.float32) * (HEAD_DIM ** -0.5)
-    causal = jnp.arange(seq_len)[:, None] >= jnp.arange(seq_len)[None, :]
-    attn_probs = jax.nn.softmax(jnp.where(causal, scores, -1e30), axis=-1).astype(jnp.bfloat16)
-    attn_mixed = jnp.einsum("bhqk,bkhd->bqhd", attn_probs, qkv_proj[:, :, 2], preferred_element_type=jnp.float32).astype(jnp.bfloat16)
-    attn_out = jnp.einsum("bsn,nm->bsm", attn_mixed.reshape(n_batch, seq_len, n_heads * HEAD_DIM), out_weight, preferred_element_type=jnp.float32)
-    return (x_in.astype(jnp.float32) + attn_out).astype(jnp.bfloat16)
+    cos_tab, sin_tab = jnp.cos(angles), jnp.sin(angles)
+    cos_tab = jnp.concatenate([cos_tab, cos_tab], axis=1)
+    sin_tab = jnp.concatenate([-sin_tab, sin_tab], axis=1)
+    pair = 2 * HEAD_DIM
+    steps = n_heads // 2
+    attn_mixed = pl.pallas_call(
+        attention_kernel,
+        out_shape=jax.ShapeDtypeStruct((seq_len, n_heads * HEAD_DIM), jnp.bfloat16),
+        grid=(steps,),
+        in_specs=[
+            pl.BlockSpec((seq_len, pair), lambda h: (0, h)),
+            pl.BlockSpec((seq_len, pair), lambda h: (0, h + steps)),
+            pl.BlockSpec((seq_len, pair), lambda h: (0, h + 2 * steps)),
+            pl.BlockSpec((seq_len, HEAD_DIM), lambda h: (0, 0)),
+            pl.BlockSpec((seq_len, HEAD_DIM), lambda h: (0, 0)),
+        ],
+        out_specs=pl.BlockSpec((seq_len, pair), lambda h: (0, h)),
+        compiler_params=pltpu.CompilerParams(vmem_limit_bytes=24 * 2**20),
+        cost_estimate=pl.CostEstimate(flops=8 * 10**9, bytes_accessed=7 * 2**20, transcendentals=2 * 10**6),
+        name="causal_attention",
+    )(qkv_proj, qkv_proj, qkv_proj, cos_tab, sin_tab)
+    attn_out = jnp.dot(attn_mixed, out_weight, preferred_element_type=jnp.float32)
+    return (tokens.astype(jnp.float32) + attn_out).astype(jnp.bfloat16)
 
 
 def capacity_for(n_tokens, top_k, n_experts):
@@ -59,7 +87,7 @@
     return lax.dot_general(lhs, rhs, (((1,), (1,)), ((), ())), preferred_element_type=jnp.float32)
 
 
-def exchange_kernel(n_chunk, spread_in, rows_in, gate_h, rest_h, out, r1, r2, r3, b1, b2, own, inp, spread, rows, w13, w2, xin, inner, yall, w_sem, in_sem, tx, rx, fin, ld):
+def exchange_kernel(n_chunk, spread_in, rows_in, fore_h, rest_h, out, r1, r2, r3, b1, b2, own, inp, spread, rows, w13, w2, xin, inner, yall, w_sem, in_sem, tx, rx, fin, ld):
     f, x, core = lax.axis_index("fsdp"), lax.axis_index("x"), lax.axis_index("core")
     z, y = f // 4, f % 4
     copy = pltpu.make_async_copy
@@ -119,7 +147,8 @@
         copy(inp.at[k, 0, 0, 0], xin.at[0, 0, 0], in_sem).start()
         wait(xin, in_sem)
 
-    n_tile = gate_h.shape[2] // 128
+    n_fore = fore_h.shape[2] // 128
+    n_tile = (n_fore + rest_h.shape[2] // 128) // 3
 
     def experts(k):
         load(k)
@@ -180,13 +209,13 @@
     hop1(1)
     place(2)
     hop1(2)
-    for part, half in enumerate((gate_h, rest_h)):
-        for j in range(n_tile):
-            src = half.at[:, :, pl.ds(j * 128, 128)]
-            dst = w13.at[:, core, :, pl.ds(j * 256 + part * 128, 128)]
-            copy(src, dst, w_sem.at[0]).start()
-            send(src, dst, w_sem.at[2], w_sem.at[4], partner)
-    down_h = rest_h.at[:, :, pl.ds(n_tile * 128, n_tile * 128)]
+    for t in range(2 * n_tile):
+        half, at = (fore_h, t) if t < n_fore else (rest_h, t - n_fore)
+        src = half.at[:, :, pl.ds(at * 128, 128)]
+        dst = w13.at[:, core, :, pl.ds(t % n_tile * 256 + t // n_tile * 128, 128)]
+        copy(src, dst, w_sem.at[0]).start()
+        send(src, dst, w_sem.at[2], w_sem.at[4], partner)
+    down_h = rest_h.at[:, :, pl.ds((2 * n_tile - n_fore) * 128, n_tile * 128)]
     copy(down_h, w2.at[:, core], w_sem.at[1]).start()
     send(down_h, w2.at[:, core], w_sem.at[3], w_sem.at[5], partner)
     for k in (4, 5, 3):
@@ -246,10 +275,10 @@
     wait(out.at[:, 0, 0, pl.ds(1, 3)], fin.at[2])
 
 
-def run_exchange(spread, rows, gate_h, rest_h):
+def run_exchange(spread, rows, fore_h, rest_h):
     blk, dim = 8, rows.shape[1]
     n_chunk = spread.shape[0] // (64 * blk)
-    width = gate_h.shape[2]
+    width = (fore_h.shape[2] + rest_h.shape[2]) // 3
     bf = jnp.bfloat16
     shapes = [(4, 4, 4), (3, 4, 4), (3, 4, 4), (3, 4, 4), (3, 4, 4), (3, 4, 3), (4, 4)]
     outs = pl.pallas_call(
@@ -275,7 +304,7 @@
         ],
         compiler_params=pltpu.CompilerParams(has_side_effects=True, collective_id=0, vmem_limit_bytes=60 * 2**20),
         name="expert_exchange",
-    )(spread, rows, gate_h, rest_h)
+    )(spread, rows, fore_h, rest_h)
     return outs[0]
 
 
@@ -315,9 +344,12 @@
         n_qkv = w_qkv.shape[1]
         n_attn = n_qkv + w_out.shape[1]
         dense = gather_rows(w_qkv, w_out, ws_gate, ws_up, lax.optimization_barrier(ws_down.T))
-        gate_h = lax.all_to_all(stage_expert(w_gate), "fsdp", 0, 0, tiled=True)
-        rest = jnp.concatenate([stage_expert(w_up), stage_expert(jnp.swapaxes(w_down, 1, 2))], axis=2)
-        dense, rest, gate_h = lax.optimization_barrier((dense, rest, gate_h))
+        up_half = stage_expert(w_up)
+        cut = w_up.shape[2] // 256 * 128
+        fore = jnp.concatenate([stage_expert(w_gate), up_half[:, :, :cut]], axis=2)
+        rest = jnp.concatenate([up_half[:, :, cut:], stage_expert(jnp.swapaxes(w_down, 1, 2))], axis=2)
+        fore_h = lax.all_to_all(fore, "fsdp", 0, 0, tiled=True)
+        dense, rest, fore_h = lax.optimization_barrier((dense, rest, fore_h))
         rest_h = lax.all_to_all(rest, "fsdp", 0, 0, tiled=True)
         qkv_full, out_full, shared_full = dense[:, :n_qkv], dense[:, n_qkv:n_attn], dense[:, n_attn:]
 
@@ -344,12 +376,12 @@
 
         hidden = attention_block(x_in, qkv_full, out_full).reshape(n_tokens, model_dim)
         normed = rms_norm(hidden)
-        s_gate = jnp.dot(normed, shared_full[:, :s_ff], preferred_element_type=jnp.float32)
-        s_up = jnp.dot(normed, shared_full[:, s_ff:2 * s_ff], preferred_element_type=jnp.float32)
+        s_both = jnp.dot(normed, shared_full[:, :2 * s_ff], preferred_element_type=jnp.float32)
+        s_gate, s_up = s_both[:, :s_ff], s_both[:, s_ff:]
         s_inner = (jax.nn.silu(s_gate) * s_up).astype(jnp.bfloat16)
         shared_out = nt_dot(s_inner, shared_full[:, 2 * s_ff:])
         routed_rows, shared_out = lax.optimization_barrier((normed, shared_out))
-        back = run_exchange(spread, routed_rows, gate_h, rest_h)
+        back = run_exchange(spread, routed_rows, fore_h, rest_h)
         routed = jnp.dot(merge, back.reshape(n_rows, model_dim), preferred_element_type=jnp.float32)
 
         summed = hidden.astype(jnp.float32) + shared_out + routed

time: 640 us -> 664 us (1.038)
  Pallas kernels: 284 us -> 304 us
  waiting for transfers between devices: 157 us -> 174 us
    pallas_call x0 -> x1, Pallas kernels: none -> 19.8 us  [attention_block(): pl.pallas_call(attention_kernel, out_shape=jax.ShapeDtypeStruct((seq_len,...]
    all_to_all x1, waiting for transfers between devices: 17.6 us -> 37.3 us  [local_step(): fore_h = lax.all_to_all(fore, 'fsdp', 0, 0, tiled=True)]
    unnamed x35 -> x39, local copies, waits for them, and re-layouts: 18.8 us -> 17.3 us
    dot_general x5 -> x3, matrix products: 39.8 us -> 41 us  [the longest x1 16.6 us: attention_block(): jnp.dot(normed, qkv_weight, preferred_element_type=jnp.float32)]
  transfers between devices with their start and end apart: 6 -> 6, of which waited for: 3 -> 3; matrix products, arithmetic and copies ran while one was open for 19% -> 15% of each run, Pallas kernels for 0% -> 0%
where the time goes in v6:
time: 664 us; the launch traced here: 652 us
  Pallas kernels  304 us (46%)
  waiting for transfers between devices  174 us (26%)
  matrix products  65.7 us (10%)
  local copies, waits for them, and re-layouts  59.3 us (9%)
  other arithmetic  20.2 us (3%)
  starting transfers between devices  15.2 us (2%)
  between operations  14.1 us (2%)
    pallas_call x1, Pallas kernels, run_exchange(): pl.pallas_call(functools.partial(exchange_kernel, n_chunk), out_shape=[ja...  284 us
    all_gather x1, waiting for transfers between devices, gather_rows(): return lax.all_gather(piece, ALL, axis=0, tiled=True)  101 us
    all_to_all x1, waiting for transfers between devices, local_step(): fore_h = lax.all_to_all(fore, 'fsdp', 0, 0, tiled=True)  37.3 us
    all_to_all x1, waiting for transfers between devices, local_step(): rest_h = lax.all_to_all(rest, 'fsdp', 0, 0, tiled=True)  35.3 us
    scatter x1, local copies, waits for them, and re-layouts, local_step(): jnp.zeros((n_rows,), gates.dtype).at[row]  20.7 us
    pallas_call x1, Pallas kernels, attention_block(): pl.pallas_call(attention_kernel, out_shape=jax.ShapeDtypeStruct((seq_len,...  19.8 us
    unnamed x39, local copies, waits for them, and re-layouts  17.3 us
    dot_general x1, matrix products, attention_block(): jnp.dot(normed, qkv_weight, preferred_element_type=jnp.float32)  16.6 us
  transfers between devices with their start and end apart: 6, of which 3 were waited for; matrix products, arithmetic and copies ran while one was open for 15% of the time, Pallas kernels for 0%

profile of v6, /device:TPU:1, one launch (start us, length us, event | category | flops | bytes accessed | tf_op | source)
XLA Modules:
  0.0 652.2 jit_solution(6918908344213948928)
XLA Ops:
  6.5 1.1 copy-done
  7.6 0.9 dynamic-slice_dynamic-update-slice_fusion
  10.0 0.9 dynamic-slice_dynamic-update-slice_fusion.2
  12.6 1.5 constant_dynamic-slice_fusion.3
  14.1 1.5 collective-permute-start
  15.5 7.0 %constant_dynamic-slice_fusion.2 = (bf16[8,1408,64]{2,1,0:T(8,128)(2,1)}, bf16[8,1408,64]{2,1,0:T(8,128)(2,1)}) fusion(bf16[8,1408,128]{2,1,0:T(8,128)(2,1)} %param.17, s32[]{:T(128)S(6)} %select_n.278, s32[]{:T(128)S(6)} %select_n.279), kind=kLoop, calls=%fused_computation.109 | loop fusion | bytes 5767176 | tf_op jit(solution)/shard_map/dynamic-slice
  22.5 4.1 copy.23
  26.7 2.7 constant_dynamic-slice_fusion
  29.8 4.2 copy.22
  34.0 2.5 broadcast_select_fusion.2
  37.2 4.6 bitcast_select_fusion.1
  41.8 2.3 fusion.14
  44.1 8.0 %all-to-all-start = ((bf16[16,64,2048]{2,1,0:T(8,128)(2,1)}), bf16[16,64,2048]{2,1,0:T(8,128)(2,1)}, u32[]{:S(2)}, u32[]{:S(2)}) async-start(bf16[16,64,2048]{2,1,0:T(8,128)(2,1)} %fusion.14), calls=%async_computation | async-start | bytes 8388608 | tf_op jit(solution)/shard_map/all_to_all | solution.py:351
  53.5 9.2 %scatter_custom_fusion = s32[3072]{0:T(1024)S(1)} fusion(s32[2304]{0:T(1024)S(1)} %fusion.42, s32[2304]{0:T(1024)S(1)} %add_select_fusion, s32[]{:T(128)} %constant.150.clone.1), kind=kCustom, calls=%fused_computation.103 | custom fusion | bytes 12292 | tf_op jit(solution)/shard_map/scatter | solution.py:372
  62.7 20.7 %scatter_custom_fusion.1 = bf16[3072]{0:T(1024)(128)(2,1)S(1)} fusion(s32[2304]{0:T(1024)S(1)} %fusion.42, bf16[2304]{0:T(1024)(128)(2,1)S(1)} %reshape.523, bf16[]{:T(256)} %constant.160.clone.1), kind=kCustom, calls=%fused_computation.105 | custom fusion | bytes 6146 | tf_op jit(solution)/shard_map/scatter | solution.py:373
  84.3 1.8 fusion.19
  86.2 2.4 fusion.12.spread_in
  88.6 1.3 fusion.29
  89.9 2.3 maximum_maximum_fusion
  92.2 37.3 %all-to-all-done.fore_h = bf16[16,64,2048]{2,1,0:T(8,128)(2,1)} async-done(((bf16[16,64,2048]{2,1,0:T(8,128)(2,1)}), bf16[16,64,2048]{2,1,0:T(8,128)(2,1)}, u32[]{:S(2)}, u32[]{:S(2)}) %all-to-all-start) | async-done | bytes 4194336 | tf_op jit(solution)/shard_map/all_to_all | solution.py:351
  129.4 100.9 %all-gather.2.cloned.1.call-done = bf16[2048,16640]{1,0:T(8,128)(2,1)} async-done(((bf16[16,16640]{1,0:T(8,128)(2,1)}), bf16[2048,16640]{1,0:T(8,128)(2,1)}) %all-gather.2.cloned.1.call-update) | async-done | bytes 68157456 | tf_op jit(solution)/shard_map/all_gather | solution.py:324
  230.3 16.6 %fusion.6.q_ref.k_ref.v_ref = bf16[384,6144]{1,0:T(8,128)(2,1)} fusion(bf16[2048,16640]{1,0:T(8,128)(2,1)} %all-gather.2.cloned.1.call-done, bf16[1,384,2048]{2,1,0:T(8,128)(2,1)S(1)} %copy-done.9, f32[384]{0:T(512)S(1)} %add_rsqrt_fusion.1), kind=kOutput, calls=%fused_computation.8 | convolution fusion | flops 9668395008 | bytes 31458816 | tf_op jit(solution)/shard_map/dot_general | solution.py:53
  246.9 2.3 copy-done.2
  249.3 19.8 %causal_attention.1 = bf16[384,2048]{1,0:T(8,128)(2,1)S(1)} custom-call(bf16[384,6144]{1,0:T(8,128)(2,1)S(1)} %copy-done.2, bf16[384,6144]{1,0:T(8,128)(2,1)S(1)} %copy-done.2, bf16[384,6144]{1,0:T(8,128)(2,1)S(1)} %copy-done.2, f32[384,128]{1,0:T(8,128)S(1)} %get-tuple-element.32.cos_ref, f32[384,128]{1,0:T(8,128)S(1)} %get-tuple-element.33.sin_ref), custom_call_target="tpu_custom_call" | custom-call | flops 8000000000 | bytes 7340032 | tf_op jit(solution)/shard_map/causal_attention/pallas_call | solution.py:62
  269.1 8.1 %fusion.15 = (f32[384]{0:T(512)S(1)}, bf16[384,2048]{1,0:T(8,128)(2,1)}) fusion(bf16[384,2048]{1,0:T(8,128)(2,1)S(1)} %causal_attention.1, bf16[2048,16640]{1,0:T(8,128)(2,1)} %all-gather.2.cloned.1.call-done, bf16[1,384,2048]{2,1,0:T(8,128)(2,1)S(1)} %copy-done.9), kind=kOutput, calls=%fused_computation.26 | convolution fusion | flops 3225943552 | bytes 13108736 | tf_op jit(solution)/shard_map/dot_general | solution.py:78
  277.2 5.2 all-to-all-start.1
  282.4 1.7 fusion.16.rows_in
  284.2 16.2 %fusion.2 = f32[384,5632]{1,0:T(8,128)} fusion(bf16[384,2048]{1,0:T(8,128)(2,1)S(1)} %fusion.16.rows_in, bf16[2048,16640]{1,0:T(8,128)(2,1)} %all-gather.2.cloned.1.call-done), kind=kOutput, calls=%fused_computation.4 | convolution fusion | flops 8858370048 | bytes 33292288 | tf_op jit(solution)/shard_map/dot_general | solution.py:379
  300.4 13.5 %fusion.4 = f32[384,2048]{1,0:T(8,128)} fusion(bf16[2048,16640]{1,0:T(8,128)(2,1)} %all-gather.2.cloned.1.call-done, f32[384,5632]{1,0:T(8,128)} %fusion.2), kind=kOutput, calls=%fused_computation.6 | convolution fusion | flops 4435673088 | bytes 23330816 | tf_op jit(solution)/shard_map/dot_general | solution.py:87
  313.9 35.3 %all-to-all-done.1.rest_h = bf16[16,64,2176]{2,1,0:T(8,128)(2,1)} async-done(((bf16[16,64,2176]{2,1,0:T(8,128)(2,1)}), bf16[16,64,2176]{2,1,0:T(8,128)(2,1)}, u32[]{:S(2)}, u32[]{:S(2)}) %all-to-all-start.1) | async-done | bytes 4456480 | tf_op jit(solution)/shard_map/all_to_all | solution.py:353
  349.2 284.4 %expert_exchange.1 = (bf16[6,4,4,4,8,2048]{5,4,3,2,1,0:T(8,128)(2,1)}, bf16[6,3,4,4,8,2048]{5,4,3,2,1,0:T(8,128)(2,1)}, bf16[6,3,4,4,8,2048]{5,4,3,2,1,0:T(8,128...) custom-call(bf16[3072,384]{1,0:T(8,128)(2,1)} %fusion.12.spread_in, ...), custom_call_target="tpu_custom_call" | custom-call | tf_op jit(solution)/shard_map/expert_exchange/pallas_call | solution.py:284
  633.7 11.3 %fusion.24 = bf16[1,384,2048]{2,1,0:T(8,128)(2,1)} fusion(bf16[3072,2048]{1,0:T(8,128)(2,1)} %bitcast.21, f32[384,2048]{1,0:T(8,128)} %fusion.4, bf16[384,2048]{1,0:T(8,128)(2,1)S(1)} %copy-done.10, s32[3072]{0:T(1024)S(1)} %scatter_custom_fusion, bf16[3072]{0:T(1024)(128)(2,1)S(1)} %scatter_custom_fusion.1), kind=kOutput, calls=%fused_computation.35 | convolution fusion | flops 4837343232 | bytes 18892800 | tf_op jit(solution)/shard_map/dot_general | solution.py:385
  (53 shorter events, 6.6 us)
Async XLA Ops:
  6.5 1.1 copy-start
  6.5 223.8 %all-gather.2.cloned.1.call-start = ((), (), s32[]{:S(2)}) async-start(), calls=%async_computation.2 | async-start | bytes 68689920 | tf_op jit(solution)/shard_map/all_gather | solution.py:324
  11.8 0.8 copy-start.11
  14.1 19.9 %collective-permute-start = (bf16[8,64,1408]{2,1,0:T(8,128)(2,1)S(1)}, bf16[8,64,1408]{2,1,0:T(8,128)(2,1)}, u32[]{:S(2)}, u32[]{:S(2)}) collective-permute-start(bf16[8,64,1408]{2,1,0:T(8,128)(2,1)S(1)} %constant_dynamic-slice_fusion.3), channel_id=1, source_target_pairs={{0,1},{1,0},{2,3},{3,2},{4,5},{5,4},{6,7},{7,6},{8,9},{9,8},{10,11... | collective-permute-start | bytes 4325384 | tf_op jit(solution)/shard_map/ppermute | solution.py:331
  26.6 9.9 %collective-permute-start.1 = (bf16[8,64,1408]{2,1,0:T(8,128)(2,1)}, bf16[8,64,1408]{2,1,0:T(8,128)(2,1)}, u32[]{:S(2)}, u32[]{:S(2)}) collective-permute-start(bf16[8,64,1408]{2,1,0:T(8,128)(2,1)} %bitcast.20), channel_id=1, source_target_pairs={{0,1},{1,0},{2,3},{3,2},{4,5},{5,4},{6,7},{7,6},{8,9},{9,8},{10,11... | collective-permute-start | bytes 4325384 | tf_op jit(solution)/shard_map/ppermute | solution.py:331
  29.3 7.2 %collective-permute-start.2 = (bf16[8,64,1408]{2,1,0:T(8,128)(2,1)}, bf16[8,64,1408]{2,1,0:T(8,128)(2,1)}, u32[]{:S(2)}, u32[]{:S(2)}) collective-permute-start(bf16[8,64,1408]{2,1,0:T(8,128)(2,1)} %constant_dynamic-slice_fusion), channel_id=1, source_target_pairs={{0,1},{1,0},{2,3},{3,2},{4,5},{5,4},{6,7},{7,6},{8,9},{9,8},{10,11... | collective-permute-start | bytes 4325384 | tf_op jit(solution)/shard_map/ppermute | solution.py:331
  34.0 2.5 copy-start.5
  34.0 3.2 copy-start.8
  36.5 5.4 copy-start.3
  44.1 8.0 %copy-start.12 = (s32[1,384,6]{1,0,2:T(1,128)S(1)}, s32[1,384,6]{1,0,2:T(1,128)}, u32[]{:S(2)}) copy-start(s32[1,384,6]{1,0,2:T(1,128)} %param.22) | copy-start | bytes 27652
  44.1 8.3 %copy-start.13 = (s32[1,384,6]{1,0,2:T(1,128)S(1)}, s32[1,384,6]{1,0,2:T(1,128)}, u32[]{:S(2)}) copy-start(s32[1,384,6]{1,0,2:T(1,128)} %param.21) | copy-start | bytes 27652
  44.1 8.7 %copy-start.14 = (bf16[1,384,6]{1,2,0:T(8,128)(2,1)S(1)}, bf16[1,384,6]{1,2,0:T(8,128)(2,1)}, u32[]{:S(2)}) copy-start(bf16[1,384,6]{1,2,0:T(8,128)(2,1)} %param.23) | copy-start | bytes 13828
  44.1 85.3 %all-to-all-start = ((bf16[16,64,2048]{2,1,0:T(8,128)(2,1)}), bf16[16,64,2048]{2,1,0:T(8,128)(2,1)}, u32[]{:S(2)}, u32[]{:S(2)}) async-start(bf16[16,64,2048]{2,1,0:T(8,128)(2,1)} %fusion.14), calls=%async_computation | async-start | bytes 8388608 | tf_op jit(solution)/shard_map/all_to_all | solution.py:351
  86.1 3.7 copy-start.6
  86.1 3.7 copy-start.7
  89.9 140.5 %copy-start.9 = (bf16[1,384,2048]{2,1,0:T(8,128)(2,1)S(1)}, bf16[1,384,2048]{2,1,0:T(8,128)(2,1)}, u32[]{:S(2)}) copy-start(bf16[1,384,2048]{2,1,0:T(8,128)(2,1)} %param.12) | copy-start | bytes 4718596
  246.9 2.3 copy-start.2
  277.2 72.0 %all-to-all-start.1 = ((bf16[16,64,2176]{2,1,0:T(8,128)(2,1)}), bf16[16,64,2176]{2,1,0:T(8,128)(2,1)}, u32[]{:S(2)}, u32[]{:S(2)}) async-start(bf16[16,64,2176]{2,1,0:T(8,128)(2,1)} %maximum_maximum_fusion), calls=%async_computation.1 | async-start | bytes 8912896 | tf_op jit(solution)/shard_map/all_to_all | solution.py:353
  284.1 16.2 %copy-start.4 = (bf16[384,2048]{1,0:T(8,128)(2,1)}, bf16[384,2048]{1,0:T(8,128)(2,1)S(1)}, u32[]{:S(2)}) copy-start(bf16[384,2048]{1,0:T(8,128)(2,1)S(1)} %fusion.16.rows_in) | copy-start | bytes 4718596
  313.9 319.8 %copy-start.10 = (bf16[384,2048]{1,0:T(8,128)(2,1)S(1)}, bf16[384,2048]{1,0:T(8,128)(2,1)}, u32[]{:S(2)}) copy-start(bf16[384,2048]{1,0:T(8,128)(2,1)} %get-tuple-element.29) | copy-start | bytes 4718596
  633.7 11.3 %copy-start.1 = (bf16[2816,128]{1,0:T(8,128)(2,1)S(1)}, bf16[2816,128]{1,0:T(8,128)(2,1)}, u32[]{:S(2)}) copy-start(bf16[2816,128]{1,0:T(8,128)(2,1)} %param.20) | copy-start | bytes 2162692
Sparse Core Ops, SparseCore 0:
  12.7 217.5 all-gather.1

commit v7 on v5

--- a/solution.py
+++ b/solution.py
@@ -314,8 +314,10 @@
 
         n_qkv = w_qkv.shape[1]
         n_attn = n_qkv + w_out.shape[1]
-        dense = gather_rows(w_qkv, w_out, ws_gate, ws_up, lax.optimization_barrier(ws_down.T))
-        gate_h = lax.all_to_all(stage_expert(w_gate), "fsdp", 0, 0, tiled=True)
+        dense = gather_rows(w_qkv, w_out, ws_gate, ws_up, ws_down.T)
+        staged = (stage_expert(w_gate), w_up, w_down, expert_ids, slot_ids, gate_vals)
+        gate_half, w_up, w_down, expert_ids, slot_ids, gate_vals = lax.optimization_barrier(staged)
+        gate_h = lax.all_to_all(gate_half, "fsdp", 0, 0, tiled=True)
         rest = jnp.concatenate([stage_expert(w_up), stage_expert(jnp.swapaxes(w_down, 1, 2))], axis=2)
         dense, rest, gate_h = lax.optimization_barrier((dense, rest, gate_h))
         rest_h = lax.all_to_all(rest, "fsdp", 0, 0, tiled=True)

time: 640 us -> 634 us (level)
  the two profiles are of different devices: /device:TPU:1 before, /device:TPU:8 now
where the time goes in v7:
time: 634 us; the launch traced here: 625 us
  Pallas kernels  292 us (46%)
  waiting for transfers between devices  155 us (24%)
  matrix products  68.1 us (11%)
  local copies, waits for them, and re-layouts  55.6 us (9%)
  other arithmetic  25.7 us (4%)
  starting transfers between devices  14.8 us (2%)
  between operations  14.1 us (2%)
    pallas_call x1, Pallas kernels, run_exchange(): pl.pallas_call(functools.partial(exchange_kernel, n_chunk), out_shape=[ja...  292 us
    all_gather x1, waiting for transfers between devices, gather_rows(): return lax.all_gather(piece, ALL, axis=0, tiled=True)  108 us
    all_to_all x1, waiting for transfers between devices, local_step(): rest_h = lax.all_to_all(rest, 'fsdp', 0, 0, tiled=True)  30.2 us
    scatter x1, local copies, waits for them, and re-layouts, local_step(): jnp.zeros((n_rows,), gates.dtype).at[row]  21.2 us
    dot_general x1, matrix products, nt_dot(): lax.dot_general(lhs, rhs, (((1,), (1,)), ((), ())), preferred_element_typ...  17 us
    dot_general x1, matrix products, attention_block(): jnp.einsum('bsd,dn->bsn', normed, qkv_weight, preferred_element_type=jnp....  15.4 us
    all_to_all x1, waiting for transfers between devices, local_step(): gate_h = lax.all_to_all(gate_half, 'fsdp', 0, 0, tiled=True)  13.3 us
  transfers between devices with their start and end apart: 6, of which 4 were waited for; matrix products, arithmetic and copies ran while one was open for 18% of the time, Pallas kernels for 0%

profile of v7, /device:TPU:8, one launch (start us, length us, event | category | flops | bytes accessed | tf_op | source)
XLA Modules:
  0.0 625.0 jit_solution(9554079508589717670)
XLA Ops:
  11.7 2.6 constant_dynamic-slice_fusion.1
  14.8 3.1 collective-permute-done
  17.9 2.4 broadcast_select_fusion.3
  20.3 1.9 pad_maximum_fusion
  22.1 4.6 copy.21
  26.7 1.5 dynamic-slice_bitcast_fusion
  29.2 8.6 %all-to-all-start = ((bf16[16,64,1408]{2,1,0:T(8,128)(2,1)}), bf16[16,64,1408]{2,1,0:T(8,128)(2,1)}, u32[]{:S(2)}, u32[]{:S(2)}) async-start(bf16[16,64,1408]{2,1,0:T(8,128)(2,1)} %pad_maximum_fusion), calls=%async_computation | async-start | bytes 5767168 | tf_op jit(solution)/shard_map/all_to_all | solution.py:320
  37.8 2.6 constant_dynamic-slice_fusion
  41.8 9.0 %scatter_custom_fusion = s32[3072]{0:T(1024)S(1)} fusion(s32[2304]{0:T(1024)S(1)} %fusion.74, s32[2304]{0:T(1024)S(1)} %add_select_fusion, s32[]{:T(128)} %constant.159.clone.1), kind=kCustom, calls=%fused_computation.133 | custom fusion | bytes 12292 | tf_op jit(solution)/shard_map/scatter | solution.py:342
  50.8 21.2 %scatter_custom_fusion.1 = bf16[3072]{0:T(1024)(128)(2,1)S(1)} fusion(s32[2304]{0:T(1024)S(1)} %fusion.74, bf16[2304]{0:T(1024)(128)(2,1)S(1)} %reshape.674, bf16[]{:T(256)} %constant.169.clone.1), kind=kCustom, calls=%fused_computation.135 | custom fusion | bytes 6146 | tf_op jit(solution)/shard_map/scatter | solution.py:343
  72.0 2.4 fusion.19.spread_in
  74.4 2.6 bitcast_select_fusion.1
  77.2 2.0 broadcast_select_fusion.1
  79.2 3.0 maximum_maximum_fusion
  82.2 13.3 %all-to-all-done.gate_h = bf16[16,64,1408]{2,1,0:T(8,128)(2,1)} async-done(((bf16[16,64,1408]{2,1,0:T(8,128)(2,1)}), bf16[16,64,1408]{2,1,0:T(8,128)(2,1)}, u32[]{:S(2)}, u32[]{:S(2)}) %all-to-all-start) | async-done | bytes 2883616 | tf_op jit(solution)/shard_map/all_to_all | solution.py:320
  95.4 107.9 %all-gather.2.cloned.1.call-done = bf16[2048,16640]{1,0:T(8,128)(2,1)} async-done(((bf16[16,16640]{1,0:T(8,128)(2,1)}), bf16[2048,16640]{1,0:T(8,128)(2,1)}) %all-gather.2.cloned.1.call-update) | async-done | bytes 68157456 | tf_op jit(solution)/shard_map/all_gather | solution.py:295
  203.3 15.4 %fusion.44 = bf16[48,8,48,128]{3,1,2,0:T(8,128)(2,1)S(1)} fusion(bf16[2048,16640]{1,0:T(8,128)(2,1)} %all-gather.2.cloned.1.call-done, bf16[1,384,2048]{2,1,0:T(8,128)(2,1)} %param.12, f32[384]{0:T(512)S(1)} %add_rsqrt_fusion.1), kind=kOutput, calls=%fused_computation.50 | convolution fusion | flops 9668395008 | bytes 31458816 | tf_op jit(solution)/shard_map/bsd,dn->bsn/dot_general | solution.py:41
  218.8 1.3 copy.34
  220.0 2.5 fusion.88
  222.6 2.9 copy.31
  225.4 6.0 all-to-all-start.1
  231.4 2.2 fusion.62
  233.6 2.3 fusion.51
  235.9 1.9 fusion.55
  237.8 5.1 fusion.89
  243.0 5.1 fusion.48
  248.1 7.3 %fusion.32 = (f32[384]{0:T(512)S(1)}, bf16[384,2048]{1,0:T(8,128)(2,1)S(1)}) fusion(bf16[384,2048]{0,1:T(8,128)(2,1)S(1)} %bitcast.56, bf16[2048,16640]{1,0:T(8,128)(2,1)} %all-gather.2.cloned.1.call-done, bf16[1,384,2048]{2,1,0:T(8,128)(2,1)S(1)} %copy-done.5), kind=kOutput, calls=%fused_computation.38 | convolution fusion | flops 3225943552 | bytes 13108736 | tf_op jit(solution)/shard_map/bsn,nm->bsm/dot_general | solution.py:50
  256.9 10.1 %fusion.7 = f32[384,2816]{1,0:T(8,128)} fusion(bf16[384,2048]{1,0:T(8,128)(2,1)S(1)} %fusion.33.rows_in, bf16[2048,16640]{1,0:T(8,128)(2,1)} %all-gather.2.cloned.1.call-done), kind=kOutput, calls=%fused_computation.9 | convolution fusion | flops 4429185024 | bytes 17432576 | tf_op jit(solution)/shard_map/dot_general | solution.py:349
  267.0 17.0 %fusion.3 = f32[384,2048]{1,0:T(8,128)} fusion(bf16[2048,16640]{1,0:T(8,128)(2,1)} %all-gather.2.cloned.1.call-done, bf16[384,2048]{1,0:T(8,128)(2,1)S(1)} %fusion.33.rows_in, f32[384,2816]{1,0:T(8,128)} %fusion.7), kind=kOutput, calls=%fused_computation.5 | convolution fusion | flops 8864858112 | bytes 32112640 | tf_op jit(solution)/shard_map/dot_general | solution.py:59
  284.0 30.2 %all-to-all-done.1.rest_h = bf16[16,64,2816]{2,1,0:T(8,128)(2,1)} async-done(((bf16[16,64,2816]{2,1,0:T(8,128)(2,1)}), bf16[16,64,2816]{2,1,0:T(8,128)(2,1)}, u32[]{:S(2)}, u32[]{:S(2)}) %all-to-all-start.1) | async-done | bytes 5767200 | tf_op jit(solution)/shard_map/all_to_all | solution.py:323
  314.3 292.1 %expert_exchange.1 = (bf16[6,4,4,4,8,2048]{5,4,3,2,1,0:T(8,128)(2,1)}, bf16[6,3,4,4,8,2048]{5,4,3,2,1,0:T(8,128)(2,1)}, bf16[6,3,4,4,8,2048]{5,4,3,2,1,0:T(8,128...) custom-call(bf16[3072,384]{1,0:T(8,128)(2,1)} %fusion.19.spread_in, ...), custom_call_target="tpu_custom_call" | custom-call | tf_op jit(solution)/shard_map/expert_exchange/pallas_call | solution.py:255
  606.4 11.3 %fusion.38 = bf16[1,384,2048]{2,1,0:T(8,128)(2,1)} fusion(bf16[3072,2048]{1,0:T(8,128)(2,1)} %bitcast.55, f32[384,2048]{1,0:T(8,128)} %fusion.3, bf16[384,2048]{1,0:T(8,128)(2,1)S(1)} %copy-done.8, s32[3072]{0:T(1024)S(1)} %scatter_custom_fusion, bf16[3072]{0:T(1024)(128)(2,1)S(1)} %scatter_custom_fusion.1), kind=kOutput, calls=%fused_computation.47 | convolution fusion | flops 4837343232 | bytes 18892800 | tf_op jit(solution)/shard_map/dot_general | solution.py:355
  (55 shorter events, 9.6 us)
Async XLA Ops:
  6.5 1.2 copy-start
  6.5 196.8 %all-gather.2.cloned.1.call-start = ((), (), s32[]{:S(2)}) async-start(), calls=%async_computation.2 | async-start | bytes 68689920 | tf_op jit(solution)/shard_map/all_gather | solution.py:295
  7.7 6.6 %copy-start.4 = (bf16[1,384,2048]{2,1,0:T(8,128)(2,1)S(1)}, bf16[1,384,2048]{2,1,0:T(8,128)(2,1)}, u32[]{:S(2)}) copy-start(bf16[1,384,2048]{2,1,0:T(8,128)(2,1)} %param.12) | copy-start | bytes 4718596
  10.9 0.8 copy-start.9
  14.3 3.6 collective-permute-start
  28.2 46.2 %collective-permute-start.2 = (bf16[8,64,1408]{2,1,0:T(8,128)(2,1)S(1)}, bf16[8,64,1408]{2,1,0:T(8,128)(2,1)}, u32[]{:S(2)}, u32[]{:S(2)}) collective-permute-start(bf16[8,64,1408]{2,1,0:T(8,128)(2,1)S(1)} %dynamic-slice_bitcast_fusion), channel_id=1, source_target_pairs={{0,1},{1,0},{2,3},{3,2},{4,5},{5,4},{6,7},{7,6},{8,9},{9,8},{10,11... | collective-permute-start | bytes 4325384 | tf_op jit(solution)/shard_map/ppermute | solution.py:302
  29.2 11.2 %copy-start.10 = (s32[1,384,6]{1,0,2:T(1,128)S(1)}, s32[1,384,6]{1,0,2:T(1,128)}, u32[]{:S(2)}) copy-start(s32[1,384,6]{1,0,2:T(1,128)} %param.22) | copy-start | bytes 27652
  29.2 11.5 %copy-start.11 = (s32[1,384,6]{1,0,2:T(1,128)S(1)}, s32[1,384,6]{1,0,2:T(1,128)}, u32[]{:S(2)}) copy-start(s32[1,384,6]{1,0,2:T(1,128)} %param.21) | copy-start | bytes 27652
  29.2 66.2 %all-to-all-start = ((bf16[16,64,1408]{2,1,0:T(8,128)(2,1)}), bf16[16,64,1408]{2,1,0:T(8,128)(2,1)}, u32[]{:S(2)}, u32[]{:S(2)}) async-start(bf16[16,64,1408]{2,1,0:T(8,128)(2,1)} %pad_maximum_fusion), calls=%async_computation | async-start | bytes 5767168 | tf_op jit(solution)/shard_map/all_to_all | solution.py:320
  37.8 3.2 copy-start.12
  40.4 36.6 %collective-permute-start.1 = (bf16[8,64,1408]{2,1,0:T(8,128)(2,1)}, bf16[8,64,1408]{2,1,0:T(8,128)(2,1)}, u32[]{:S(2)}, u32[]{:S(2)}) collective-permute-start(bf16[8,64,1408]{2,1,0:T(8,128)(2,1)} %constant_dynamic-slice_fusion), channel_id=1, source_target_pairs={{0,1},{1,0},{2,3},{3,2},{4,5},{5,4},{6,7},{7,6},{8,9},{9,8},{10,11... | collective-permute-start | bytes 4325384 | tf_op jit(solution)/shard_map/ppermute | solution.py:302
  74.4 2.8 copy-start.3
  225.4 88.8 %all-to-all-start.1 = ((bf16[16,64,2816]{2,1,0:T(8,128)(2,1)}), bf16[16,64,2816]{2,1,0:T(8,128)(2,1)}, u32[]{:S(2)}, u32[]{:S(2)}) async-start(bf16[16,64,2816]{2,1,0:T(8,128)(2,1)} %maximum_maximum_fusion), calls=%async_computation.1 | async-start | bytes 11534336 | tf_op jit(solution)/shard_map/all_to_all | solution.py:323
  237.8 5.1 copy-start.6
  243.0 5.1 copy-start.5
  255.4 1.2 copy-start.7
  256.9 10.1 %copy-start.2 = (bf16[384,2048]{1,0:T(8,128)(2,1)}, bf16[384,2048]{1,0:T(8,128)(2,1)S(1)}, u32[]{:S(2)}) copy-start(bf16[384,2048]{1,0:T(8,128)(2,1)S(1)} %fusion.33.rows_in) | copy-start | bytes 4718596
  284.0 322.3 %copy-start.8 = (bf16[384,2048]{1,0:T(8,128)(2,1)S(1)}, bf16[384,2048]{1,0:T(8,128)(2,1)}, u32[]{:S(2)}) copy-start(bf16[384,2048]{1,0:T(8,128)(2,1)} %copy-done.7) | copy-start | bytes 4718596
  606.4 11.3 %copy-start.1 = (bf16[2816,128]{1,0:T(8,128)(2,1)S(1)}, bf16[2816,128]{1,0:T(8,128)(2,1)}, u32[]{:S(2)}) copy-start(bf16[2816,128]{1,0:T(8,128)(2,1)} %param.20) | copy-start | bytes 2162692
Sparse Core Ops, SparseCore 0:
  11.8 191.4 all-gather.1
